TPU v7x, 128 devices: a whole 4x4x4 slice. The times are simulated.
128 devices in a mesh: dp: 8 (over z, y_lo), tensor: 16 (over x, y_hi, core).
Axes of the slice: x: 4, y: 4 (y_hi: 2, y_lo: 2; y = y_hi * 2 + y_lo), z: 4, core: 2. Of those that a mesh axis runs over, the one named last changes fastest.
Arguments:
- tokens: bfloat16 [2048, 4096], P(('dp', 'tensor')), may hold values from -4 to 4
- lengths: int32 [8], replicated, may hold values from 64 to 256, as said below
- norm_gains: float32 [2, 4096], replicated, may hold values from 0.25 to 1.75
- query_weight: bfloat16 [2, 4096, 4096], P(None, None, 'tensor'), may hold values from -0.09375 to 0.09375
- key_weight: bfloat16 [2, 4096, 1024], P(None, None, 'tensor'), may hold values from -0.09375 to 0.09375
- value_weight: bfloat16 [2, 4096, 1024], P(None, None, 'tensor'), may hold values from -0.09375 to 0.09375
- out_weight: bfloat16 [2, 4096, 4096], P(None, 'tensor'), may hold values from -0.09375 to 0.09375
- query_probe: bfloat16 [2, 4096, 4096], P(None, 'dp', 'tensor'), may hold values from -0.09375 to 0.09375
- key_probe: bfloat16 [2, 4096, 1024], P(None, 'dp', 'tensor'), may hold values from -0.09375 to 0.09375
- value_probe: bfloat16 [2, 4096, 1024], P(None, 'dp', 'tensor'), may hold values from -0.09375 to 0.09375
- out_probe: bfloat16 [2, 4096, 4096], P(None, 'tensor', 'dp'), may hold values from -0.09375 to 0.09375
Outputs:
- query_product: float32 [2, 4096, 4096], P(None, 'dp', 'tensor')
- key_product: float32 [2, 4096, 1024], P(None, 'dp', 'tensor')
- value_product: float32 [2, 4096, 1024], P(None, 'dp', 'tensor')
- out_product: float32 [2, 4096, 4096], P(None, 'tensor', 'dp')
Inputs may be any that keep to these rules, and one draw needn't show every extreme that they name: lengths[i] counts the leading valid positions of sequence i; the last sequence is full.
All inputs are finite; a program needn't handle non-finite values.
Results may differ from a plain program's by a relative error of at most 0.035.
Values may be sent and summed in bfloat16 or wider, within the bound.
A program may use at most 128 MiB of HBM per device.

v0:
```python
import math

import jax
import jax.numpy as jnp
from jax import lax
from jax.sharding import PartitionSpec as P

HD = 128
LEN = 256


EPS = 1e-05
THETA = 500000.0


def turned_gather(arrays, axis, dims):
    turned = [jnp.moveaxis(a, dim, 0) for a, dim in zip(arrays, dims)]
    both = jnp.concatenate([t.reshape(len(t), -1) for t in turned], axis=1)
    result, at, done = (lax.all_gather(both, axis, axis=0, tiled=True), 0, [])
    for t, dim in zip(turned, dims):
        share = result[:, at : at + t[0].size].reshape(-1, *t.shape[1:])
        done.append(jnp.moveaxis(share, 0, dim))
        at += t[0].size
    return tuple(done)


def sent_together(arrays, axis, dim, along):
    widths = [a.shape[along] for a in arrays]
    both = jnp.concatenate(arrays, axis=along)
    result = lax.all_gather(both, axis, axis=dim, tiled=True)
    return tuple(jnp.split(result, [sum(widths[:k]) for k in range(1, len(widths))], axis=along))


def swapped(value, axis, apart):
    mask = 2**apart
    pairs = [(source, source ^ mask) for source in range(lax.axis_size(axis))]
    return lax.ppermute(value, axis, pairs)


def split_up(x, dim, length):
    before, after = (x.shape[:dim], x.shape[dim + 1 :])
    return jnp.moveaxis(x.reshape(*before, length, -1, *after), dim, 0)


def sum_at_owner(x, axis, dim):
    pieces = split_up(x, dim, lax.axis_size(axis))
    arrived = lax.all_to_all(pieces, axis, split_axis=0, concat_axis=0, tiled=True)
    return arrived.astype(jnp.float32).sum(axis=0)


def side_by_side(arrays, axis, dim, along):
    ends, at = ([], 0)
    for a in arrays[:-1]:
        at += a.shape[along]
        ends.append(at)
    both = jnp.concatenate(arrays, axis=along)
    return tuple(
        jnp.split(lax.psum_scatter(both, axis, scatter_dimension=dim, tiled=True), ends, axis=along)
    )


def sum_packed(arrays, axis, dims):
    length = lax.axis_size(axis)
    pieces = [split_up(a, dim, length) for a, dim in zip(arrays, dims)]
    lines = jnp.concatenate([b.reshape(length, -1) for b in pieces], axis=1)
    width = max(16, -(-lines.shape[1] // 1024) * 8)
    lines = jnp.pad(lines, ((0, 0), (0, width * 128 - lines.shape[1]))).reshape(-1, 128)
    ravelled, at, done = (lax.psum_scatter(lines, axis, tiled=True).reshape(-1), 0, [])
    for b in pieces:
        part = b[0]
        done.append(ravelled[at : at + part.size].reshape(part.shape))
        at += part.size
    return tuple(done)


def multiply(pattern, left_side, right_side):
    return jnp.einsum(pattern, left_side, right_side, preferred_element_type=jnp.float32)


def matmul(left_side, right_side):
    return jnp.dot(left_side, right_side, preferred_element_type=jnp.float32)


def contract_rows(left_side, right_side):
    return lax.dot_general(
        left_side, right_side, (((0,), (0,)), ((), ())), preferred_element_type=jnp.float32
    )


def contract_last(left_side, right_side):
    return lax.dot_general(
        left_side, right_side, (((1,), (1,)), ((), ())), preferred_element_type=jnp.float32
    )


def rope_tables(length, head_size):
    position = jnp.arange(length).astype(jnp.float32)
    column = jnp.arange(head_size // 2).astype(jnp.float32)
    frequency = jnp.exp(-math.log(THETA) * 2.0 * column / head_size)
    angles = position[:, None] * frequency[None, :]
    return (jnp.cos(angles), jnp.sin(angles))


def rotate(values, cosine_table, sine_table, direction):
    middle = values.shape[-1] // 2
    leading = values[..., :middle]
    trailing = values[..., middle:]
    cosine = cosine_table[None, :, None, :]
    sine_part = direction * sine_table[None, :, None, :]
    return jnp.concatenate(
        [leading * cosine - trailing * sine_part, trailing * cosine + leading * sine_part], axis=-1
    )


def allowed_mask(size, length):
    row_index = jnp.arange(size)[:, None]
    column_index = jnp.arange(size)[None, :]
    return (column_index <= row_index) & (column_index < length)


def attend(queries, key_heads, value_heads, tangent_queries, tangent_keys, tangent_values, length):
    repeat = queries.shape[1] // key_heads.shape[1]
    key_heads = jnp.repeat(key_heads, repeat, axis=1)
    value_heads = jnp.repeat(value_heads, repeat, axis=1)
    tangent_keys = jnp.repeat(tangent_keys, repeat, axis=1)
    tangent_values = jnp.repeat(tangent_values, repeat, axis=1)
    scaling = 1.0 / math.sqrt(queries.shape[-1])
    allowed = allowed_mask(queries.shape[0], length)[None]
    scores = multiply("ihd,jhd->hij", queries, key_heads) * scaling
    powers = jnp.where(allowed, jnp.exp(scores), 0.0)
    weights = powers / jnp.sum(powers, axis=-1, keepdims=True)
    weights_low = weights.astype(jnp.bfloat16)
    blended = multiply("hij,jhd->ihd", weights_low, value_heads).astype(jnp.bfloat16)
    tangent_scores = (
        multiply("ihd,jhd->hij", tangent_queries, key_heads)
        + multiply("ihd,jhd->hij", queries, tangent_keys)
    ) * scaling
    tangent_weights = weights * (
        tangent_scores - jnp.sum(weights * tangent_scores, axis=-1, keepdims=True)
    )
    tangent_blended = multiply(
        "hij,jhd->ihd", tangent_weights.astype(jnp.bfloat16), value_heads
    ) + multiply("hij,jhd->ihd", weights_low, tangent_values)
    return (blended, tangent_blended.astype(jnp.bfloat16))


def attend_back(queries, key_heads, value_heads, grad_mixed, length):
    repeat = queries.shape[1] // key_heads.shape[1]
    key_heads = jnp.repeat(key_heads, repeat, axis=1)
    value_heads = jnp.repeat(value_heads, repeat, axis=1)
    scaling = 1.0 / math.sqrt(queries.shape[-1])
    allowed = allowed_mask(queries.shape[0], length)[None]
    scores = multiply("ihd,jhd->hij", queries, key_heads) * scaling
    powers = jnp.where(allowed, jnp.exp(scores), 0.0)
    weights = powers / jnp.sum(powers, axis=-1, keepdims=True)
    weights_low = weights.astype(jnp.bfloat16)
    grad_weights = multiply("ihd,jhd->hij", grad_mixed, value_heads)
    grad_values = multiply("hij,ihd->jhd", weights_low, grad_mixed)
    grad_scores = (
        weights * (grad_weights - jnp.sum(weights * grad_weights, axis=-1, keepdims=True)) * scaling
    ).astype(jnp.bfloat16)
    grad_queries = multiply("hij,jhd->ihd", grad_scores, key_heads)
    grad_keys = multiply("hij,ihd->jhd", grad_scores, queries)
    return (grad_queries, grad_keys, grad_values)


def normalize(stream, gain_row):
    wide_stream = stream.astype(jnp.float32)
    inverse = lax.rsqrt(jnp.mean(wide_stream * wide_stream, axis=-1, keepdims=True) + EPS)
    return (wide_stream, inverse, (wide_stream * inverse * gain_row).astype(jnp.bfloat16))


def norm_tangent(wide_stream, inverse, tangent, gain_row):
    shift = jnp.mean(wide_stream * tangent, axis=-1, keepdims=True)
    return (
        gain_row * (tangent * inverse - wide_stream * inverse * inverse * inverse * shift)
    ).astype(jnp.bfloat16)


def norm_back(wide_stream, inverse, grad_normed, gain_row):
    scaled = grad_normed * gain_row
    shift = jnp.mean(wide_stream * scaled, axis=-1, keepdims=True)
    return inverse * (scaled - wide_stream * inverse * inverse * shift)


def body(
    tokens,
    lengths,
    norm_gains,
    query_weight,
    key_weight,
    value_weight,
    out_weight,
    query_probe,
    key_probe,
    value_probe,
    out_probe,
):
    tensor_count = lax.axis_size("tensor")
    tensor_index = lax.axis_index("tensor")
    data_index = lax.axis_index("dp")
    share_rows = tokens.shape[0]
    group_rows = share_rows * tensor_count
    seq_count = group_rows // LEN
    layer_count = query_weight.shape[0]
    half_width = key_weight.shape[2]
    cosine_table, sine_table = rope_tables(LEN, HD)
    group_lengths = lax.dynamic_slice_in_dim(lengths, data_index * seq_count, seq_count)
    position = jnp.arange(group_rows) % LEN
    group_mask = (position < jnp.repeat(group_lengths, LEN)).astype(jnp.float32)
    share_mask = lax.dynamic_slice_in_dim(group_mask, tensor_index * share_rows, share_rows)
    lower_half = tensor_index % 2 == 0

    def heads_of(values):
        return values.reshape(seq_count, LEN, -1, HD)

    def join_halves(own_part, other_part):
        return jnp.where(
            lower_half,
            jnp.concatenate([own_part, other_part], axis=-1),
            jnp.concatenate([other_part, own_part], axis=-1),
        )

    def own_columns(values):
        return jnp.where(lower_half, values[:, :half_width], values[:, half_width:])

    def other_columns(values):
        return jnp.where(lower_half, values[:, half_width:], values[:, :half_width])

    query_full_probe, key_own_probe, value_own_probe, out_full_probe = turned_gather(
        (query_probe, key_probe, value_probe, out_probe), "dp", (1, 1, 1, 2)
    )
    owned_parts = (key_weight, value_weight, key_own_probe, value_own_probe)
    key_full, value_full, key_full_probe, value_full_probe = owned_parts
    stream = tokens
    tangent = None
    stored = []
    for layer_index in range(layer_count):
        final_layer = layer_index == layer_count - 1
        gain_row = norm_gains[layer_index]
        wide_stream, inverse, normed = normalize(stream, gain_row)
        tangent_normed = (
            None if tangent is None else norm_tangent(wide_stream, inverse, tangent, gain_row)
        )
        if tangent_normed is None:
            normed_all = lax.all_gather(normed, "tensor", axis=0, tiled=True)
            tangent_all = None
        else:
            normed_all, tangent_all = sent_together((normed, tangent_normed), "tensor", 0, 1)

        def project(weight, probe_part):
            primal = matmul(normed_all, weight)
            moved_part = matmul(normed_all, probe_part)
            if tangent_all is not None:
                moved_part = moved_part + matmul(tangent_all, weight)
            return (primal, moved_part)

        query_primal, query_moved = project(
            query_weight[layer_index], query_full_probe[layer_index]
        )
        key_primal, key_moved = project(key_full[layer_index], key_full_probe[layer_index])
        value_primal, value_moved = project(value_full[layer_index], value_full_probe[layer_index])
        own_projections = (key_primal, key_moved, value_primal, value_moved)
        other_projections = (
            swapped(own_projections[0].astype(jnp.bfloat16), "tensor", 0).astype(jnp.float32),
            swapped(own_projections[1].astype(jnp.bfloat16), "tensor", 0).astype(jnp.float32),
            swapped(own_projections[2].astype(jnp.bfloat16), "tensor", 0).astype(jnp.float32),
            swapped(own_projections[3].astype(jnp.bfloat16), "tensor", 0).astype(jnp.float32),
        )
        key_primal, key_moved, value_primal, value_moved = [
            join_halves(own_part, other_part)
            for own_part, other_part in zip(own_projections, other_projections)
        ]
        queries = rotate(heads_of(query_primal), cosine_table, sine_table, 1.0).astype(jnp.bfloat16)
        key_heads = rotate(heads_of(key_primal), cosine_table, sine_table, 1.0).astype(jnp.bfloat16)
        value_heads = heads_of(value_primal).astype(jnp.bfloat16)
        tangent_queries = rotate(heads_of(query_moved), cosine_table, sine_table, 1.0).astype(
            jnp.bfloat16
        )
        tangent_keys = rotate(heads_of(key_moved), cosine_table, sine_table, 1.0).astype(
            jnp.bfloat16
        )
        tangent_values = heads_of(value_moved).astype(jnp.bfloat16)
        blended, tangent_blended = lax.map(
            lambda pieces: attend(*pieces),
            (
                queries,
                key_heads,
                value_heads,
                tangent_queries,
                tangent_keys,
                tangent_values,
                group_lengths,
            ),
        )
        blended = blended.reshape(group_rows, -1)
        tangent_blended = tangent_blended.reshape(group_rows, -1)
        tangent_part = matmul(tangent_blended, out_weight[layer_index]) + matmul(
            blended, out_full_probe[layer_index]
        )
        if final_layer:
            tangent_sum = sum_at_owner(tangent_part.astype(jnp.bfloat16), "tensor", 0)
        else:
            primal_part = matmul(blended, out_weight[layer_index])
            primal_sum, tangent_sum = tuple(
                (
                    part.astype(jnp.float32)
                    for part in side_by_side(
                        (primal_part.astype(jnp.bfloat16), tangent_part.astype(jnp.bfloat16)),
                        "tensor",
                        0,
                        1,
                    )
                )
            )
        stored.append((wide_stream, inverse, normed_all, queries, key_heads, value_heads, blended))
        if not final_layer:
            stream = (wide_stream + primal_sum).astype(jnp.bfloat16)
        tangent = tangent_sum if tangent is None else tangent + tangent_sum
    cotangent = share_mask[:, None] * tangent
    collected = [None] * layer_count
    for layer_index in reversed(range(layer_count)):
        wide_stream, inverse, normed_all, queries, key_heads, value_heads, blended = stored[
            layer_index
        ]
        cotangent_low = cotangent.astype(jnp.bfloat16)
        cotangent_low = lax.all_gather(cotangent_low, "tensor", axis=0, tiled=True)
        out_product = contract_rows(blended, cotangent_low)
        grad_mixed = contract_last(cotangent_low, out_weight[layer_index]).astype(jnp.bfloat16)
        grad_queries, grad_keys, grad_values = lax.map(
            lambda pieces: attend_back(*pieces),
            (queries, key_heads, value_heads, heads_of(grad_mixed), group_lengths),
        )
        key_count = key_heads.shape[2]
        query_low = (
            rotate(grad_queries, cosine_table, sine_table, -1.0)
            .astype(jnp.bfloat16)
            .reshape(group_rows, -1)
        )
        key_grouped = grad_keys.reshape(seq_count, LEN, key_count, -1, HD).sum(axis=3)
        key_low = (
            rotate(key_grouped, cosine_table, sine_table, -1.0)
            .astype(jnp.bfloat16)
            .reshape(group_rows, -1)
        )
        value_low = (
            grad_values.reshape(seq_count, LEN, key_count, -1, HD)
            .sum(axis=3)
            .astype(jnp.bfloat16)
            .reshape(group_rows, -1)
        )
        query_product = contract_rows(normed_all, query_low)
        key_mine = own_columns(key_low)
        value_mine = own_columns(value_low)
        key_recv, value_recv = swapped(
            (other_columns(key_low), other_columns(value_low)), "tensor", 0
        )
        key_product = contract_rows(normed_all, key_mine) + contract_rows(normed_all, key_recv)
        value_product = contract_rows(normed_all, value_mine) + contract_rows(
            normed_all, value_recv
        )
        collected[layer_index] = tuple(
            (
                part.astype(jnp.float32)
                for part in sum_packed(
                    (
                        query_product.astype(jnp.bfloat16),
                        key_product.astype(jnp.bfloat16),
                        value_product.astype(jnp.bfloat16),
                        out_product.astype(jnp.bfloat16),
                    ),
                    "dp",
                    (0, 0, 0, 1),
                )
            )
        )
        if layer_index > 0:
            grad_part = contract_last(query_low, query_weight[layer_index])
            key_own_weight = key_full[layer_index]
            value_own_weight = value_full[layer_index]
            grad_part = (
                grad_part
                + contract_last(key_mine, key_own_weight)
                + contract_last(key_recv, key_own_weight)
            )
            grad_part = (
                grad_part
                + contract_last(value_mine, value_own_weight)
                + contract_last(value_recv, value_own_weight)
            )
            grad_normed = sum_at_owner(grad_part.astype(jnp.bfloat16), "tensor", 0)
            cotangent = cotangent + norm_back(
                wide_stream, inverse, grad_normed, norm_gains[layer_index]
            )
    query_stack = jnp.stack([collected[number][0] for number in range(layer_count)])
    key_stack = jnp.stack([collected[number][1] for number in range(layer_count)])
    value_stack = jnp.stack([collected[number][2] for number in range(layer_count)])
    out_stack = jnp.stack([collected[number][3] for number in range(layer_count)])
    return (query_stack, key_stack, value_stack, out_stack)


def solution(mesh):
    placed = (
        P(("dp", "tensor"), None),
        P(),
        P(),
        P(None, None, "tensor"),
        P(None, None, "tensor"),
        P(None, None, "tensor"),
        P(None, "tensor", None),
        P(None, "dp", "tensor"),
        P(None, "dp", "tensor"),
        P(None, "dp", "tensor"),
        P(None, "tensor", "dp"),
    )
    return jax.shard_map(
        body,
        mesh=mesh,
        in_specs=placed,
        out_specs=(
            P(None, "dp", "tensor"),
            P(None, "dp", "tensor"),
            P(None, "dp", "tensor"),
            P(None, "tensor", "dp"),
        ),
        check_vma=False,
    )
```

profile of v0, /device:TPU:1, one launch (start us, length us, event | category | flops | bytes accessed | tf_op | source)
XLA Modules:
  0.0 920.6 jit_solution(7696534953255749129)
XLA Ops:
  12.1 2.3 pad_maximum_fusion.3
  14.5 3.8 slice_bitcast_fusion.7
  18.3 3.0 copy.49
  24.2 38.5 %all-gather.6.cloned.1.call-done = bf16[256,4096]{1,0:T(8,128)(2,1)} async-done(((bf16[16,4096]{1,0:T(8,128)(2,1)}), bf16[256,4096]{1,0:T(8,128)(2,1)}) %all-gather.6.cloned.1.call-update) | async-done | bytes 2097168 | tf_op jit(solution)/shard_map/all_gather | solution.py:246
  62.7 2.6 fusion.105
  68.9 201.5 %all-gather.8.cloned.1.call-done = bf16[4096,1280]{0,1:T(8,128)(2,1)} async-done(((bf16[512,1280]{0,1:T(8,128)(2,1)}), bf16[4096,1280]{0,1:T(8,128)(2,1)}) %all-gather.8.cloned.1.call-update) | async-done | bytes 10485776 | tf_op jit(solution)/shard_map/all_gather | solution.py:19
  275.2 5.2 fusion.350
  290.1 2.3 multiply_reduce_fusion.3
  292.5 2.3 fusion.140
  300.0 2.5 convolution_convert_fusion.4
  305.7 2.4 pad_maximum_fusion.2
  308.5 79.9 %reduce-scatter.4.cloned.1.call-done = bf16[16,8192]{1,0:T(8,128)(2,1)} async-done(((bf16[256,8192]{1,0:T(8,128)(2,1)}), bf16[16,8192]{1,0:T(8,128)(2,1)}) %reduce-scatter.4.cloned.1.call-update) | async-done | bytes 262160 | tf_op jit(solution)/shard_map/reduce_scatter | solution.py:58
  391.9 4.1 copy.64
  396.0 52.8 %all-gather.10.cloned.1.call-done = bf16[256,8192]{1,0:T(8,128)(2,1)} async-done(((bf16[16,8192]{1,0:T(8,128)(2,1)}), bf16[256,8192]{1,0:T(8,128)(2,1)}) %all-gather.10.cloned.1.call-update) | async-done | bytes 4194320 | tf_op jit(solution)/shard_map/all_gather | solution.py:30
  448.9 2.6 fusion.91
  451.5 2.4 fusion.361
  474.6 2.4 multiply_reduce_fusion.2
  477.0 2.4 fusion.141
  484.6 2.5 fusion.13
  489.5 4.4 all-to-all-start
  494.0 10.1 %all-gather.12.cloned.1.call-start = ((), (), s32[]{:S(2)}) async-start(), calls=%async_computation.9 | async-start | bytes 2228224 | tf_op jit(solution)/shard_map/all_gather | solution.py:327
  505.2 17.3 %all-to-all-done = bf16[16,16,4096]{2,1,0:T(8,128)(2,1)} async-done(((bf16[16,16,4096]{2,1,0:T(8,128)(2,1)}), bf16[16,16,4096]{2,1,0:T(8,128)(2,1)}, u32[]{:S(2)}, u32[]{:S(2)}) %all-to-all-start) | async-done | bytes 2097184 | tf_op jit(solution)/shard_map/all_to_all | solution.py:47
  526.1 48.3 %all-gather.12.cloned.1.call-done = bf16[256,4096]{1,0:T(8,128)(2,1)} async-done(((bf16[16,4096]{1,0:T(8,128)(2,1)}), bf16[256,4096]{1,0:T(8,128)(2,1)}) %all-gather.12.cloned.1.call-update) | async-done | bytes 2097168 | tf_op jit(solution)/shard_map/all_gather | solution.py:327
  574.4 3.6 fusion.71
  582.2 2.6 convolution_bitcast_fusion.5
  584.8 2.6 convolution_bitcast_fusion.1
  596.2 4.6 all-to-all-start.1
  600.9 2.3 convolution_convert_fusion
  603.2 2.3 copy.119
  608.3 3.8 reshape_reshape.21
  612.1 2.3 fusion.265
  617.8 2.4 copy.86
  620.1 2.8 reshape_reshape.22
  623.0 2.9 fusion.9
  632.8 19.3 %pad_maximum_fusion.1 = bf16[8,327680]{1,0:T(8,128)(2,1)} fusion(bf16[8,131072]{1,0:T(8,128)(2,1)} %bitcast.295, bf16[8,32768]{1,0:T(8,128)(2,1)S(1)} %copy-done.19, bf16[8,32768]{1,0:T(8,128)(2,1)S(1)} %copy-done.18, bf16[8,131072]{1,0:T(8,128)(2,1)} %reshape_reshape.21), kind=kLoop, calls=%fused_computation.9 | loop fusion | flops 20971520 | bytes 10485760 | tf_op jit(solution)/shard_map/concatenate | solution.py:65
  652.0 7.2 reshape.1041
  659.3 22.8 %all-gather.14.cloned.1.call-done = bf16[256,4096]{1,0:T(8,128)(2,1)} async-done(((bf16[16,4096]{1,0:T(8,128)(2,1)}), bf16[256,4096]{1,0:T(8,128)(2,1)}) %all-gather.14.cloned.1.call-update) | async-done | bytes 2097168 | tf_op jit(solution)/shard_map/all_gather | solution.py:327
  682.1 3.0 fusion.68
  689.8 2.3 convolution_convert_fusion.2
  692.1 2.2 copy.118
  699.5 3.9 reshape_reshape.18
  703.4 2.5 fusion.7
  706.0 2.4 copy.85
  708.3 2.8 reshape_reshape.20
  715.7 16.9 %pad_maximum_fusion = bf16[8,327680]{1,0:T(8,128)(2,1)} fusion(bf16[8,131072]{1,0:T(8,128)(2,1)S(1)} %bitcast.294, bf16[8,32768]{1,0:T(8,128)(2,1)} %reshape_reshape.20, bf16[8,32768]{1,0:T(8,128)(2,1)} %reshape_reshape.19, bf16[8,131072]{1,0:T(8,128)(2,1)} %reshape_reshape.18), kind=kLoop, calls=%fused_computation.8 | loop fusion | flops 20971520 | bytes 10485760 | tf_op jit(solution)/shard_map/concatenate | solution.py:65
  732.7 7.3 reshape.1038
  740.0 53.7 %reduce-scatter.8.cloned.1.call-done = bf16[2560,128]{1,0:T(8,128)(2,1)} async-done(((bf16[20480,128]{1,0:T(8,128)(2,1)}), bf16[2560,128]{1,0:T(8,128)(2,1)}) %reduce-scatter.8.cloned.1.call-update) | async-done | bytes 655376 | tf_op jit(solution)/shard_map/reduce_scatter | solution.py:68
  796.1 111.0 %reduce-scatter.6.cloned.1.call-done = bf16[2560,128]{1,0:T(8,128)(2,1)} async-done(((bf16[20480,128]{1,0:T(8,128)(2,1)}), bf16[2560,128]{1,0:T(8,128)(2,1)}) %reduce-scatter.6.cloned.1.call-update) | async-done | bytes 655376 | tf_op jit(solution)/shard_map/reduce_scatter | solution.py:68
  (300 shorter events, 120.1 us)
Async XLA Ops:
  7.2 55.5 %all-gather.6.cloned.1.call-start = ((), (), s32[]{:S(2)}) async-start(), calls=%async_computation.5 | async-start | bytes 2228224 | tf_op jit(solution)/shard_map/all_gather | solution.py:246
  10.8 259.6 %all-gather.8.cloned.1.call-start = ((), (), s32[]{:S(2)}) async-start(), calls=%async_computation.6 | async-start | bytes 11796480 | tf_op jit(solution)/shard_map/all_gather | solution.py:19
  14.4 373.9 %reduce-scatter.4.cloned.1.call-start = ((), (), s32[]{:S(2)}) async-start(), calls=%async_computation.7 | async-start | bytes 4456448 | tf_op jit(solution)/shard_map/reduce_scatter | solution.py:58
  18.3 47.3 %copy-start.12 = (bf16[2,4096,64]{1,2,0:T(8,128)(2,1)S(1)}, bf16[2,4096,64]{1,2,0:T(8,128)(2,1)}, u32[]{:S(2)}) copy-start(bf16[2,4096,64]{1,2,0:T(8,128)(2,1)} %param.15) | copy-start | bytes 3145732
  24.2 439.6 %copy-start.22 = (f32[256,64]{0,1:T(8,128)}, f32[256,64]{0,1:T(8,128)S(1)}, u32[]{:S(2)}) copy-start(f32[256,64]{0,1:T(8,128)S(1)} %get-tuple-element.175) | copy-start | bytes 196612
  62.7 4.0 copy-start.21
  65.3 2.9 collective-permute-start.1
  66.4 2.5 collective-permute-start
  273.5 22.7 %collective-permute-start.3 = (bf16[256,64]{0,1:T(8,128)(2,1)}, bf16[256,64]{0,1:T(8,128)(2,1)}, u32[]{:S(2)}, u32[]{:S(2)}) collective-permute-start(bf16[256,64]{0,1:T(8,128)(2,1)} %fusion.92), channel_id=1, source_target_pairs={{0,1},{1,0},{2,3},{3,2},{4,5},{5,4},{6,7},{7,6},{8,9},{9,8},{10,11... | collective-permute-start | bytes 98312 | tf_op jit(solution)/shard_map/ppermute | solution.py:37
  275.1 9.0 collective-permute-start.2
  284.1 13.6 %copy-start.37 = (bf16[256,2,64]{0,2,1:T(8,128)(2,1)}, bf16[256,2,64]{0,2,1:T(8,128)(2,1)S(1)}, u32[]{:S(2)}) copy-start(bf16[256,2,64]{0,2,1:T(8,128)(2,1)S(1)} %get-tuple-element.153) | copy-start | bytes 196612
  284.1 13.6 %copy-start.39 = (bf16[256,2,64]{0,2,1:T(8,128)(2,1)}, bf16[256,2,64]{0,2,1:T(8,128)(2,1)S(1)}, u32[]{:S(2)}) copy-start(bf16[256,2,64]{0,2,1:T(8,128)(2,1)S(1)} %get-tuple-element.154) | copy-start | bytes 196612
  289.1 3.3 copy-start.45
  296.2 7.3 copy-start.26
  308.2 80.2 %copy-start.30 = (bf16[16,4096]{1,0:T(8,128)(2,1)S(1)}, bf16[16,4096]{1,0:T(8,128)(2,1)}, u32[]{:S(2)}) copy-start(bf16[16,4096]{1,0:T(8,128)(2,1)} %param.11) | copy-start | bytes 393220
  308.2 140.7 %all-gather.10.cloned.1.call-start = ((), (), s32[]{:S(2)}) async-start(), calls=%async_computation.8 | async-start | bytes 4456448 | tf_op jit(solution)/shard_map/all_gather | solution.py:30
  448.9 5.4 copy-start.1
  453.9 10.6 %collective-permute-start.6 = (bf16[256,64]{0,1:T(8,128)(2,1)S(1)}, bf16[256,64]{0,1:T(8,128)(2,1)S(1)}, u32[]{:S(2)}, u32[]{:S(2)}) collective-permute-start(bf16[256,64]{0,1:T(8,128)(2,1)S(1)} %get-tuple-element.186), channel_id=1, source_target_pairs={{0,1},{1,0},{2,3},{3,2},{4,5},{5,4},{6,7},{7,6},{8,9},{9,8},{10,11... | collective-permute-start | bytes 98312 | tf_op jit(solution)/shard_map/ppermute | solution.py:37
  455.1 9.5 %collective-permute-start.4 = (bf16[256,64]{0,1:T(8,128)(2,1)S(1)}, bf16[256,64]{0,1:T(8,128)(2,1)S(1)}, u32[]{:S(2)}, u32[]{:S(2)}) collective-permute-start(bf16[256,64]{0,1:T(8,128)(2,1)S(1)} %fusion.103), channel_id=1, source_target_pairs={{0,1},{1,0},{2,3},{3,2},{4,5},{5,4},{6,7},{7,6},{8,9},{9,8},{10,11... | collective-permute-start | bytes 98312 | tf_op jit(solution)/shard_map/ppermute | solution.py:37
  456.1 3.3 copy-start.7
  457.5 23.3 %collective-permute-start.7 = (bf16[256,64]{0,1:T(8,128)(2,1)}, bf16[256,64]{0,1:T(8,128)(2,1)}, u32[]{:S(2)}, u32[]{:S(2)}) collective-permute-start(bf16[256,64]{0,1:T(8,128)(2,1)} %fusion.79), channel_id=1, source_target_pairs={{0,1},{1,0},{2,3},{3,2},{4,5},{5,4},{6,7},{7,6},{8,9},{9,8},{10,11... | collective-permute-start | bytes 98312 | tf_op jit(solution)/shard_map/ppermute | solution.py:37
  459.2 6.1 collective-permute-start.5
  472.7 4.3 copy-start.49
  474.6 4.8 copy-start.41
  474.6 4.8 copy-start.42
  480.8 6.3 copy-start.33
  489.5 32.9 %all-to-all-start = ((bf16[16,16,4096]{2,1,0:T(8,128)(2,1)}), bf16[16,16,4096]{2,1,0:T(8,128)(2,1)}, u32[]{:S(2)}, u32[]{:S(2)}) async-start(bf16[16,16,4096]{2,1,0:T(8,128)(2,1)} %bitcast.299), calls=%async_computation.1 | async-start | bytes 4194304 | tf_op jit(solution)/shard_map/all_to_all | solution.py:47
  494.0 80.4 %all-gather.12.cloned.1.call-start = ((), (), s32[]{:S(2)}) async-start(), calls=%async_computation.9 | async-start | bytes 2228224 | tf_op jit(solution)/shard_map/all_gather | solution.py:327
  588.2 3.0 copy-start.23
  588.2 3.1 copy-start.8
  590.2 3.5 collective-permute-start.9
  590.9 2.0 collective-permute-start.8
  596.2 4.6 copy-start.34
  596.2 33.1 %all-to-all-start.1 = ((bf16[16,16,4096]{2,1,0:T(8,128)(2,1)}), bf16[16,16,4096]{2,1,0:T(8,128)(2,1)}, u32[]{:S(2)}, u32[]{:S(2)}) async-start(bf16[16,16,4096]{2,1,0:T(8,128)(2,1)} %bitcast.296), calls=%async_computation.2 | async-start | bytes 4194304 | tf_op jit(solution)/shard_map/all_to_all | solution.py:47
  600.8 81.3 %all-gather.14.cloned.1.call-start = ((), (), s32[]{:S(2)}) async-start(), calls=%async_computation.10 | async-start | bytes 2228224 | tf_op jit(solution)/shard_map/all_gather | solution.py:327
  600.8 4.7 copy-start.29
  612.1 4.4 copy-start.3
  629.0 3.7 copy-start.18
  629.0 3.8 copy-start.19
  632.3 161.4 %reduce-scatter.8.cloned.1.call-start = ((), (), s32[]{:S(2)}) async-start(), calls=%async_computation.12 | async-start | bytes 5898240 | tf_op jit(solution)/shard_map/reduce_scatter | solution.py:68
  659.3 25.8 %copy-start.38 = (bf16[256,2,64]{0,2,1:T(8,128)(2,1)S(1)}, bf16[256,2,64]{0,2,1:T(8,128)(2,1)}, u32[]{:S(2)}) copy-start(bf16[256,2,64]{0,2,1:T(8,128)(2,1)} %copy-done.37) | copy-start | bytes 196612
  659.3 25.8 %copy-start.40 = (bf16[256,2,64]{0,2,1:T(8,128)(2,1)S(1)}, bf16[256,2,64]{0,2,1:T(8,128)(2,1)}, u32[]{:S(2)}) copy-start(bf16[256,2,64]{0,2,1:T(8,128)(2,1)} %copy-done.39) | copy-start | bytes 196612
  659.3 25.8 %copy-start.48 = (bf16[256,128]{0,1:T(8,128)(2,1)S(1)}, bf16[256,128]{0,1:T(8,128)(2,1)}, u32[]{:S(2)}) copy-start(bf16[256,128]{0,1:T(8,128)(2,1)} %copy-done.47) | copy-start | bytes 196612
  659.3 247.8 %reduce-scatter.6.cloned.1.call-start = ((), (), s32[]{:S(2)}) async-start(), calls=%async_computation.11 | async-start | bytes 5898240 | tf_op jit(solution)/shard_map/reduce_scatter | solution.py:68
  685.1 4.6 copy-start.27
  694.4 9.1 collective-permute-start.11
  695.2 16.0 %collective-permute-start.10 = (bf16[256,64]{0,1:T(8,128)(2,1)S(1)}, bf16[256,64]{0,1:T(8,128)(2,1)S(1)}, u32[]{:S(2)}, u32[]{:S(2)}) collective-permute-start(bf16[256,64]{0,1:T(8,128)(2,1)S(1)} %get-tuple-element.88), channel_id=1, source_target_pairs={{0,1},{1,0},{2,3},{3,2},{4,5},{5,4},{6,7},{7,6},{8,9},{9,8},{10,11... | collective-permute-start | bytes 98312 | tf_op jit(solution)/shard_map/ppermute | solution.py:37
  712.4 3.3 copy-start.11
  (43 other events, 90.4 us)
Sparse Core Ops, SparseCore 0:
  10.9 51.6 all-gather.5
  64.3 206.0 all-gather.7
  308.3 80.0 reduce-scatter.3
  392.0 56.7 all-gather.9
  526.2 48.1 all-gather.11
  632.4 49.6 all-gather.13
  684.5 109.1 reduce-scatter.7
  796.1 111.0 reduce-scatter.5
where the time goes:
time: 932 us; the launch traced here: 921 us
  waiting for transfers between devices  626 us (67%)
  matrix products  104 us (11%)
  local copies, waits for them, and re-layouts  81 us (9%)
  other arithmetic  70.1 us (8%)
  starting transfers between devices  24.2 us (3%)
  between operations  15.4 us (2%)
    all_gather x1, waiting for transfers between devices, turned_gather(): result, at, done = (lax.all_gather(both, axis, axis=0, tiled=True), 0, [])  201 us
    reduce_scatter x2, waiting for transfers between devices, sum_packed(): lax.psum_scatter(lines, axis, tiled=True).reshape(-1)  165 us
    reduce_scatter x1, waiting for transfers between devices, side_by_side(): lax.psum_scatter(both, axis, scatter_dimension=dim, tiled=True)  79.9 us
    all_gather x2, waiting for transfers between devices, body(): cotangent_low = lax.all_gather(cotangent_low, 'tensor', axis=0, tiled=True)  71.1 us
    all_gather x1, waiting for transfers between devices, sent_together(): result = lax.all_gather(both, axis, axis=dim, tiled=True)  52.8 us
    all_gather x1, waiting for transfers between devices, body(): normed_all = lax.all_gather(normed, 'tensor', axis=0, tiled=True)  38.5 us
    concatenate x2, other arithmetic, sum_packed(): lines = jnp.concatenate([b.reshape(length, -1) for b in pieces], axis=1)  36.2 us
    dot_general x20, matrix products, multiply(): jnp.einsum(pattern, left_side, right_side, preferred_element_type=jnp.flo...  35.1 us
  transfers between devices with their start and end apart: 22, of which 10 were waited for; matrix products, arithmetic and copies ran while one was open for 20% of the time, Pallas kernels for 0%

commit v1 on v0

v1 whole, which is shorter than its diff:
```python
import functools
import math

import jax
import jax.numpy as jnp
from jax import lax
from jax.experimental import pallas as pl
from jax.experimental.pallas import tpu as pltpu
from jax.sharding import PartitionSpec as P

HD = 128
LEN = 256
EPS = 1e-05
THETA = 500000.0

MESH = pl.DeviceIdType.MESH
F32 = jnp.float32
BF16 = jnp.bfloat16
VMEM = pl.BlockSpec(memory_space=pltpu.VMEM)
HBM = pl.BlockSpec(memory_space=pl.ANY)
DMA = pltpu.SemaphoreType.DMA

HOPS = ((1, 1), (3, 1), (2, 1), (2, 0), (1, 0), (3, 0), (0, 1))


def back(hop):
    return ((4 - hop[0]) % 4, hop[1])


def data_at(d, hop):
    ring, pair = lax.div(d, 2), lax.rem(d, 2)
    return lax.rem(ring + hop[0], 4) * 2 + lax.rem(pair + hop[1], 2)


def chip_at(t, hop):
    return data_at(lax.div(t, 2), hop)


def tensor_at(t, hop):
    return chip_at(t, hop) * 2 + lax.rem(t, 2)


def other_core(t):
    return t + 1 - 2 * lax.rem(t, 2)


def places():
    return lax.axis_index("dp"), lax.axis_index("tensor")


def remote(src, dst, sends, recvs, j, device):
    return pltpu.make_async_remote_copy(
        src_ref=src,
        dst_ref=dst,
        send_sem=sends.at[j],
        recv_sem=recvs.at[j],
        device_id=device,
        device_id_type=MESH,
    )


def enter(over_tensor, over_data):
    d, t = places()
    barrier = pltpu.get_barrier_semaphore()
    peers = [(d, other_core(t))]
    if over_tensor:
        peers += [(d, tensor_at(t, hop)) for hop in HOPS]
    if over_data:
        peers += [(data_at(d, hop), t) for hop in HOPS]
    for peer in peers:
        pl.semaphore_signal(barrier, inc=1, device_id=peer, device_id_type=MESH)
    pl.semaphore_wait(barrier, len(peers))


class TensorGather:
    scratch = [DMA((16,)), DMA((16,))]

    def __init__(self, src, out, sends, recvs):
        self.src, self.out, self.sends, self.recvs = src, out, sends, recvs

    def cross(self, j):
        d, t = places()
        return remote(self.src, self.out.at[t], self.sends, self.recvs, j, (d, tensor_at(t, HOPS[j])))

    def arrived(self, j):
        d, t = places()
        slot = self.out.at[tensor_at(t, back(HOPS[j]))]
        return remote(slot, slot, self.sends, self.recvs, j, (d, other_core(t)))

    def handed(self, j):
        d, t = places()
        slot = self.out.at[tensor_at(t, back(HOPS[j]))]
        return remote(slot, slot, self.sends, self.recvs, 8 + j, (d, other_core(t)))

    def received(self, j):
        d, t = places()
        slot = self.out.at[tensor_at(other_core(t), back(HOPS[j]))]
        return remote(slot, slot, self.sends, self.recvs, 8 + j, (d, other_core(t)))

    def near(self):
        d, t = places()
        return remote(self.src, self.out.at[t], self.sends, self.recvs, 7, (d, other_core(t)))

    def own(self):
        d, t = places()
        return pltpu.make_async_copy(self.src, self.out.at[t], self.sends.at[15])

    def start(self):
        for j in range(7):
            self.cross(j).start()
        self.near().start()
        self.own().start()

    def finish(self):
        d, t = places()
        for j in (6, 4, 5, 3, 0, 1, 2):
            self.arrived(j).wait_recv()
            self.handed(j).start()
        slot = self.out.at[other_core(t)]
        remote(slot, slot, self.sends, self.recvs, 7, (d, other_core(t))).wait_recv()
        for j in (6, 4, 5, 3, 0, 1, 2):
            self.received(j).wait_recv()
            self.cross(j).wait_send()
            self.handed(j).wait_send()
        self.near().wait_send()
        self.own().wait()


class TensorSum:
    @staticmethod
    def scratch(columns):
        return [
            pltpu.VMEM((8, 16, columns), BF16),
            pltpu.VMEM((7, 16, columns), BF16),
            pltpu.VMEM((7, 16, columns), BF16),
            DMA((15,)),
            DMA((15,)),
        ]

    def __init__(self, part, near, sent, far, sends, recvs):
        self.part, self.near_, self.sent, self.far = part, near, sent, far
        self.sends, self.recvs = sends, recvs

    def swap(self, j):
        d, t = places()
        k = chip_at(t, HOPS[j] if j < 7 else (0, 0))
        c = lax.rem(t, 2)
        return remote(
            self.part.at[k, 1 - c], self.near_.at[k], self.sends, self.recvs, j, (d, other_core(t))
        )

    def cross(self, j):
        d, t = places()
        return remote(
            self.sent.at[j], self.far.at[j], self.sends, self.recvs, 8 + j, (d, tensor_at(t, HOPS[j]))
        )

    def pair_sum(self, k):
        d, t = places()
        c = lax.rem(t, 2)
        return self.part[k, c].astype(F32) + self.near_[k].astype(F32)

    def start(self):
        for j in range(8):
            self.swap(j).start()

    def send(self):
        d, t = places()
        for j in range(7):
            self.swap(j).wait_recv()
            self.sent[j] = self.pair_sum(chip_at(t, HOPS[j])).astype(BF16)
            self.cross(j).start()

    def total(self):
        d, t = places()
        self.swap(7).wait_recv()
        total = self.pair_sum(chip_at(t, (0, 0)))
        for j in (6, 4, 5, 3, 0, 1, 2):
            self.cross(j).wait_recv()
            total = total + self.far[j].astype(F32)
        return total

    def finish(self):
        for j in range(8):
            self.swap(j).wait_send()
        for j in range(7):
            self.cross(j).wait_send()


class DataGather:
    scratch = [DMA((8,)), DMA((7,))]
    ROUTES = (
        ((0, 1), (0, 0), (0, 1)),
        ((1, 0), (0, 0), (3, 0)),
        ((3, 0), (0, 0), (1, 0)),
        ((2, 0), (0, 0), (2, 0)),
        ((1, 0), (0, 1), (3, 1)),
        ((3, 0), (0, 1), (1, 1)),
        ((0, 1), (2, 0), (2, 1)),
    )

    def __init__(self, src, slot, sends, recvs):
        self.src, self.slot, self.sends, self.recvs = src, slot, sends, recvs

    def out(self, j):
        d, t = places()
        hop, block, unused = self.ROUTES[j]
        slot = self.slot(data_at(d, block))
        src = self.src if j < 4 else slot
        return remote(src, slot, self.sends, self.recvs, j, (data_at(d, hop), t))

    def into(self, j):
        d, t = places()
        slot = self.slot(data_at(d, self.ROUTES[j][2]))
        return remote(slot, slot, self.sends, self.recvs, j, (d, other_core(t)))

    def own(self):
        d, t = places()
        return pltpu.make_async_copy(self.src, self.slot(d), self.sends.at[7])

    def start(self):
        for j in range(4):
            self.out(j).start()
        self.own().start()

    def relay(self):
        self.into(0).wait_recv()
        self.out(4).start()
        self.out(5).start()
        self.into(3).wait_recv()
        self.out(6).start()

    def finish(self):
        for j in (1, 2, 4, 5, 6):
            self.into(j).wait_recv()
        for j in range(7):
            self.out(j).wait_send()
        self.own().wait()


class DataExchange:
    scratch = [DMA((15,)), DMA((14,))]

    def __init__(self, src, out, sends, recvs):
        self.src, self.out_, self.sends, self.recvs = src, out, sends, recvs
        self.half = src.shape[0] // 2
        self.share = src.shape[1] // 8

    def rows(self, t):
        return pl.ds(pl.multiple_of(lax.rem(t, 2) * self.half, self.half), self.half)

    def columns(self, d):
        return pl.ds(pl.multiple_of(d * self.share, self.share), self.share)

    def cross(self, j):
        d, t = places()
        peer = data_at(d, HOPS[j])
        return remote(
            self.src.at[self.rows(t), self.columns(peer)],
            self.out_.at[d, self.rows(t)],
            self.sends,
            self.recvs,
            j,
            (peer, t),
        )

    def hand(self, j, t_of):
        d, t = places()
        slot = self.out_.at[data_at(d, back(HOPS[j])), self.rows(t_of)]
        return slot

    def arrived(self, j):
        d, t = places()
        slot = self.hand(j, t)
        return remote(slot, slot, self.sends, self.recvs, j, (d, other_core(t)))

    def handed(self, j):
        d, t = places()
        slot = self.hand(j, t)
        return remote(slot, slot, self.sends, self.recvs, 7 + j, (d, other_core(t)))

    def received(self, j):
        d, t = places()
        slot = self.hand(j, other_core(t))
        return remote(slot, slot, self.sends, self.recvs, 7 + j, (d, other_core(t)))

    def own(self):
        d, t = places()
        return pltpu.make_async_copy(
            self.src.at[:, self.columns(d)], self.out_.at[d], self.sends.at[14]
        )

    def start(self):
        for j in range(7):
            self.cross(j).start()
        self.own().start()

    def finish(self):
        for j in (6, 4, 5, 3, 0, 1, 2):
            self.arrived(j).wait_recv()
            self.handed(j).start()
        for j in range(7):
            self.received(j).wait_recv()
            self.cross(j).wait_send()
            self.handed(j).wait_send()
        self.own().wait()


def taken(refs, *counts):
    out, at = [], 0
    for count in counts:
        out.append(refs[at : at + count])
        at += count
    return out


def comm_call(kernel, name, number, in_specs, out_specs, out_shape, scratch, args):
    return pl.pallas_call(
        kernel,
        name=name,
        in_specs=in_specs,
        out_specs=out_specs,
        out_shape=out_shape,
        scratch_shapes=scratch,
        compiler_params=pltpu.CompilerParams(
            collective_id=number, has_side_effects=True, vmem_limit_bytes=40 * 2**20
        ),
    )(*args)


def shape(dims, dtype):
    return jax.ShapeDtypeStruct(dims, dtype)


def slot_of(ref):
    return lambda block: ref.at[block]


def columns_of(ref):
    width = ref.shape[1] // 8
    return lambda block: ref.at[:, pl.ds(pl.multiple_of(block * width, width), width)]


def mean_of(values):
    return jnp.sum(values, axis=-1, keepdims=True) * (1.0 / values.shape[-1])


def probe_jobs(layer, probes, gathered, sems):
    q, kv, o = probes
    gq, gkv, go = gathered
    return [
        DataGather(q.at[layer], slot_of(gq), *sems[0:2]),
        DataGather(kv.at[layer], slot_of(gkv), *sems[2:4]),
        DataGather(o.at[layer], columns_of(go), *sems[4:6]),
    ]


def probe_shapes(probes):
    q, kv, o = probes
    return [
        shape((8,) + q.shape[1:], BF16),
        shape((8,) + kv.shape[1:], BF16),
        shape((o.shape[1], 8 * o.shape[2]), BF16),
    ]


def first_kernel(tokens, gain, q, kv, o, h_all, gq, gkv, go, h_low, *sems):
    wide = tokens[...].astype(F32)
    inverse = lax.rsqrt(mean_of(wide * wide) + EPS)
    h_low[...] = (wide * inverse * gain[...]).astype(BF16)
    enter(True, True)
    rows = TensorGather(h_low, h_all, *sems[:2])
    jobs = probe_jobs(0, (q, kv, o), (gq, gkv, go), sems[2:])
    rows.start()
    for job in jobs:
        job.start()
    rows.finish()
    for job in jobs:
        job.relay()
    for job in jobs:
        job.finish()


def first(tokens, gain, probes):
    rows, width = tokens.shape
    return comm_call(
        first_kernel,
        "first",
        1,
        [VMEM, VMEM, HBM, HBM, HBM],
        [VMEM, HBM, HBM, HBM],
        [shape((16, rows, width), BF16)] + probe_shapes(probes),
        [pltpu.VMEM((rows, width), BF16)] + TensorGather.scratch + DataGather.scratch * 3,
        (tokens, gain) + probes,
    )


def between_kernel(*refs):
    (
        (primal, moved, tokens, gain, q, kv, o),
        (x_out, t_out, h_all, th_all, gq, gkv, go),
        (h_low, th_low),
        sum_a,
        sum_b,
        gather_a,
        gather_b,
        sems,
    ) = taken(refs, 7, 7, 2, 5, 5, 2, 2, 6)
    enter(True, True)
    sums = [TensorSum(primal, *sum_a), TensorSum(moved, *sum_b)]
    jobs = probe_jobs(1, (q, kv, o), (gq, gkv, go), sems)
    for one in sums:
        one.start()
    for one in sums:
        one.send()
    for job in jobs:
        job.start()
    stream = (tokens[...].astype(F32) + sums[0].total()).astype(BF16)
    x_out[...] = stream
    wide = stream.astype(F32)
    inverse = lax.rsqrt(mean_of(wide * wide) + EPS)
    h_low[...] = (wide * inverse * gain[...]).astype(BF16)
    rows_a = TensorGather(h_low, h_all, *gather_a)
    tangent = sums[1].total()
    t_out[...] = tangent
    rows_a.start()
    shift = mean_of(wide * tangent)
    th_low[...] = (
        gain[...] * (tangent * inverse - wide * inverse * inverse * inverse * shift)
    ).astype(BF16)
    rows_b = TensorGather(th_low, th_all, *gather_b)
    for job in jobs:
        job.relay()
    rows_b.start()
    for one in sums:
        one.finish()
    rows_a.finish()
    rows_b.finish()
    for job in jobs:
        job.finish()


def between(primal, moved, tokens, gain, probes):
    rows, width = tokens.shape
    return comm_call(
        between_kernel,
        "between",
        2,
        [VMEM] * 4 + [HBM] * 3,
        [VMEM] * 4 + [HBM] * 3,
        [
            shape((rows, width), BF16),
            shape((rows, width), F32),
            shape((16, rows, width), BF16),
            shape((16, rows, width), BF16),
        ]
        + probe_shapes(probes),
        [pltpu.VMEM((rows, width), BF16)] * 2
        + TensorSum.scratch(width) * 2
        + TensorGather.scratch * 2
        + DataGather.scratch * 3,
        (primal, moved, tokens, gain) + probes,
    )


def turn_kernel(*refs):
    (
        (moved, t_one, mask, a_zero, a_one, h_one),
        (c_out, cb_all, ga_zero, ga_one, hs_one),
        (c_low,),
        sum_a,
        gather_a,
        sems,
    ) = taken(refs, 6, 5, 1, 5, 2, 6)
    enter(True, True)
    total = TensorSum(moved, *sum_a)
    jobs = [
        DataGather(a_zero, slot_of(ga_zero), *sems[0:2]),
        DataGather(a_one, slot_of(ga_one), *sems[2:4]),
    ]
    swap = DataExchange(h_one, hs_one, *sems[4:6])
    total.start()
    total.send()
    for job in jobs:
        job.start()
    swap.start()
    cotangent = mask[:, 0:1] * (t_one[...] + total.total())
    c_out[...] = cotangent
    c_low[...] = cotangent.astype(BF16)
    for job in jobs:
        job.relay()
    rows = TensorGather(c_low, cb_all, *gather_a)
    rows.start()
    total.finish()
    rows.finish()
    swap.finish()
    for job in jobs:
        job.finish()


def turn(moved, t_one, mask, a_zero, a_one, h_one):
    rows, width = t_one.shape
    return comm_call(
        turn_kernel,
        "turn",
        3,
        [VMEM] * 3 + [HBM] * 3,
        [VMEM] * 2 + [HBM] * 3,
        [
            shape((rows, width), F32),
            shape((16, rows, width), BF16),
            shape((8,) + a_zero.shape, BF16),
            shape((8,) + a_one.shape, BF16),
            shape((8, h_one.shape[0], h_one.shape[1] // 8), BF16),
        ],
        [pltpu.VMEM((rows, width), BF16)]
        + TensorSum.scratch(width)
        + TensorGather.scratch
        + DataGather.scratch * 2
        + DataExchange.scratch,
        (moved, t_one, mask, a_zero, a_one, h_one),
    )


def lower_kernel(*refs):
    (
        (part, c_two, x_one, gain, g_one, cb_one, h_zero),
        (cb_all, gg_one, cbs_one, hs_zero),
        (c_low,),
        sum_a,
        gather_a,
        sems,
    ) = taken(refs, 7, 4, 1, 5, 2, 6)
    enter(True, True)
    total = TensorSum(part, *sum_a)
    job = DataGather(g_one, slot_of(gg_one), *sems[0:2])
    swaps = [
        DataExchange(cb_one, cbs_one, *sems[2:4]),
        DataExchange(h_zero, hs_zero, *sems[4:6]),
    ]
    total.start()
    total.send()
    job.start()
    for swap in swaps:
        swap.start()
    scaled = total.total() * gain[...]
    wide = x_one[...].astype(F32)
    inverse = lax.rsqrt(mean_of(wide * wide) + EPS)
    shift = mean_of(wide * scaled)
    cotangent = c_two[...] + inverse * (scaled - wide * inverse * inverse * shift)
    c_low[...] = cotangent.astype(BF16)
    job.relay()
    rows = TensorGather(c_low, cb_all, *gather_a)
    rows.start()
    total.finish()
    rows.finish()
    for swap in swaps:
        swap.finish()
    job.finish()


def lower(part, c_two, x_one, gain, g_one, cb_one, h_zero):
    rows, width = c_two.shape
    return comm_call(
        lower_kernel,
        "lower",
        4,
        [VMEM] * 4 + [HBM] * 3,
        [VMEM] + [HBM] * 3,
        [
            shape((16, rows, width), BF16),
            shape((8,) + g_one.shape, BF16),
            shape((8, cb_one.shape[0], width // 8), BF16),
            shape((8, h_zero.shape[0], width // 8), BF16),
        ],
        [pltpu.VMEM((rows, width), BF16)]
        + TensorSum.scratch(width)
        + TensorGather.scratch
        + DataGather.scratch
        + DataExchange.scratch * 2,
        (part, c_two, x_one, gain, g_one, cb_one, h_zero),
    )


def last_kernel(*refs):
    (g_zero, cb_zero), (gg_zero, cbs_zero), sems = taken(refs, 2, 2, 4)
    enter(False, True)
    job = DataGather(g_zero, slot_of(gg_zero), *sems[0:2])
    swap = DataExchange(cb_zero, cbs_zero, *sems[2:4])
    job.start()
    swap.start()
    job.relay()
    swap.finish()
    job.finish()


def last(g_zero, cb_zero):
    return comm_call(
        last_kernel,
        "last",
        5,
        [HBM] * 2,
        [HBM] * 2,
        [
            shape((8,) + g_zero.shape, BF16),
            shape((8, cb_zero.shape[0], cb_zero.shape[1] // 8), BF16),
        ],
        DataGather.scratch + DataExchange.scratch,
        (g_zero, cb_zero),
    )


def swapped(value, axis, apart):
    mask = 2**apart
    pairs = [(source, source ^ mask) for source in range(lax.axis_size(axis))]
    return lax.ppermute(value, axis, pairs)


def multiply(pattern, left_side, right_side):
    return jnp.einsum(pattern, left_side, right_side, preferred_element_type=F32)


def matmul(left_side, right_side):
    return jnp.dot(left_side, right_side, preferred_element_type=F32)


def contract_rows(left_side, right_side):
    return lax.dot_general(
        left_side, right_side, (((0,), (0,)), ((), ())), preferred_element_type=F32
    )


def contract_last(left_side, right_side):
    return lax.dot_general(
        left_side, right_side, (((1,), (1,)), ((), ())), preferred_element_type=F32
    )


def rope_tables(length, head_size):
    position = jnp.arange(length).astype(F32)
    column = jnp.arange(head_size // 2).astype(F32)
    frequency = jnp.exp(-math.log(THETA) * 2.0 * column / head_size)
    angles = position[:, None] * frequency[None, :]
    return (jnp.cos(angles), jnp.sin(angles))


def rotate(values, cosine_table, sine_table, direction):
    middle = values.shape[-1] // 2
    leading = values[..., :middle]
    trailing = values[..., middle:]
    cosine = cosine_table[:, None, :]
    sine_part = direction * sine_table[:, None, :]
    return jnp.concatenate(
        [leading * cosine - trailing * sine_part, trailing * cosine + leading * sine_part], axis=-1
    )


def attention_weights(queries, key_heads, allowed):
    scaling = 1.0 / math.sqrt(queries.shape[-1])
    scores = multiply("ihd,jd->hij", queries, key_heads) * scaling
    powers = jnp.where(allowed, jnp.exp(scores), 0.0)
    return powers / jnp.sum(powers, axis=-1, keepdims=True)


def attend(q, k, v, tq, tk, tv, allowed):
    scaling = 1.0 / math.sqrt(q.shape[-1])
    weights = attention_weights(q, k, allowed)
    weights_low = weights.astype(BF16)
    blended = multiply("hij,jd->ihd", weights_low, v).astype(BF16)
    tangent_scores = (multiply("ihd,jd->hij", tq, k) + multiply("ihd,jd->hij", q, tk)) * scaling
    tangent_weights = weights * (
        tangent_scores - jnp.sum(weights * tangent_scores, axis=-1, keepdims=True)
    )
    tangent_blended = multiply("hij,jd->ihd", tangent_weights.astype(BF16), v) + multiply(
        "hij,jd->ihd", weights_low, tv
    )
    return (blended, tangent_blended.astype(BF16))


def attend_back(q, k, v, grad_mixed, allowed):
    scaling = 1.0 / math.sqrt(q.shape[-1])
    weights = attention_weights(q, k, allowed)
    weights_low = weights.astype(BF16)
    grad_weights = multiply("ihd,jd->hij", grad_mixed, v)
    grad_values = multiply("hij,ihd->jd", weights_low, grad_mixed)
    grad_scores = (
        weights * (grad_weights - jnp.sum(weights * grad_weights, axis=-1, keepdims=True)) * scaling
    ).astype(BF16)
    grad_queries = multiply("hij,jd->ihd", grad_scores, k)
    grad_keys = multiply("hij,ihd->jd", grad_scores, q)
    return (grad_queries, grad_keys, grad_values)


def body(
    tokens,
    lengths,
    norm_gains,
    query_weight,
    key_weight,
    value_weight,
    out_weight,
    query_probe,
    key_probe,
    value_probe,
    out_probe,
):
    tensor_index = lax.axis_index("tensor")
    data_index = lax.axis_index("dp")
    share_rows, width = tokens.shape
    half = key_weight.shape[2]
    cosine_table, sine_table = rope_tables(LEN, HD)
    length = lax.dynamic_slice_in_dim(lengths, data_index, 1)[0]
    row_index = jnp.arange(LEN)[:, None]
    column_index = jnp.arange(LEN)[None, :]
    allowed = ((column_index <= row_index) & (column_index < length))[None]
    share_position = tensor_index * share_rows + jnp.arange(share_rows)
    share_mask = jnp.broadcast_to(
        (share_position < length).astype(F32)[:, None], (share_rows, 128)
    )
    lower_half = tensor_index % 2 == 0
    gains = [norm_gains[layer][None, :] for layer in range(2)]

    kv_probe = jnp.concatenate([key_probe, value_probe], axis=-1)
    kv_weight = [
        jnp.concatenate([key_weight[layer], value_weight[layer]], axis=-1) for layer in range(2)
    ]
    probes = (query_probe, kv_probe, out_probe)

    def heads_of(values):
        return values.reshape(LEN, -1, HD)

    def turned(values, direction=1.0):
        return rotate(heads_of(values), cosine_table, sine_table, direction)

    def joined(own, other):
        return jnp.where(
            lower_half,
            jnp.concatenate([own, other], axis=-1),
            jnp.concatenate([other, own], axis=-1),
        )

    def forward(layer, normed, normed_tangent, probe_q, probe_kv, probe_o):
        q = matmul(normed, query_weight[layer])
        tq = matmul(normed, probe_q)
        kv = matmul(normed, kv_weight[layer])
        tkv = matmul(normed, probe_kv)
        if normed_tangent is not None:
            tq = tq + matmul(normed_tangent, query_weight[layer])
            tkv = tkv + matmul(normed_tangent, kv_weight[layer])
        own = jnp.concatenate([kv, tkv], axis=-1)
        other = swapped(own.astype(BF16), "tensor", 0).astype(F32)
        k, v, tk, tv = [
            joined(own[:, at : at + half], other[:, at : at + half])
            for at in range(0, 4 * half, half)
        ]
        q, tq = turned(q).astype(BF16), turned(tq).astype(BF16)
        k, tk = turned(k)[:, 0].astype(BF16), turned(tk)[:, 0].astype(BF16)
        v, tv = v.astype(BF16), tv.astype(BF16)
        a, ta = attend(q, k, v, tq, tk, tv, allowed)
        a, ta = a.reshape(LEN, -1), ta.reshape(LEN, -1)
        moved = (matmul(ta, out_weight[layer]) + matmul(a, probe_o)).astype(BF16)
        primal = matmul(a, out_weight[layer]).astype(BF16) if layer == 0 else None
        return (q, k, v, a, primal, moved)

    def backward(layer, q, k, v, cb):
        grad_mixed = contract_last(cb, out_weight[layer]).astype(BF16)
        gq, gk, gv = attend_back(q, k, v, heads_of(grad_mixed), allowed)
        gq = rotate(gq, cosine_table, sine_table, -1.0).astype(BF16).reshape(LEN, -1)
        gk = rotate(gk[:, None], cosine_table, sine_table, -1.0)[:, 0].astype(BF16)
        gv = gv.astype(BF16)
        low = jnp.concatenate([gk[:, :half], gv[:, :half]], axis=-1)
        high = jnp.concatenate([gk[:, half:], gv[:, half:]], axis=-1)
        mine, theirs = jnp.where(lower_half, low, high), jnp.where(lower_half, high, low)
        came = swapped(theirs, "tensor", 0)
        gkv = (mine.astype(F32) + came.astype(F32)).astype(BF16)
        return (gq, gkv)

    def by_owner(part):
        return part.reshape(8, 2, share_rows, width)

    def whole(rows):
        return rows.reshape(LEN, width)

    def all_rows(blocks):
        return blocks.reshape(-1, blocks.shape[-1])

    h_zero, pq, pkv, po = first(tokens, gains[0], probes)
    h_zero = whole(h_zero)
    q0, k0, v0, a_zero, primal, moved = forward(
        0, h_zero, None, all_rows(pq), all_rows(pkv), po
    )
    x_one, t_one, h_one, th_one, pq, pkv, po = between(
        by_owner(primal), by_owner(moved), tokens, gains[1], probes
    )
    h_one, th_one = whole(h_one), whole(th_one)
    q1, k1, v1, a_one, unused, moved = forward(
        1, h_one, th_one, all_rows(pq), all_rows(pkv), po
    )
    c_two, cb_one, ga_zero, ga_one, hs_one = turn(
        by_owner(moved), t_one, share_mask, a_zero, a_one, h_one
    )
    cb_one = whole(cb_one)
    gq, gkv = backward(1, q1, k1, v1, cb_one)
    g_one = jnp.concatenate([gq, gkv], axis=-1)
    part = contract_last(gq, query_weight[1]) + contract_last(gkv, kv_weight[1])
    cb_zero, gg_one, cbs_one, hs_zero = lower(
        by_owner(part.astype(BF16)), c_two, x_one, gains[1], g_one, cb_one, h_zero
    )
    cb_zero = whole(cb_zero)
    gq, gkv = backward(0, q0, k0, v0, cb_zero)
    g_zero = jnp.concatenate([gq, gkv], axis=-1)
    gg_zero, cbs_zero = last(g_zero, cb_zero)

    sides = [(hs_zero, gg_zero, ga_zero, cbs_zero), (hs_one, gg_one, ga_one, cbs_one)]
    products = []
    for hs, gg, ga, cbs in sides:
        inner = contract_rows(all_rows(hs), all_rows(gg))
        outer = contract_rows(all_rows(ga), all_rows(cbs))
        q_width = inner.shape[1] - 2 * half
        products.append(
            (inner[:, :q_width], inner[:, q_width:-half], inner[:, -half:], outer)
        )
    return tuple(jnp.stack([products[0][n], products[1][n]]) for n in range(4))


def solution(mesh):
    placed = (
        P(("dp", "tensor"), None),
        P(),
        P(),
        P(None, None, "tensor"),
        P(None, None, "tensor"),
        P(None, None, "tensor"),
        P(None, "tensor", None),
        P(None, "dp", "tensor"),
        P(None, "dp", "tensor"),
        P(None, "dp", "tensor"),
        P(None, "tensor", "dp"),
    )
    return jax.shard_map(
        body,
        mesh=mesh,
        in_specs=placed,
        out_specs=(
            P(None, "dp", "tensor"),
            P(None, "dp", "tensor"),
            P(None, "dp", "tensor"),
            P(None, "tensor", "dp"),
        ),
        check_vma=False,
    )
```

time: 932 us -> 432 us (0.46)
  waiting for transfers between devices: 626 us -> 0.01 us
  Pallas kernels: 0 us -> 293 us
  other arithmetic: 70.1 us -> 16.5 us
  matrix products: 104 us -> 63.6 us
  local copies, waits for them, and re-layouts: 81 us -> 49.5 us
  starting transfers between devices: 24.2 us -> 2.57 us
  between operations: 15.4 us -> 2.46 us
    all_gather x5 -> x0, waiting for transfers between devices: 364 us -> none  [the longest x1 201 us: turned_gather(): result, at, done = (lax.all_gather(both, axis, axis=0, tiled=True), 0, [])]
    pallas_call x0 -> x5, Pallas kernels: none -> 293 us  [comm_call(): pl.pallas_call(kernel, name=name, in_specs=in_specs, out_specs=out_specs,...]
    reduce_scatter x3 -> x0, waiting for transfers between devices: 245 us -> none  [the longest x2 165 us: sum_packed(): lax.psum_scatter(lines, axis, tiled=True).reshape(-1)]
    concatenate x9 -> x5, other arithmetic: 42.4 us -> 0.89 us  [the longest x2 0.7 us: forward(): own = jnp.concatenate([kv, tkv], axis=-1)]
    dot_general x40 -> x35, matrix products: 63.1 us -> 44.9 us  [the longest x15 25.7 us: matmul(): return jnp.dot(left_side, right_side, preferred_element_type=F32)]
    all_to_all x2 -> x0, waiting for transfers between devices: 17.5 us -> none  [sum_at_owner(): lax.all_to_all(pieces, axis, split_axis=0, concat_axis=0, tiled=True)]
    dot_general x12 -> x4, matrix products: 23.1 us -> 6.39 us  [contract_rows(): lax.dot_general(left_side, right_side, (((0,), (0,)), ((), ())), preferre...]
    another operation x6 -> x4, local copies, waits for them, and re-layouts: 16.7 us -> 1.6 us  [body(): jnp.stack([products[0][n], products[1][n]])]
  transfers between devices with their start and end apart: 22 -> 4, of which waited for: 10 -> 0; matrix products, arithmetic and copies ran while one was open for 20% -> 9% of each run, Pallas kernels for 0% -> 0%
where the time goes in v1:
time: 432 us; the launch traced here: 428 us
  Pallas kernels  293 us (68%)
  matrix products  63.6 us (15%)
  local copies, waits for them, and re-layouts  49.5 us (11%)
  other arithmetic  16.5 us (4%)
    pallas_call x5, Pallas kernels, comm_call(): pl.pallas_call(kernel, name=name, in_specs=in_specs, out_specs=out_specs,...  293 us
    dot_general x15, matrix products, matmul(): return jnp.dot(left_side, right_side, preferred_element_type=F32)  25.7 us
    dot_general x20, matrix products, multiply(): jnp.einsum(pattern, left_side, right_side, preferred_element_type=F32)  19.2 us
    unnamed x185, local copies, waits for them, and re-layouts  18.9 us
    dot_general x4, local copies, waits for them, and re-layouts, matmul(): return jnp.dot(left_side, right_side, preferred_element_type=F32)  17.1 us
    dot_general x4, matrix products, contract_last(): lax.dot_general(left_side, right_side, (((1,), (1,)), ((), ())), preferre...  8.94 us
  transfers between devices with their start and end apart: 4, of which 0 were waited for; matrix products, arithmetic and copies ran while one was open for 9% of the time, Pallas kernels for 0%

profile of v1, /device:TPU:1, one launch (start us, length us, event | category | flops | bytes accessed | tf_op | source)
XLA Modules:
  0.0 427.6 jit_solution(9968880600466387888)
XLA Ops:
  0.6 1.2 copy.15
  1.8 1.1 copy.16
  4.0 2.4 slice_bitcast_fusion.4
  6.4 53.3 %first.1 = (bf16[16,16,4096]{2,1,0:T(8,128)(2,1)S(1)}, bf16[8,512,256]{2,1,0:T(8,128)(2,1)S(1)}, bf16[8,512,128]{2,1,0:T(8,128)(2,1)S(1)}, bf16[256,4096]{1,0:T(8,128)(2,1)S(1)}) custom-call(bf16[16,4096]{1,0:T(8,128)(2,1)S(1)} %copy-done.12, f32[1,4096]{1,0:T(1,128)S(1)} %get-tuple-element.107.gain, bf16[2,512,256]{2,1,0:T(8,128)(2,1)S(1)} %copy-done.8, ...), custom_call_target="tpu_custom_call" | custom-call | tf_op jit(solution)/shard_map/first/pallas_call | solution.py:318
  62.5 1.7 collective-permute-start
  66.6 4.1 copy.26
  70.8 4.7 %slice_bitcast_fusion.1 = (bf16[256,4096]{0,1:T(8,128)(2,1)}, bf16[256,4096]{0,1:T(8,128)(2,1)}) fusion(bf16[2,4096,256]{2,1,0:T(8,128)(2,1)} %param.14), kind=kLoop, calls=%fused_computation.26 | loop fusion | bytes 8388608 | tf_op jit(solution)/shard_map/dot_general | solution.py:624
  75.4 4.1 copy.21
  79.6 3.2 fusion.217
  82.8 1.5 fusion.216
  84.2 1.2 dynamic_slice.3
  86.0 1.6 broadcast_multiply_fusion
  87.6 1.2 subtract_convert_fusion.3
  91.1 4.2 copy.39
  95.2 1.1 compare_convert_fusion
  99.1 1.2 multiply_reduce_fusion.3
  102.7 2.5 fusion.15
  107.1 2.1 fusion.3
  109.1 85.1 %between.1 = (bf16[16,4096]{1,0:T(8,128)(2,1)S(1)}, f32[16,4096]{1,0:T(8,128)S(1)}, bf16[16,16,4096]{2,1,0:T(8,128)(2,1)S(1)}, bf16[16,16,4096]{2,1,0:T(8,128)(2...) custom-call(bf16[8,2,16,4096]{3,2,1,0:T(8,128)(2,1)S(1)} %bitcast.291, ...), custom_call_target="tpu_custom_call" | custom-call | tf_op jit(solution)/shard_map/between/pallas_call | solution.py:318
  196.6 1.3 copy-done.22
  200.8 2.7 fusion.220
  210.1 1.2 fusion.128
  212.3 1.0 fusion.27
  213.4 1.4 convolution_convert_fusion.1
  215.1 1.1 fusion.40
  216.2 2.2 multiply_reduce_fusion.2
  218.4 2.3 fusion.70
  220.7 1.5 fusion.47
  222.2 4.3 %fusion.7 = f32[256,4096]{1,0:T(8,128)} fusion(bf16[256,256]{0,1:T(8,128)(2,1)S(1)} %bitcast.316, bf16[2,256,4096]{2,1,0:T(8,128)(2,1)} %param.17), kind=kOutput, calls=%fused_computation.11 | convolution fusion | flops 536870912 | bytes 6422528 | tf_op jit(solution)/shard_map/dot_general | solution.py:624
  226.7 3.6 fusion.4
  230.4 58.2 %turn.1 = (f32[16,4096]{1,0:T(8,128)S(1)}, bf16[16,16,4096]{2,1,0:T(8,128)(2,1)S(1)}, bf16[8,256,256]{2,1,0:T(8,128)(2,1)S(1)}, bf16[8,256,256]{2,1,0:T(8,128)(2,1)S(1)}, bf16[8,256,512]{2,1,0:T(8,128)(2,1)S(1)}) custom-call(bf16[8,2,16,4096]{3,2,1,0:T(8,128)(2,1)S(1)} %bitcast.290, f32[16,4096]{1,0:T(8,128)S(1)} %copy-done.14, ...), custom_call_target="tpu_custom_call" | custom-call | tf_op jit(solution)/shard_map/turn/pallas_call | solution.py:318
  292.1 1.3 fusion.54
  293.5 1.5 convolution_bitcast_fusion.11
  295.0 1.5 convolution_bitcast_fusion.7
  298.0 4.4 %fusion.11 = f32[256,4096]{1,0:T(8,128)} fusion(bf16[256,256]{0,1:T(8,128)(2,1)S(1)} %bitcast.309, bf16[2,4096,256]{2,1,0:T(8,128)(2,1)} %param.14), kind=kOutput, calls=%fused_computation.15 | convolution fusion | flops 536870912 | bytes 6422528 | tf_op jit(solution)/shard_map/dot_general | solution.py:634
  302.7 3.0 fusion.2
  305.8 68.3 %lower.1 = (bf16[16,16,4096]{2,1,0:T(8,128)(2,1)S(1)}, bf16[8,256,384]{2,1,0:T(8,128)(2,1)S(1)}, bf16[8,256,512]{2,1,0:T(8,128)(2,1)S(1)}, bf16[8,256,512]{2,1,0:T(8,128)(2,1)S(1)}) custom-call(bf16[8,2,16,4096]{3,2,1,0:T(8,128)(2,1)S(1)} %bitcast.284, f32[16,4096]{1,0:T(8,128)S(1)} %get-tuple-element.37.refs_1_, bf16[16,4096]{1,0:T(8,128)(2,1)S(1)} %copy-done.16, ...), custom_call_target="tpu_custom_call" | custom-call | tf_op jit(solution)/shard_map/lower/pallas_call | solution.py:318
  374.0 1.2 copy-done.26
  377.4 2.2 convolution_bitcast_fusion.6
  379.6 1.5 convolution_bitcast_fusion.9
  381.1 1.3 fusion.55
  382.5 3.1 convolution_bitcast_fusion
  387.7 1.6 convolution_bitcast_fusion.2
  389.6 28.1 %last.1 = (bf16[8,256,384]{2,1,0:T(8,128)(2,1)S(1)}, bf16[8,256,512]{2,1,0:T(8,128)(2,1)S(1)}) custom-call(bf16[256,384]{1,0:T(8,128)(2,1)S(1)} %pad_maximum_fusion.10.refs_0_, bf16[256,4096]{1,0:T(8,128)(2,1)S(1)} %bitcast.293), custom_call_target="tpu_custom_call" | custom-call | tf_op jit(solution)/shard_map/last/pallas_call | solution.py:318
  417.7 1.0 convolution_bitcast_fusion.1
  419.8 1.0 pad_maximum_fusion.1
  420.9 2.8 copy.71
  424.7 1.0 pad_maximum_fusion.2
  (268 shorter events, 42.1 us)
Async XLA Ops:
  0.6 3.3 copy-start.47
  59.7 23.0 %copy-start = (bf16[16,16,4096]{2,1,0:T(8,128)(2,1)}, bf16[16,16,4096]{2,1,0:T(8,128)(2,1)S(1)}, u32[]{:S(2)}) copy-start(bf16[16,16,4096]{2,1,0:T(8,128)(2,1)S(1)} %get-tuple-element.26) | copy-start | bytes 6291460
  60.4 5.5 %copy-start.48 = (f32[256,128]{1,0:T(8,128)}, f32[256,128]{1,0:T(8,128)S(1)}, u32[]{:S(2)}) copy-start(f32[256,128]{1,0:T(8,128)S(1)} %get-tuple-element.116) | copy-start | bytes 393220
  61.8 4.8 %copy-start.58 = (f32[256,128]{1,0:T(8,128)}, f32[256,128]{1,0:T(8,128)S(1)}, u32[]{:S(2)}) copy-start(f32[256,128]{1,0:T(8,128)S(1)} %get-tuple-element.118) | copy-start | bytes 393220
  62.5 33.8 %collective-permute-start = (bf16[256,256]{1,0:T(8,128)(2,1)}, bf16[256,256]{1,0:T(8,128)(2,1)}, u32[]{:S(2)}, u32[]{:S(2)}) collective-permute-start(bf16[256,256]{1,0:T(8,128)(2,1)} %pad_maximum_fusion.11), channel_id=1, source_target_pairs={{0,1},{1,0},{2,3},{3,2},{4,5},{5,4},{6,7},{7,6},{8,9},{9,8},{10,11... | collective-permute-start | bytes 393224 | tf_op jit(solution)/shard_map/ppermute | solution.py:616
  79.6 3.2 copy-start.41
  87.6 7.6 %copy-start.43 = (f32[256,64]{0,1:T(8,128)}, f32[256,64]{0,1:T(8,128)S(1)}, u32[]{:S(2)}) copy-start(f32[256,64]{0,1:T(8,128)S(1)} %get-tuple-element.110) | copy-start | bytes 196612
  87.6 7.6 %copy-start.49 = (f32[256,64]{0,1:T(8,128)}, f32[256,64]{0,1:T(8,128)S(1)}, u32[]{:S(2)}) copy-start(f32[256,64]{0,1:T(8,128)S(1)} %get-tuple-element.109) | copy-start | bytes 196612
  88.9 13.3 %copy-start.59 = (bf16[256,2,64]{0,2,1:T(8,128)(2,1)}, bf16[256,2,64]{0,2,1:T(8,128)(2,1)S(1)}, u32[]{:S(2)}) copy-start(bf16[256,2,64]{0,2,1:T(8,128)(2,1)S(1)} %get-tuple-element.96) | copy-start | bytes 196612
  88.9 13.3 %copy-start.61 = (bf16[256,2,64]{0,2,1:T(8,128)(2,1)}, bf16[256,2,64]{0,2,1:T(8,128)(2,1)S(1)}, u32[]{:S(2)}) copy-start(bf16[256,2,64]{0,2,1:T(8,128)(2,1)S(1)} %get-tuple-element.97) | copy-start | bytes 196612
  89.0 13.2 %copy-start.80 = (pred[256,256]{0,1:T(8,128)(4,1)}, pred[256,256]{0,1:T(8,128)(4,1)S(1)}, u32[]{:S(2)}) copy-start(pred[256,256]{0,1:T(8,128)(4,1)S(1)} %fusion.81) | copy-start | bytes 196612
  91.0 6.3 %copy-start.54 = (f32[256,1,64]{2,0,1:T(8,128)S(1)}, f32[256,1,64]{2,0,1:T(8,128)}, u32[]{:S(2)}) copy-start(f32[256,1,64]{2,0,1:T(8,128)} %slice_bitcast_fusion.19) | copy-start | bytes 196612
  91.0 6.4 %copy-start.53 = (f32[256,1,64]{2,0,1:T(8,128)S(1)}, f32[256,1,64]{2,0,1:T(8,128)}, u32[]{:S(2)}) copy-start(f32[256,1,64]{2,0,1:T(8,128)} %slice_bitcast_fusion.17) | copy-start | bytes 196612
  91.0 6.6 %copy-start.84 = (f32[256]{0:T(256)S(1)}, f32[256]{0:T(256)}, u32[]{:S(2)}) copy-start(f32[256]{0:T(256)} %iota_convert_fusion) | copy-start | bytes 3076
  91.1 6.6 %copy-start.87 = (f32[64]{0:T(128)S(1)}, f32[64]{0:T(128)}, u32[]{:S(2)}) copy-start(f32[64]{0:T(128)} %multiply_exponential_fusion) | copy-start | bytes 772
  98.3 3.8 copy-start.72
  101.8 4.4 %copy-start.45 = (bf16[128,2,256]{2,0,1:T(8,128)(2,1)}, bf16[128,2,256]{2,0,1:T(8,128)(2,1)S(1)}, u32[]{:S(2)}) copy-start(bf16[128,2,256]{2,0,1:T(8,128)(2,1)S(1)} %convolution_convert_fusion.2) | copy-start | bytes 393220
  109.1 88.8 %copy-start.35 = (bf16[4096,64]{0,1:T(8,128)(2,1)S(1)}, bf16[4096,64]{0,1:T(8,128)(2,1)}, u32[]{:S(2)}) copy-start(bf16[4096,64]{0,1:T(8,128)(2,1)} %get-tuple-element.56) | copy-start | bytes 1572868
  109.1 88.8 %copy-start.37 = (bf16[4096,64]{0,1:T(8,128)(2,1)S(1)}, bf16[4096,64]{0,1:T(8,128)(2,1)}, u32[]{:S(2)}) copy-start(bf16[4096,64]{0,1:T(8,128)(2,1)} %get-tuple-element.128) | copy-start | bytes 1572868
  200.8 3.4 copy-start.34
  207.2 2.5 collective-permute-start.1
  208.9 3.3 copy-start.70
  209.0 3.4 copy-start.81
  210.1 4.7 %copy-start.68 = (bf16[256,2,64]{0,2,1:T(8,128)(2,1)S(1)}, bf16[256,2,64]{0,2,1:T(8,128)(2,1)}, u32[]{:S(2)}) copy-start(bf16[256,2,64]{0,2,1:T(8,128)(2,1)} %get-tuple-element.92) | copy-start | bytes 196612
  210.1 4.7 %copy-start.69 = (bf16[256,2,64]{0,2,1:T(8,128)(2,1)S(1)}, bf16[256,2,64]{0,2,1:T(8,128)(2,1)}, u32[]{:S(2)}) copy-start(bf16[256,2,64]{0,2,1:T(8,128)(2,1)} %get-tuple-element.93) | copy-start | bytes 196612
  211.4 9.3 %copy-start.76 = (bf16[256,128,1]{1,0,2:T(8,128)(2,1)}, bf16[256,128,1]{1,0,2:T(8,128)(2,1)S(1)}, u32[]{:S(2)}) copy-start(bf16[256,128,1]{1,0,2:T(8,128)(2,1)S(1)} %maximum_bitcast_fusion.3) | copy-start | bytes 196612
  211.4 3.6 copy-start.78
  211.5 3.6 copy-start.79
  216.1 4.6 %copy-start.82 = (bf16[256,64]{1,0:T(8,128)(2,1)S(1)}, bf16[256,64]{1,0:T(8,128)(2,1)}, u32[]{:S(2)}) copy-start(bf16[256,64]{1,0:T(8,128)(2,1)} %slice.291) | copy-start | bytes 98308
  216.1 4.6 %copy-start.83 = (bf16[256,64]{1,0:T(8,128)(2,1)S(1)}, bf16[256,64]{1,0:T(8,128)(2,1)}, u32[]{:S(2)}) copy-start(bf16[256,64]{1,0:T(8,128)(2,1)} %get-tuple-element.90) | copy-start | bytes 98308
  226.6 3.6 copy-start.90
  226.7 3.7 copy-start.14
  230.4 59.2 %copy-start.32 = (bf16[2,256,4096]{2,1,0:T(8,128)(2,1)S(1)}, bf16[2,256,4096]{2,1,0:T(8,128)(2,1)}, u32[]{:S(2)}) copy-start(bf16[2,256,4096]{2,1,0:T(8,128)(2,1)} %param.17) | copy-start | bytes 12582916
  292.1 5.8 %copy-start.51 = (f32[256,64]{0,1:T(8,128)S(1)}, f32[256,64]{0,1:T(8,128)}, u32[]{:S(2)}) copy-start(f32[256,64]{0,1:T(8,128)} %get-tuple-element.108) | copy-start | bytes 196612
  297.4 5.1 %collective-permute-start.2 = (bf16[256,128]{1,0:T(8,128)(2,1)S(1)}, bf16[256,128]{1,0:T(8,128)(2,1)S(1)}, u32[]{:S(2)}, u32[]{:S(2)}) collective-permute-start(bf16[256,128]{1,0:T(8,128)(2,1)S(1)} %broadcast_select_fusion.1), channel_id=1, source_target_pairs={{0,1},{1,0},{2,3},{3,2},{4,5},{5,4},{6,7},{7,6},{8,9},{9,8},{10,11... | collective-permute-start | bytes 196616 | tf_op jit(solution)/shard_map/ppermute | solution.py:616
  298.0 4.7 %copy-start.39 = (bf16[4096,64]{0,1:T(8,128)(2,1)S(1)}, bf16[4096,64]{0,1:T(8,128)(2,1)}, u32[]{:S(2)}) copy-start(bf16[4096,64]{0,1:T(8,128)(2,1)} %get-tuple-element.128) | copy-start | bytes 1572868
  302.7 3.1 copy-start.2
  305.8 69.5 %copy-start.33 = (bf16[2,256,4096]{2,1,0:T(8,128)(2,1)S(1)}, bf16[2,256,4096]{2,1,0:T(8,128)(2,1)}, u32[]{:S(2)}) copy-start(bf16[2,256,4096]{2,1,0:T(8,128)(2,1)} %param.17) | copy-start | bytes 12582916
  375.2 4.4 %copy-start.60 = (bf16[256,2,64]{0,2,1:T(8,128)(2,1)S(1)}, bf16[256,2,64]{0,2,1:T(8,128)(2,1)}, u32[]{:S(2)}) copy-start(bf16[256,2,64]{0,2,1:T(8,128)(2,1)} %copy-done.59) | copy-start | bytes 196612
  375.2 4.4 %copy-start.62 = (bf16[256,2,64]{0,2,1:T(8,128)(2,1)S(1)}, bf16[256,2,64]{0,2,1:T(8,128)(2,1)}, u32[]{:S(2)}) copy-start(bf16[256,2,64]{0,2,1:T(8,128)(2,1)} %copy-done.61) | copy-start | bytes 196612
  382.4 4.0 copy-start.52
  382.4 4.0 copy-start.71
  382.4 4.1 copy-start.86
  382.4 4.1 copy-start.89
  387.5 1.9 collective-permute-start.3
  389.4 28.3 %copy-start.19 = (bf16[8,256,512]{2,1,0:T(8,128)(2,1)S(1)}, bf16[8,256,512]{2,1,0:T(8,128)(2,1)}, u32[]{:S(2)}) copy-start(bf16[8,256,512]{2,1,0:T(8,128)(2,1)} %copy-done.18) | copy-start | bytes 6291460
  419.8 3.9 copy-start.25
  419.8 3.9 copy-start.28
  (47 other events, 82.4 us)

commit v2 on v1

v2 whole, which is shorter than its diff:
```python
import functools
import math

import jax
import jax.numpy as jnp
import numpy as np
from jax import lax
from jax.experimental import pallas as pl
from jax.experimental.pallas import tpu as pltpu
from jax.sharding import PartitionSpec as P

HD = 128
LEN = 256
EPS = 1e-05
THETA = 500000.0

MESH = pl.DeviceIdType.MESH
F32 = jnp.float32
BF16 = jnp.bfloat16
VMEM = pl.BlockSpec(memory_space=pltpu.VMEM)
HBM = pl.BlockSpec(memory_space=pl.ANY)
DMA = pltpu.SemaphoreType.DMA

HOPS = ((1, 1), (3, 1), (2, 1), (2, 0), (1, 0), (3, 0), (0, 1))


def back(hop):
    return ((4 - hop[0]) % 4, hop[1])


def data_at(d, hop):
    ring, pair = lax.div(d, 2), lax.rem(d, 2)
    return lax.rem(ring + hop[0], 4) * 2 + lax.rem(pair + hop[1], 2)


def chip_at(t, hop):
    return data_at(lax.div(t, 2), hop)


def tensor_at(t, hop):
    return chip_at(t, hop) * 2 + lax.rem(t, 2)


def other_core(t):
    return t + 1 - 2 * lax.rem(t, 2)


def places():
    return lax.axis_index("dp"), lax.axis_index("tensor")


def remote(src, dst, sends, recvs, j, device):
    return pltpu.make_async_remote_copy(
        src_ref=src,
        dst_ref=dst,
        send_sem=sends.at[j],
        recv_sem=recvs.at[j],
        device_id=device,
        device_id_type=MESH,
    )


def enter(over_tensor, over_data):
    d, t = places()
    barrier = pltpu.get_barrier_semaphore()
    peers = [(d, other_core(t))]
    if over_tensor:
        peers += [(d, tensor_at(t, hop)) for hop in HOPS]
    if over_data:
        peers += [(data_at(d, hop), t) for hop in HOPS]
    for peer in peers:
        pl.semaphore_signal(barrier, inc=1, device_id=peer, device_id_type=MESH)
    pl.semaphore_wait(barrier, len(peers))


class RingGather:
    ROUTES = (
        ((0, 1), (0, 0), (0, 1)),
        ((1, 0), (0, 0), (3, 0)),
        ((3, 0), (0, 0), (1, 0)),
        ((2, 0), (0, 0), (2, 0)),
        ((1, 0), (0, 1), (3, 1)),
        ((3, 0), (0, 1), (1, 1)),
    )
    LAST = ((0, 1), (2, 0), (2, 1))
    WAITS = 7

    def __init__(self, src, slot, sends, recvs):
        self.src, self.slot, self.sends, self.recvs = src, slot, sends, recvs
        self.routes = self.ROUTES + (self.LAST,)

    def place(self, hop):
        d, t = places()
        return data_at(d, hop)

    def device(self, hop):
        d, t = places()
        return (data_at(d, hop), t)

    def out(self, j):
        hop, block, unused = self.routes[j]
        slot = self.slot(self.place(block))
        src = self.src if j < 4 else slot
        return remote(src, slot, self.sends, self.recvs, j, self.device(hop))

    def into(self, j):
        slot = self.slot(self.place(self.routes[j][2]))
        return remote(slot, slot, self.sends, self.recvs, j, self.device((0, 1)))

    def own(self):
        return pltpu.make_async_copy(self.src, self.slot(self.place((0, 0))), self.sends.at[7])

    def hand(self, j):
        pass

    def start(self):
        for j in range(4):
            self.out(j).start()
        self.own().start()

    def relay(self):
        self.into(0).wait_recv()
        self.out(4).start()
        self.out(5).start()
        if self.LAST[0] == (0, 1):
            self.into(3).wait_recv()
        self.out(6).start()
        self.hand(0)

    def finish(self):
        for j in (1, 2, 3, 4, 5, 6):
            if j != 3 or self.LAST[0] != (0, 1):
                self.into(j).wait_recv()
                self.hand(j)
        for j in range(7):
            self.out(j).wait_send()
        self.own().wait()


class DataGather(RingGather):
    scratch = [DMA((8,)), DMA((7,))]


class TensorGather(RingGather):
    scratch = [DMA((16,)), DMA((15,))]
    LAST = ((2, 0), (0, 1), (2, 1))

    def place(self, hop):
        d, t = places()
        return tensor_at(t, hop)

    def device(self, hop):
        d, t = places()
        return (d, tensor_at(t, hop))

    def near(self):
        d, t = places()
        return pltpu.make_async_remote_copy(
            src_ref=self.src,
            dst_ref=self.slot(t),
            send_sem=self.sends.at[15],
            recv_sem=self.recvs.at[14],
            device_id=(d, other_core(t)),
            device_id_type=MESH,
        )

    def handover(self, j, block):
        d, t = places()
        slot = self.slot(block)
        return pltpu.make_async_remote_copy(
            src_ref=slot,
            dst_ref=slot,
            send_sem=self.sends.at[8 + j],
            recv_sem=self.recvs.at[7 + j],
            device_id=(d, other_core(t)),
            device_id_type=MESH,
        )

    def hand(self, j):
        self.handover(j, self.place(self.routes[j][2])).start()

    def start(self):
        super().start()
        self.near().start()

    def finish(self):
        super().finish()
        d, t = places()
        far = other_core(t)
        slot = self.slot(far)
        pltpu.make_async_remote_copy(
            src_ref=slot,
            dst_ref=slot,
            send_sem=self.sends.at[15],
            recv_sem=self.recvs.at[14],
            device_id=(d, far),
            device_id_type=MESH,
        ).wait_recv()
        self.near().wait_send()
        for j in range(7):
            self.handover(j, tensor_at(far, self.routes[j][2])).wait_recv()
            self.handover(j, self.place(self.routes[j][2])).wait_send()


class TensorSum:
    STEPS = ((2, 1), (1, 1), (3, 1), (2, 0), (1, 0), (3, 0))
    BLOCKS = STEPS + ((0, 1), (0, 0))

    @staticmethod
    def scratch(columns):
        return [
            pltpu.VMEM((8, 16, columns), BF16),
            pltpu.VMEM((7, 16, columns), BF16),
            pltpu.VMEM((7, 16, columns), BF16),
            DMA((15,)),
            DMA((15,)),
        ]

    def __init__(self, part, near, sent, far, sends, recvs):
        self.part, self.near_, self.sent, self.far = part, near, sent, far
        self.sends, self.recvs = sends, recvs

    def swap(self, j):
        d, t = places()
        k = chip_at(t, self.BLOCKS[j])
        c = lax.rem(t, 2)
        return remote(
            self.part.at[k, 1 - c], self.near_.at[k], self.sends, self.recvs, j, (d, other_core(t))
        )

    def cross(self, j):
        d, t = places()
        hop = (self.STEPS[j][0], 0) if j < 6 else (0, 1)
        return remote(
            self.sent.at[j], self.far.at[j], self.sends, self.recvs, 8 + j, (d, tensor_at(t, hop))
        )

    def pair_sum(self, j):
        d, t = places()
        k = chip_at(t, self.BLOCKS[j])
        c = lax.rem(t, 2)
        return self.part[k, c].astype(F32) + self.near_[k].astype(F32)

    def start(self):
        for j in range(8):
            self.swap(j).start()

    def send(self):
        for j in range(6):
            self.swap(j).wait_recv()
            self.sent[j] = self.pair_sum(j).astype(BF16)
            self.cross(j).start()

    def middle(self):
        self.swap(6).wait_recv()
        total = self.pair_sum(6)
        for j in (1, 2, 0):
            self.cross(j).wait_recv()
            total = total + self.far[j].astype(F32)
        self.sent[6] = total.astype(BF16)
        self.cross(6).start()

    def total(self):
        self.swap(7).wait_recv()
        total = self.pair_sum(7)
        for j in (4, 5, 3, 6):
            self.cross(j).wait_recv()
            total = total + self.far[j].astype(F32)
        return total

    def finish(self):
        for j in range(8):
            self.swap(j).wait_send()
        for j in range(7):
            self.cross(j).wait_send()


class DataSpread:
    scratch = [DMA((8,)), DMA((7,))]

    def __init__(self, src, out, sends, recvs):
        self.src, self.out_, self.sends, self.recvs = src, out, sends, recvs
        self.share = src.shape[1] // 8

    def columns(self, d):
        return pl.ds(pl.multiple_of(d * self.share, self.share), self.share)

    def cross(self, j):
        d, t = places()
        peer = data_at(d, HOPS[j])
        return remote(
            self.src.at[:, self.columns(peer)],
            self.out_.at[d],
            self.sends,
            self.recvs,
            j,
            (peer, t),
        )

    def arrived(self, j):
        d, t = places()
        slot = self.out_.at[data_at(d, back(HOPS[j]))]
        return remote(slot, slot, self.sends, self.recvs, j, (d, other_core(t)))

    def own(self):
        d, t = places()
        return pltpu.make_async_copy(
            self.src.at[:, self.columns(d)], self.out_.at[d], self.sends.at[7]
        )

    def start(self):
        for j in range(7):
            self.cross(j).start()
        self.own().start()

    def finish(self):
        for j in range(7):
            self.arrived(j).wait_recv()
            self.cross(j).wait_send()
        self.own().wait()


class DataExchange:
    scratch = [DMA((15,)), DMA((14,))]

    def __init__(self, src, out, sends, recvs):
        self.src, self.out_, self.sends, self.recvs = src, out, sends, recvs
        self.half = src.shape[0] // 2
        self.share = src.shape[1] // 8

    def rows(self, t):
        return pl.ds(pl.multiple_of(lax.rem(t, 2) * self.half, self.half), self.half)

    def columns(self, d):
        return pl.ds(pl.multiple_of(d * self.share, self.share), self.share)

    def cross(self, j):
        d, t = places()
        peer = data_at(d, HOPS[j])
        return remote(
            self.src.at[self.rows(t), self.columns(peer)],
            self.out_.at[d, self.rows(t)],
            self.sends,
            self.recvs,
            j,
            (peer, t),
        )

    def hand(self, j, t_of):
        d, t = places()
        slot = self.out_.at[data_at(d, back(HOPS[j])), self.rows(t_of)]
        return slot

    def arrived(self, j):
        d, t = places()
        slot = self.hand(j, t)
        return remote(slot, slot, self.sends, self.recvs, j, (d, other_core(t)))

    def handed(self, j):
        d, t = places()
        slot = self.hand(j, t)
        return remote(slot, slot, self.sends, self.recvs, 7 + j, (d, other_core(t)))

    def received(self, j):
        d, t = places()
        slot = self.hand(j, other_core(t))
        return remote(slot, slot, self.sends, self.recvs, 7 + j, (d, other_core(t)))

    def own(self):
        d, t = places()
        return pltpu.make_async_copy(
            self.src.at[:, self.columns(d)], self.out_.at[d], self.sends.at[14]
        )

    def start(self):
        for j in range(7):
            self.cross(j).start()
        self.own().start()

    def finish(self):
        for j in (6, 4, 5, 3, 0, 1, 2):
            self.arrived(j).wait_recv()
            self.handed(j).start()
        for j in range(7):
            self.received(j).wait_recv()
            self.cross(j).wait_send()
            self.handed(j).wait_send()
        self.own().wait()


def taken(refs, *counts):
    out, at = [], 0
    for count in counts:
        out.append(refs[at : at + count])
        at += count
    return out


def comm_call(kernel, name, number, in_specs, out_specs, out_shape, scratch, args):
    return pl.pallas_call(
        kernel,
        name=name,
        in_specs=in_specs,
        out_specs=out_specs,
        out_shape=out_shape,
        scratch_shapes=scratch,
        compiler_params=pltpu.CompilerParams(
            collective_id=number, has_side_effects=True, vmem_limit_bytes=40 * 2**20
        ),
    )(*args)


def shape(dims, dtype):
    return jax.ShapeDtypeStruct(dims, dtype)


def slot_of(ref):
    return lambda block: ref.at[block]


def columns_of(ref):
    width = ref.shape[1] // 8
    return lambda block: ref.at[:, pl.ds(pl.multiple_of(block * width, width), width)]


def mean_of(values):
    return jnp.sum(values, axis=-1, keepdims=True) * (1.0 / values.shape[-1])


def strip(which, core):
    return pl.ds(pl.multiple_of(which * 128 + core * 64, 64), 64)


class CoreShare:
    scratch = [DMA((2,)), DMA((2,))]

    def __init__(self, sources, slot, sends, recvs):
        self.sources, self.slot, self.sends, self.recvs = sources, slot, sends, recvs

    def copy(self, j, core):
        d, t = places()
        slot = self.slot(j, core)
        src = slot if self.sources is None else self.sources[j]
        return remote(src, slot, self.sends, self.recvs, j, (d, other_core(t)))

    def start(self):
        d, t = places()
        for j in range(2):
            self.copy(j, lax.rem(t, 2)).start()

    def finish(self):
        d, t = places()
        for j in range(2):
            self.copy(j, 1 - lax.rem(t, 2)).wait_recv()
            self.copy(j, lax.rem(t, 2)).wait_send()


class Probes:
    COUNT = 4
    scratch = DataGather.scratch * 4 + CoreShare.scratch

    def __init__(self, layer, probes, gathered, sems):
        q, k, v, o = probes
        gq, gkv, go = gathered
        d, t = places()
        core = lax.rem(t, 2)
        width = k.shape[2]

        def part(which):
            return lambda block: gkv.at[
                strip(which, core), pl.ds(pl.multiple_of(block * width, width), width)
            ]

        self.jobs = [
            DataGather(k.at[layer], part(0), *sems[0:2]),
            DataGather(v.at[layer], part(1), *sems[2:4]),
            DataGather(q.at[layer], slot_of(gq), *sems[4:6]),
            DataGather(o.at[layer], columns_of(go), *sems[6:8]),
        ]
        self.share = CoreShare(None, lambda j, c: gkv.at[strip(j, c)], *sems[8:10])

    @staticmethod
    def shapes(probes):
        q, k, v, o = probes
        return [
            shape((8,) + q.shape[1:], BF16),
            shape((4 * k.shape[1], 8 * k.shape[2]), BF16),
            shape((o.shape[1], 8 * o.shape[2]), BF16),
        ]

    def start(self):
        for job in self.jobs:
            job.start()

    def relay(self):
        for job in self.jobs:
            job.relay()

    def finish(self):
        for job in self.jobs[:2]:
            job.finish()
        self.share.start()
        for job in self.jobs[2:]:
            job.finish()
        self.share.finish()


def first_kernel(*refs):
    (
        (tokens, gains, q, k, v, o, kw, vw),
        (h_all, hs, gq, gkv, go, kv),
        (h_low, mini),
        row_sems,
        spread_sems,
        slice_sems,
        share_sems,
        own_sems,
        probe_sems,
    ) = taken(refs, 8, 6, 2, 2, 2, 2, 2, 1, 10)
    d, t = places()
    core = lax.rem(t, 2)
    wide = tokens[...].astype(F32)
    inverse = lax.rsqrt(mean_of(wide * wide) + EPS)
    h_low[...] = (wide * inverse * gains[0:1]).astype(BF16)
    enter(True, True)
    spread = DataSpread(h_low, mini, *spread_sems)
    rows = TensorGather(h_low, slot_of(h_all), *row_sems)
    slices = TensorGather(mini, lambda block: hs.at[:, block], *slice_sems)
    share = CoreShare((kw, vw), lambda j, c: kv.at[:, strip(j, c)], *share_sems)
    probes = Probes(0, (q, k, v, o), (gq, gkv, go), probe_sems)
    own = [
        pltpu.make_async_copy(src, kv.at[:, strip(j, core)], own_sems[0].at[j])
        for j, src in enumerate((kw, vw))
    ]
    spread.start()
    rows.start()
    probes.start()
    rows.relay()
    spread.finish()
    slices.start()
    share.start()
    for copy in own:
        copy.start()
    rows.finish()
    probes.relay()
    slices.relay()
    slices.finish()
    share.finish()
    for copy in own:
        copy.wait()
    probes.finish()


def first(tokens, gains, probes, kw, vw):
    rows, width = tokens.shape
    return comm_call(
        first_kernel,
        "first",
        1,
        [VMEM, VMEM] + [HBM] * 6,
        [VMEM] + [HBM] * 5,
        [shape((16, rows, width), BF16), shape((8, 16, rows, width // 8), BF16)]
        + Probes.shapes(probes)
        + [shape((2, 4 * kw.shape[1], width), BF16)],
        [pltpu.VMEM((rows, width), BF16), pltpu.VMEM((8, rows, width // 8), BF16)]
        + TensorGather.scratch
        + DataSpread.scratch
        + TensorGather.scratch
        + CoreShare.scratch
        + [DMA((2,))]
        + Probes.scratch,
        (tokens, gains) + probes + (kw, vw),
    )


def between_kernel(*refs):
    (
        (primal, moved, tokens, gains, q, k, v, o),
        (x_out, t_out, h_all, th_all, gq, gkv, go),
        (h_low, th_low),
        sum_a,
        sum_b,
        gather_a,
        gather_b,
        sems,
    ) = taken(refs, 8, 7, 2, 5, 5, 2, 2, 10)
    gain = gains[1:2]
    enter(True, True)
    sums = [TensorSum(primal, *sum_a), TensorSum(moved, *sum_b)]
    probes = Probes(1, (q, k, v, o), (gq, gkv, go), sems)
    for one in sums:
        one.start()
    for one in sums:
        one.send()
    probes.start()
    for one in sums:
        one.middle()
    stream = (tokens[...].astype(F32) + sums[0].total()).astype(BF16)
    x_out[...] = stream
    wide = stream.astype(F32)
    inverse = lax.rsqrt(mean_of(wide * wide) + EPS)
    h_low[...] = (wide * inverse * gain).astype(BF16)
    rows_a = TensorGather(h_low, slot_of(h_all), *gather_a)
    rows_a.start()
    tangent = sums[1].total()
    t_out[...] = tangent
    shift = mean_of(wide * tangent)
    th_low[...] = (gain * (tangent * inverse - wide * inverse * inverse * inverse * shift)).astype(
        BF16
    )
    rows_b = TensorGather(th_low, slot_of(th_all), *gather_b)
    rows_b.start()
    rows_a.relay()
    probes.relay()
    rows_b.relay()
    for one in sums:
        one.finish()
    rows_a.finish()
    rows_b.finish()
    probes.finish()


def between(primal, moved, tokens, gains, probes):
    rows, width = tokens.shape
    return comm_call(
        between_kernel,
        "between",
        2,
        [VMEM] * 4 + [HBM] * 4,
        [VMEM] * 4 + [HBM] * 3,
        [
            shape((rows, width), BF16),
            shape((rows, width), F32),
            shape((16, rows, width), BF16),
            shape((16, rows, width), BF16),
        ]
        + Probes.shapes(probes),
        [pltpu.VMEM((rows, width), BF16)] * 2
        + TensorSum.scratch(width) * 2
        + TensorGather.scratch * 2
        + Probes.scratch,
        (primal, moved, tokens, gains) + probes,
    )


def turn_kernel(*refs):
    (
        (lengths, moved, t_one, a_zero, a_one, h_one),
        (c_out, cb_all, ga_zero, ga_one, hs_one),
        (c_low,),
        sum_a,
        gather_a,
        sems,
    ) = taken(refs, 6, 5, 1, 5, 2, 6)
    d, t = places()
    enter(True, True)
    total = TensorSum(moved, *sum_a)
    jobs = [
        DataGather(a_zero, slot_of(ga_zero), *sems[0:2]),
        DataGather(a_one, slot_of(ga_one), *sems[2:4]),
    ]
    swap = DataExchange(h_one, hs_one, *sems[4:6])
    total.start()
    total.send()
    for job in jobs:
        job.start()
    total.middle()
    swap.start()
    position = t * t_one.shape[0] + lax.broadcasted_iota(jnp.int32, t_one.shape, 0)
    mask = jnp.where(position < lengths[d], 1.0, 0.0)
    cotangent = mask * (t_one[...] + total.total())
    c_out[...] = cotangent
    c_low[...] = cotangent.astype(BF16)
    rows = TensorGather(c_low, slot_of(cb_all), *gather_a)
    rows.start()
    for job in jobs:
        job.relay()
    rows.relay()
    total.finish()
    rows.finish()
    swap.finish()
    for job in jobs:
        job.finish()


SMEM = pl.BlockSpec(memory_space=pltpu.SMEM)


def turn(lengths, moved, t_one, a_zero, a_one, h_one):
    rows, width = t_one.shape
    return comm_call(
        turn_kernel,
        "turn",
        3,
        [SMEM] + [VMEM] * 2 + [HBM] * 3,
        [VMEM] * 2 + [HBM] * 3,
        [
            shape((rows, width), F32),
            shape((16, rows, width), BF16),
            shape((8,) + a_zero.shape, BF16),
            shape((8,) + a_one.shape, BF16),
            shape((8, h_one.shape[0], h_one.shape[1] // 8), BF16),
        ],
        [pltpu.VMEM((rows, width), BF16)]
        + TensorSum.scratch(width)
        + TensorGather.scratch
        + DataGather.scratch * 2
        + DataExchange.scratch,
        (lengths, moved, t_one, a_zero, a_one, h_one),
    )


class Cotangents:
    def __init__(self, gq, gkv, gathered, came, merged, sems):
        self.gkv, self.came, self.merged = gkv, came, merged
        width = gq.shape[1]
        self.jobs = [
            DataGather(gq, lambda block: gathered.at[block, :, 0:width], *sems[0:2]),
            DataGather(
                merged,
                lambda block: gathered.at[block, :, width : width + merged.shape[1]],
                *sems[2:4],
            ),
        ]
        self.sends, self.recvs = sems[4:6]

    @staticmethod
    def scratch(gkv):
        return (
            [pltpu.VMEM(gkv.shape[1:], BF16)] * 2
            + DataGather.scratch * 2
            + [DMA((1,)), DMA((1,))]
        )

    def swap(self):
        d, t = places()
        return remote(
            self.gkv.at[1 - lax.rem(t, 2)],
            self.came,
            self.sends,
            self.recvs,
            0,
            (d, other_core(t)),
        )

    def start(self):
        d, t = places()
        self.swap().start()
        self.jobs[0].start()
        self.swap().wait()
        mine = self.gkv[lax.rem(t, 2)].astype(F32) + self.came[...].astype(F32)
        self.merged[...] = mine.astype(BF16)
        self.jobs[1].start()

    def relay(self):
        for job in self.jobs:
            job.relay()

    def finish(self):
        for job in self.jobs:
            job.finish()


def lower_kernel(*refs):
    (
        (part, c_two, x_one, gains, gkv, gq, cb_one),
        (cb_all, gg, cbs, mini),
        (c_low,),
        sum_a,
        gather_a,
        (came, merged),
        sems,
        swap_sems,
        spread_sems,
    ) = taken(refs, 7, 4, 1, 5, 2, 2, 6, 2, 2)
    enter(True, True)
    total = TensorSum(part, *sum_a)
    jobs = Cotangents(gq, gkv, gg, came, merged, sems)
    swap = DataExchange(cb_one, cbs, *swap_sems)
    total.start()
    total.send()
    jobs.start()
    total.middle()
    swap.start()
    scaled = total.total() * gains[1:2]
    wide = x_one[...].astype(F32)
    inverse = lax.rsqrt(mean_of(wide * wide) + EPS)
    shift = mean_of(wide * scaled)
    cotangent = c_two[...] + inverse * (scaled - wide * inverse * inverse * shift)
    c_low[...] = cotangent.astype(BF16)
    rows = TensorGather(c_low, slot_of(cb_all), *gather_a)
    spread = DataSpread(c_low, mini, *spread_sems)
    rows.start()
    spread.start()
    jobs.relay()
    rows.relay()
    total.finish()
    rows.finish()
    swap.finish()
    spread.finish()
    jobs.finish()


def lower(part, c_two, x_one, gains, gkv, gq, cb_one):
    rows, width = c_two.shape
    return comm_call(
        lower_kernel,
        "lower",
        4,
        [VMEM] * 5 + [HBM] * 2,
        [VMEM] + [HBM] * 3,
        [
            shape((16, rows, width), BF16),
            shape((8, gq.shape[0], gq.shape[1] + gkv.shape[2]), BF16),
            shape((8, cb_one.shape[0], width // 8), BF16),
            shape((8, rows, width // 8), BF16),
        ],
        [pltpu.VMEM((rows, width), BF16)]
        + TensorSum.scratch(width)
        + TensorGather.scratch
        + Cotangents.scratch(gkv)
        + DataExchange.scratch
        + DataSpread.scratch,
        (part, c_two, x_one, gains, gkv, gq, cb_one),
    )


def last_kernel(*refs):
    (gkv, mini, gq), (gg, cbs), (came, merged), sems, slice_sems = taken(refs, 3, 2, 2, 6, 2)
    enter(True, True)
    slices = TensorGather(mini, lambda block: cbs.at[:, block], *slice_sems)
    jobs = Cotangents(gq, gkv, gg, came, merged, sems)
    slices.start()
    jobs.start()
    slices.relay()
    jobs.relay()
    slices.finish()
    jobs.finish()


def last(gkv, mini, gq):
    return comm_call(
        last_kernel,
        "last",
        5,
        [VMEM] * 2 + [HBM],
        [HBM] * 2,
        [
            shape((8, gq.shape[0], gq.shape[1] + gkv.shape[2]), BF16),
            shape((8, 16) + mini.shape[1:], BF16),
        ],
        Cotangents.scratch(gkv) + TensorGather.scratch,
        (gkv, mini, gq),
    )


def contract(left_side, right_side, left_dim, right_dim):
    return lax.dot_general(
        left_side,
        right_side,
        (((left_dim,), (right_dim,)), ((), ())),
        preferred_element_type=F32,
    )


def turned(values, cosine, sine):
    return values * cosine + pltpu.roll(values, values.shape[1] // 2, 1) * sine


def attention_weights(q, k, length):
    size = q.shape[0]
    row = lax.broadcasted_iota(jnp.int32, (size, size), 0)
    column = lax.broadcasted_iota(jnp.int32, (size, size), 1)
    allowed = (column <= row) & (column < length)
    scores = contract(q, k, 1, 1) * (1.0 / math.sqrt(q.shape[1]))
    powers = jnp.where(allowed, jnp.exp(scores), 0.0)
    return powers / jnp.sum(powers, axis=-1, keepdims=True)


def forward_kernel(steps, second, *refs):
    more = 1 if second else 0
    (
        (lengths, cosine, sine, wq, kv, pq, pkv, wo, po, h),
        th,
        (q_out, k_out, v_out, a_out, moved),
        primal,
        (q_sum, tq_sum, kv_sum, tkv_sum, ta_low),
    ) = taken(refs, 10, more, 5, 1 - more, 5)
    i = pl.program_id(0)
    sums = (q_sum, tq_sum, kv_sum, tkv_sum)

    @pl.when(i == 0)
    def _():
        for one in sums:
            one[...] = jnp.zeros_like(one)

    @pl.when(i < steps)
    def _():
        normed = h[...]
        q_sum[...] += contract(normed, wq[...], 1, 0)
        kv_sum[...] += contract(normed, kv[...], 1, 1)
        tq = contract(normed, pq[...], 1, 0)
        tkv = contract(normed, pkv[...], 1, 1)
        if second:
            tq = tq + contract(th[0][...], wq[...], 1, 0)
            tkv = tkv + contract(th[0][...], kv[...], 1, 1)
        tq_sum[...] += tq
        tkv_sum[...] += tkv

    @pl.when(i == steps - 1)
    def _():
        length = lengths[lax.axis_index("dp")]
        scaling = 1.0 / math.sqrt(HD)
        cos, sin = cosine[...], sine[...]
        k = turned(kv_sum[:, 0:HD], cos, sin).astype(BF16)
        v = kv_sum[:, HD:].astype(BF16)
        tk = turned(tkv_sum[:, 0:HD], cos, sin).astype(BF16)
        tv = tkv_sum[:, HD:].astype(BF16)
        k_out[...] = k
        v_out[...] = v
        for at in range(0, q_sum.shape[1], HD):
            head = slice(at, at + HD)
            q = turned(q_sum[:, head], cos, sin).astype(BF16)
            tq = turned(tq_sum[:, head], cos, sin).astype(BF16)
            q_out[:, head] = q
            weights = attention_weights(q, k, length)
            low = weights.astype(BF16)
            a_out[:, head] = contract(low, v, 1, 0).astype(BF16)
            scores = (contract(tq, k, 1, 1) + contract(q, tk, 1, 1)) * scaling
            change = weights * (scores - jnp.sum(weights * scores, axis=-1, keepdims=True))
            ta = contract(change.astype(BF16), v, 1, 0) + contract(low, tv, 1, 0)
            ta_low[:, head] = ta.astype(BF16)

    @pl.when(i >= steps)
    def _():
        moved[...] = (
            contract(ta_low[...], wo[...], 1, 0) + contract(a_out[...], po[...], 1, 0)
        ).astype(BF16)
        if not second:
            primal[0][...] = contract(a_out[...], wo[...], 1, 0).astype(BF16)


def whole(dims):
    return pl.BlockSpec(dims, lambda i: (0,) * len(dims))


TILE = 1024


def forward(layer, lengths, tables, wq, kv, pq, pkv, wo, po, h, th=None):
    rows, width = h.shape
    columns = wq.shape[2]
    steps = width // TILE
    second = th is not None

    def now(i):
        return jnp.minimum(i, steps - 1)

    def later(i):
        return jnp.maximum(i - steps, 0)

    into = pl.BlockSpec((rows, TILE), lambda i: (0, now(i)))
    out = pl.BlockSpec((rows, TILE), lambda i: (0, later(i)))
    in_specs = [
        SMEM,
        whole((rows, HD)),
        whole((rows, HD)),
        pl.BlockSpec((None, TILE, columns), lambda i: (layer, now(i), 0)),
        pl.BlockSpec((None, 2 * HD, TILE), lambda i: (layer, 0, now(i))),
        pl.BlockSpec((TILE, columns), lambda i: (now(i), 0)),
        pl.BlockSpec((2 * HD, TILE), lambda i: (0, now(i))),
        pl.BlockSpec((None, columns, TILE), lambda i: (layer, 0, later(i))),
        pl.BlockSpec((columns, TILE), lambda i: (0, later(i))),
        into,
    ] + [into] * second
    out_specs = [
        whole((rows, columns)),
        whole((rows, HD)),
        whole((rows, HD)),
        whole((rows, columns)),
        out,
    ] + [out] * (not second)
    out_shape = [
        shape((rows, columns), BF16),
        shape((rows, HD), BF16),
        shape((rows, HD), BF16),
        shape((rows, columns), BF16),
        shape((rows, width), BF16),
    ] + [shape((rows, width), BF16)] * (not second)
    args = (lengths,) + tables + (wq, kv, pq, pkv, wo, po, h) + ((th,) if second else ())
    return pl.pallas_call(
        functools.partial(forward_kernel, steps, second),
        name=f"forward_{layer}",
        grid=(2 * steps,),
        in_specs=in_specs,
        out_specs=out_specs,
        out_shape=out_shape,
        scratch_shapes=[
            pltpu.VMEM((rows, columns), F32),
            pltpu.VMEM((rows, columns), F32),
            pltpu.VMEM((rows, 2 * HD), F32),
            pltpu.VMEM((rows, 2 * HD), F32),
            pltpu.VMEM((rows, columns), BF16),
        ],
        compiler_params=pltpu.CompilerParams(vmem_limit_bytes=40 * 2**20),
    )(*args)


def backward_kernel(steps, lowest, *refs):
    more = 0 if lowest else 1
    (
        (lengths, cosine, sine, q_in, k_in, v_in, cb, wo),
        weights_in,
        (gq_out, gkv_out),
        part,
        (ga_sum, gkv_low),
    ) = taken(refs, 8, 2 * more, 2, more, 2)
    i = pl.program_id(0)

    @pl.when(i == 0)
    def _():
        ga_sum[...] = jnp.zeros_like(ga_sum)

    @pl.when(i < steps)
    def _():
        ga_sum[...] += contract(cb[...], wo[...], 1, 1)

    @pl.when(i == steps - 1)
    def _():
        length = lengths[lax.axis_index("dp")]
        scaling = 1.0 / math.sqrt(HD)
        cos, sin = cosine[...], -sine[...]
        k, v = k_in[...], v_in[...]
        gk, gv = None, None
        for at in range(0, ga_sum.shape[1], HD):
            head = slice(at, at + HD)
            q = q_in[:, head]
            ga = ga_sum[:, head].astype(BF16)
            weights = attention_weights(q, k, length)
            grads = contract(ga, v, 1, 1)
            value = contract(weights.astype(BF16), ga, 0, 0)
            scores = (
                weights * (grads - jnp.sum(weights * grads, axis=-1, keepdims=True)) * scaling
            ).astype(BF16)
            gq_out[:, head] = turned(contract(scores, k, 1, 0), cos, sin).astype(BF16)
            key = contract(scores, q, 0, 0)
            gk = key if gk is None else gk + key
            gv = value if gv is None else gv + value
        gk = turned(gk, cos, sin).astype(BF16)
        gv = gv.astype(BF16)
        half = HD // 2
        gkv_low[:, 0:HD] = gk
        gkv_low[:, HD:] = gv
        gkv_out[0] = jnp.concatenate([gk[:, 0:half], gv[:, 0:half]], axis=-1)
        gkv_out[1] = jnp.concatenate([gk[:, half:], gv[:, half:]], axis=-1)

    if not lowest:

        @pl.when(i >= steps)
        def _():
            part[0][...] = (
                contract(gq_out[...], weights_in[0][...], 1, 1)
                + contract(gkv_low[...], weights_in[1][...], 1, 0)
            ).astype(BF16)


def backward(layer, lengths, tables, q, k, v, cb, wo, wq, kv):
    rows, width = cb.shape
    columns = wo.shape[1]
    steps = width // TILE
    lowest = layer == 0

    def now(i):
        return jnp.minimum(i, steps - 1)

    def later(i):
        return jnp.maximum(i - steps, 0)

    in_specs = [
        SMEM,
        whole((rows, HD)),
        whole((rows, HD)),
        whole((rows, columns)),
        whole((rows, HD)),
        whole((rows, HD)),
        pl.BlockSpec((rows, TILE), lambda i: (0, now(i))),
        pl.BlockSpec((None, columns, TILE), lambda i: (layer, 0, now(i))),
    ]
    out_specs = [whole((rows, columns)), whole((2, rows, HD))]
    out_shape = [shape((rows, columns), BF16), shape((2, rows, HD), BF16)]
    args = (lengths,) + tables + (q, k, v, cb, wo)
    if not lowest:
        in_specs += [
            pl.BlockSpec((None, TILE, columns), lambda i: (layer, later(i), 0)),
            pl.BlockSpec((None, 2 * HD, TILE), lambda i: (layer, 0, later(i))),
        ]
        out_specs.append(pl.BlockSpec((rows, TILE), lambda i: (0, later(i))))
        out_shape.append(shape((rows, width), BF16))
        args += (wq, kv)
    return pl.pallas_call(
        functools.partial(backward_kernel, steps, lowest),
        name=f"backward_{layer}",
        grid=(steps if lowest else 2 * steps,),
        in_specs=in_specs,
        out_specs=out_specs,
        out_shape=out_shape,
        scratch_shapes=[
            pltpu.VMEM((rows, columns), F32),
            pltpu.VMEM((rows, 2 * HD), BF16),
        ],
        compiler_params=pltpu.CompilerParams(vmem_limit_bytes=40 * 2**20),
    )(*args)


def products_kernel(*refs):
    sides, (q_out, k_out, v_out, o_out) = taken(refs, 8, 4)
    i = pl.program_id(0)
    columns, half = q_out.shape[2], k_out.shape[1]
    for layer in range(2):
        hs, gg, ga, cs = [ref[...].reshape(-1, ref.shape[-1]) for ref in sides[4 * layer :][:4]]
        q = contract(hs, gg[:, 0:columns], 0, 0)
        kv = contract(gg[:, columns:], hs, 0, 0)
        o = contract(ga, cs, 0, 0)

        @pl.when(i == 0)
        def _():
            q_out[layer] = q
            k_out[layer] = kv[0:half]
            v_out[layer] = kv[half:]
            o_out[layer] = o

        @pl.when(i > 0)
        def _():
            q_out[layer] += q
            k_out[layer] += kv[0:half]
            v_out[layer] += kv[half:]
            o_out[layer] += o


def products(*sides):
    chunk = 2
    columns, share = sides[2].shape[2], sides[0].shape[2]
    half = (sides[1].shape[2] - columns) // 2
    out_shape = [
        shape((2, share, columns), F32),
        shape((2, half, share), F32),
        shape((2, half, share), F32),
        shape((2, columns, share), F32),
    ]
    return pl.pallas_call(
        products_kernel,
        name="products",
        grid=(8 // chunk,),
        in_specs=[
            pl.BlockSpec((chunk,) + side.shape[1:], lambda i: (i, 0, 0)) for side in sides
        ],
        out_specs=[whole(out.shape) for out in out_shape],
        out_shape=out_shape,
        compiler_params=pltpu.CompilerParams(vmem_limit_bytes=40 * 2**20),
    )(*sides)


def rope_tables():
    angles = np.arange(LEN)[:, None] * THETA ** (-2.0 * np.arange(HD // 2) / HD)[None, :]
    cosine, sine = np.cos(angles), np.sin(angles)
    return (
        jnp.asarray(np.concatenate([cosine, cosine], axis=1), F32),
        jnp.asarray(np.concatenate([-sine, sine], axis=1), F32),
    )


def body(
    tokens,
    lengths,
    gains,
    query_weight,
    key_weight,
    value_weight,
    out_weight,
    query_probe,
    key_probe,
    value_probe,
    out_probe,
):
    rows, width = tokens.shape
    tables = rope_tables()

    def turned_over(array):
        return jnp.swapaxes(array, 1, 2)

    def by_owner(part):
        return part.reshape(8, 2, rows, width)

    def all_rows(blocks):
        return blocks.reshape(-1, blocks.shape[-1])

    def by_batch(blocks):
        return blocks.reshape(blocks.shape[0], -1, blocks.shape[-1])

    probes = (query_probe, turned_over(key_probe), turned_over(value_probe), out_probe)
    h_zero, hs_zero, pq, pkv, po, kv = first(
        tokens, gains, probes, turned_over(key_weight), turned_over(value_weight)
    )
    q0, k0, v0, a_zero, moved, primal = forward(
        0, lengths, tables, query_weight, kv, all_rows(pq), pkv, out_weight, po, all_rows(h_zero)
    )
    x_one, t_one, h_one, th_one, pq, pkv, po = between(
        by_owner(primal), by_owner(moved), tokens, gains, probes
    )
    h_one = all_rows(h_one)
    q1, k1, v1, a_one, moved = forward(
        1,
        lengths,
        tables,
        query_weight,
        kv,
        all_rows(pq),
        pkv,
        out_weight,
        po,
        h_one,
        all_rows(th_one),
    )
    c_two, cb_one, ga_zero, ga_one, hs_one = turn(
        lengths, by_owner(moved), t_one, a_zero, a_one, h_one
    )
    cb_one = all_rows(cb_one)
    gq, gkv, part = backward(
        1, lengths, tables, q1, k1, v1, cb_one, out_weight, query_weight, kv
    )
    cb_zero, gg_one, cs_one, mini = lower(
        by_owner(part), c_two, x_one, gains, gkv, gq, cb_one
    )
    gq, gkv = backward(
        0, lengths, tables, q0, k0, v0, all_rows(cb_zero), out_weight, query_weight, kv
    )
    gg_zero, cs_zero = last(gkv, mini, gq)
    q, k, v, o = products(
        by_batch(hs_zero), gg_zero, ga_zero, by_batch(cs_zero), hs_one, gg_one, ga_one, cs_one
    )
    return (q, turned_over(k), turned_over(v), o)


def solution(mesh):
    placed = (
        P(("dp", "tensor"), None),
        P(),
        P(),
        P(None, None, "tensor"),
        P(None, None, "tensor"),
        P(None, None, "tensor"),
        P(None, "tensor", None),
        P(None, "dp", "tensor"),
        P(None, "dp", "tensor"),
        P(None, "dp", "tensor"),
        P(None, "tensor", "dp"),
    )
    return jax.shard_map(
        body,
        mesh=mesh,
        in_specs=placed,
        out_specs=(
            P(None, "dp", "tensor"),
            P(None, "dp", "tensor"),
            P(None, "dp", "tensor"),
            P(None, "tensor", "dp"),
        ),
        check_vma=False,
    )
```

time: 432 us -> 276 us (0.64)
  matrix products: 63.6 us -> 0 us
  local copies, waits for them, and re-layouts: 49.5 us -> 13.4 us
  Pallas kernels: 293 us -> 261 us
  other arithmetic: 16.5 us -> 0 us
    pallas_call x5, Pallas kernels: 293 us -> 222 us  [comm_call(): pl.pallas_call(kernel, name=name, in_specs=in_specs, out_specs=out_specs,...]
    dot_general x43 -> x0, matrix products: 60.2 us -> none  [the longest x15 25.7 us: matmul(): return jnp.dot(left_side, right_side, preferred_element_type=F32)]
    pallas_call x0 -> x5, Pallas kernels: none -> 39.2 us  [the longest x2 21.2 us: forward(): pl.pallas_call(functools.partial(forward_kernel, steps, second), name=f'f...]
    dot_general x4 -> x0, local copies, waits for them, and re-layouts: 17.1 us -> none  [matmul(): return jnp.dot(left_side, right_side, preferred_element_type=F32)]
    another operation x11 -> x0, other arithmetic: 8.52 us -> none
    slice x11 -> x0, local copies, waits for them, and re-layouts: 6.34 us -> none  [the longest x4 3.43 us: forward(): own[:, at:at + half]]
    unnamed x185 -> x46, local copies, waits for them, and re-layouts: 18.9 us -> 13.4 us
  transfers between devices with their start and end apart: 4 -> 0, of which waited for: 0 -> 0; matrix products, arithmetic and copies ran while one was open for 9% -> 0% of each run, Pallas kernels for 0% -> 0%
where the time goes in v2:
time: 276 us
  Pallas kernels  261 us (95%)
  local copies, waits for them, and re-layouts  13.4 us (5%)
    pallas_call x5, Pallas kernels, comm_call(): pl.pallas_call(kernel, name=name, in_specs=in_specs, out_specs=out_specs,...  222 us
    pallas_call x2, Pallas kernels, forward(): pl.pallas_call(functools.partial(forward_kernel, steps, second), name=f'f...  21.2 us
    unnamed x46, local copies, waits for them, and re-layouts  13.4 us
    pallas_call x2, Pallas kernels, backward(): pl.pallas_call(functools.partial(backward_kernel, steps, lowest), name=f'...  10.9 us
    pallas_call x1, Pallas kernels, products(): pl.pallas_call(products_kernel, name='products', grid=(8 // chunk,), in_s...  7.1 us

profile of v2, /device:TPU:1, one launch (start us, length us, event | category | flops | bytes accessed | tf_op | source)
XLA Modules:
  0.0 275.6 jit_solution(12794034444662039877)
XLA Ops:
  0.6 0.0 copy-start.4
  0.6 0.0 copy-start.5
  0.7 0.0 copy-start.11
  0.7 1.1 copy-done.11
  1.7 0.0 copy-start.12
  1.7 1.0 copy-done.12
  2.8 0.0 copy-start.13
  2.8 1.2 copy-done.13
  4.0 0.0 copy-start.14
  4.0 1.2 copy-done.14
  5.2 0.9 copy-done.17
  6.1 0.9 copy-done.18
  7.0 0.9 copy-done.19
  8.0 0.8 copy-done.20
  8.7 55.4 %first.1 = (bf16[16,16,4096]{2,1,0:T(8,128)(2,1)S(1)}, bf16[8,16,16,512]{3,2,1,0:T(8,128)(2,1)S(1)}, bf16[8,512,256]{2,1,0:T(8,128)(2,1)S(1)}, bf16[256,4096]{1,...) custom-call(bf16[16,4096]{1,0:T(8,128)(2,1)S(1)} %copy-done.17, ...), custom_call_target="tpu_custom_call" | custom-call | tf_op jit(solution)/shard_map/first/pallas_call | solution.py:400
  64.1 0.0 copy-start.6
  64.1 0.0 copy-done.4
  64.1 0.0 copy-done.5
  64.1 0.0 copy-done.22
  64.1 10.6 %forward_0.1 = (bf16[256,256]{1,0:T(8,128)(2,1)S(1)}, bf16[256,128]{1,0:T(8,128)(2,1)S(1)}, bf16[256,128]{1,0:T(8,128)(2,1)S(1)}, bf16[256,256]{1,0:T(8,128)(2,1...) custom-call(s32[8]{0:T(128)S(1)} %copy-done.22, f32[256,128]{1,0:T(8,128)S(1)} %copy-done.5, ...), custom_call_target="tpu_custom_call" | custom-call | tf_op jit(solution)/shard_map/forward_0/pallas_call | solution.py:991
  74.8 0.0 copy-done.6
  74.8 0.0 copy-start.10
  74.8 1.4 copy-done.10
  76.2 58.2 %between.1 = (bf16[16,4096]{1,0:T(8,128)(2,1)S(1)}, f32[16,4096]{1,0:T(8,128)S(1)}, bf16[16,16,4096]{2,1,0:T(8,128)(2,1)S(1)}, bf16[16,16,4096]{2,1,0:T(8,128)(2...) custom-call(bf16[8,2,16,4096]{3,2,1,0:T(8,128)(2,1)S(1)} %bitcast.32, ...), custom_call_target="tpu_custom_call" | custom-call | tf_op jit(solution)/shard_map/between/pallas_call | solution.py:400
  134.4 0.0 copy-start.1
  134.4 10.5 %forward_1.1 = (bf16[256,256]{1,0:T(8,128)(2,1)S(1)}, bf16[256,128]{1,0:T(8,128)(2,1)S(1)}, bf16[256,128]{1,0:T(8,128)(2,1)S(1)}, bf16[256,256]{1,0:T(8,128)(2,1)S(1)}, bf16[256,4096]{1,0:T(8,128)(2,1)S(1)}) custom-call(s32[8]{0:T(128)S(1)} %copy-done.22, f32[256,128]{1,0:T(8,128)S(1)} %copy-done.5, f32[256,128]{1,0:T(8,128)S(1)} %copy-done.4, ...), custom_call_target="tpu_custom_call" | custom-call | tf_op jit(solution)/shard_map/forward_1/pallas_call | solution.py:991
  145.0 0.0 copy-start
  145.0 45.3 %turn.1 = (f32[16,4096]{1,0:T(8,128)S(1)}, bf16[16,16,4096]{2,1,0:T(8,128)(2,1)S(1)}, bf16[8,256,256]{2,1,0:T(8,128)(2,1)S(1)}, bf16[8,256,256]{2,1,0:T(8,128)(2,1)S(1)}, bf16[8,256,512]{2,1,0:T(8,128)(2,1)S(1)}) custom-call(s32[8]{0:T(128)S(1)} %copy-done.22, bf16[8,2,16,4096]{3,2,1,0:T(8,128)(2,1)S(1)} %bitcast.27, ...), custom_call_target="tpu_custom_call" | custom-call | tf_op jit(solution)/shard_map/turn/pallas_call | solution.py:400
  190.3 0.0 copy-start.8
  190.3 1.4 copy-done.8
  191.7 1.0 copy-done.15
  192.7 0.0 copy-done.1
  192.7 0.0 copy-done
  192.7 7.5 %backward_1.1 = (bf16[256,256]{1,0:T(8,128)(2,1)S(1)}, bf16[2,256,128]{2,1,0:T(8,128)(2,1)S(1)}, bf16[256,4096]{1,0:T(8,128)(2,1)S(1)}) custom-call(s32[8]{0:T(128)S(1)} %copy-done.22, f32[256,128]{1,0:T(8,128)S(1)} %copy-done.5, f32[256,128]{1,0:T(8,128)S(1)} %copy-done.4, bf16[256,256]{1,0:T(8,128)(2,1)S(1)} %get-tuple-element.64.refs_3_, ...), custom_call_target="tpu_custom_call" | custom-call | tf_op jit(solution)/shard_map/backward_1/pallas_call | solution.py:1100
  200.2 0.0 copy-done.2
  200.2 0.0 copy-done.21
  200.2 0.0 copy-start.3
  200.2 1.6 copy-done.3
  201.8 45.3 %lower.1 = (bf16[16,16,4096]{2,1,0:T(8,128)(2,1)S(1)}, bf16[8,256,384]{2,1,0:T(8,128)(2,1)S(1)}, bf16[8,256,512]{2,1,0:T(8,128)(2,1)S(1)}, bf16[8,16,512]{2,1,0:T(8,128)(2,1)S(1)}) custom-call(bf16[8,2,16,4096]{3,2,1,0:T(8,128)(2,1)S(1)} %bitcast.28, f32[16,4096]{1,0:T(8,128)S(1)} %get-tuple-element.73.refs_1_, ...), custom_call_target="tpu_custom_call" | custom-call | tf_op jit(solution)/shard_map/lower/pallas_call | solution.py:400
  247.1 0.0 copy-start.7
  247.1 0.0 copy-start.9
  247.1 0.0 copy-start.16
  247.1 3.4 %backward_0.1 = (bf16[256,256]{1,0:T(8,128)(2,1)S(1)}, bf16[2,256,128]{2,1,0:T(8,128)(2,1)S(1)}) custom-call(s32[8]{0:T(128)S(1)} %copy-done.22, f32[256,128]{1,0:T(8,128)S(1)} %copy-done.5, f32[256,128]{1,0:T(8,128)S(1)} %copy-done.4, bf16[256,256]{1,0:T(8,128)(2,1)S(1)} %get-tuple-element.54.refs_3_, bf16[256,128]{1,0:T(8,128)(2,1)S(1)} %get-tuple-element.55.refs_4_, ...), custom_call_target="tpu_custom_call" | custom-call | tf_op jit(solution)/shard_map/backward_0/pallas_call | solution.py:1100
  250.5 18.0 %last.1 = (bf16[8,256,384]{2,1,0:T(8,128)(2,1)S(1)}, bf16[8,16,16,512]{3,2,1,0:T(8,128)(2,1)S(1)}) custom-call(bf16[2,256,128]{2,1,0:T(8,128)(2,1)S(1)} %get-tuple-element.78.refs_0_, bf16[8,16,512]{2,1,0:T(8,128)(2,1)S(1)} %get-tuple-element.79.refs_1_, bf16[256,256]{1,0:T(8,128)(2,1)S(1)} %get-tuple-element.80.refs_2_), custom_call_target="tpu_custom_call" | custom-call | tf_op jit(solution)/shard_map/last/pallas_call | solution.py:400
  268.5 0.0 copy-done.7
  268.5 0.0 copy-done.9
  268.5 0.0 copy-done.16
  268.5 7.1 %products.1 = (f32[2,512,256]{2,1,0:T(8,128)}, f32[2,64,512]{2,1,0:T(8,128)}, f32[2,64,512]{2,1,0:T(8,128)}, f32[2,256,512]{2,1,0:T(8,128)}) custom-call(bf16[8,256,512]{2,1,0:T(8,128)(2,1)S(1)} %bitcast.30, bf16[8,256,384]{2,1,0:T(8,128)(2,1)S(1)} %get-tuple-element.81.refs_1_, bf16[8,256,256]{2,1,0:T(8,128)(2,1)S(1)} %get-tuple-element.82.refs_2_, ...), custom_call_target="tpu_custom_call" | custom-call | tf_op jit(solution)/shard_map/products/pallas_call | solution.py:1150
  (8 shorter events, 0.0 us)
Async XLA Ops:
  0.6 63.5 %copy-start.4 = (f32[256,128]{1,0:T(8,128)S(1)}, f32[256,128]{1,0:T(8,128)}, u32[]{:S(2)}) copy-start(f32[256,128]{1,0:T(8,128)} %constant.5.clone.refs_2_) | copy-start | bytes 393220
  0.6 63.5 %copy-start.5 = (f32[256,128]{1,0:T(8,128)S(1)}, f32[256,128]{1,0:T(8,128)}, u32[]{:S(2)}) copy-start(f32[256,128]{1,0:T(8,128)} %constant.4.clone.refs_1_) | copy-start | bytes 393220
  0.7 1.1 copy-start.11
  1.7 1.0 copy-start.12
  2.8 1.2 copy-start.13
  4.0 1.2 copy-start.14
  5.2 0.9 copy-start.17
  6.1 0.9 copy-start.18
  7.0 0.9 copy-start.19
  7.9 0.8 copy-start.20
  8.7 55.4 %copy-start.22 = (s32[8]{0:T(128)S(1)}, s32[8]{0:T(128)}, u32[]{:S(2)}) copy-start(s32[8]{0:T(128)} %refs_0_.11) | copy-start | bytes 100
  64.1 10.7 %copy-start.6 = (bf16[8,16,16,512]{3,2,1,0:T(8,128)(2,1)}, bf16[8,16,16,512]{3,2,1,0:T(8,128)(2,1)S(1)}, u32[]{:S(2)}) copy-start(bf16[8,16,16,512]{3,2,1,0:T(8,128)(2,1)S(1)} %get-tuple-element.48) | copy-start | bytes 6291460
  74.8 1.4 copy-start.10
  134.4 58.2 %copy-start.1 = (bf16[2,4096,256]{2,1,0:T(8,128)(2,1)S(1)}, bf16[2,4096,256]{2,1,0:T(8,128)(2,1)}, u32[]{:S(2)}) copy-start(bf16[2,4096,256]{2,1,0:T(8,128)(2,1)} %refs_8_.1) | copy-start | bytes 12582916
  145.0 47.7 %copy-start = (bf16[2,256,4096]{2,1,0:T(8,128)(2,1)S(1)}, bf16[2,256,4096]{2,1,0:T(8,128)(2,1)}, u32[]{:S(2)}) copy-start(bf16[2,256,4096]{2,1,0:T(8,128)(2,1)} %refs_7_.9) | copy-start | bytes 12582916
  190.3 1.4 copy-start.8
  191.7 1.0 copy-start.15
  192.7 7.6 %copy-start.2 = (bf16[16,16,4096]{2,1,0:T(8,128)(2,1)}, bf16[16,16,4096]{2,1,0:T(8,128)(2,1)S(1)}, u32[]{:S(2)}) copy-start(bf16[16,16,4096]{2,1,0:T(8,128)(2,1)S(1)} %get-tuple-element.71) | copy-start | bytes 6291460
  192.7 7.6 %copy-start.21 = (f32[2,4096]{1,0:T(2,128)S(1)}, f32[2,4096]{1,0:T(2,128)}, u32[]{:S(2)}) copy-start(f32[2,4096]{1,0:T(2,128)} %refs_3_.7) | copy-start | bytes 98308
  200.2 1.6 copy-start.3
  247.1 21.4 %copy-start.7 = (bf16[8,16,16,512]{3,2,1,0:T(8,128)(2,1)S(1)}, bf16[8,16,16,512]{3,2,1,0:T(8,128)(2,1)}, u32[]{:S(2)}) copy-start(bf16[8,16,16,512]{3,2,1,0:T(8,128)(2,1)} %copy-done.6) | copy-start | bytes 6291460
  247.1 21.4 %copy-start.9 = (bf16[8,256,512]{2,1,0:T(8,128)(2,1)S(1)}, bf16[8,256,512]{2,1,0:T(8,128)(2,1)}, u32[]{:S(2)}) copy-start(bf16[8,256,512]{2,1,0:T(8,128)(2,1)} %copy-done.8) | copy-start | bytes 6291460
  247.1 21.4 %copy-start.16 = (bf16[8,256,256]{2,1,0:T(8,128)(2,1)S(1)}, bf16[8,256,256]{2,1,0:T(8,128)(2,1)}, u32[]{:S(2)}) copy-start(bf16[8,256,256]{2,1,0:T(8,128)(2,1)} %copy-done.15) | copy-start | bytes 3145732

commit v3 on v2

--- a/solution.py
+++ b/solution.py
@@ -18,10 +18,12 @@
 F32 = jnp.float32
 BF16 = jnp.bfloat16
 VMEM = pl.BlockSpec(memory_space=pltpu.VMEM)
-HBM = pl.BlockSpec(memory_space=pl.ANY)
+ANY = pl.BlockSpec(memory_space=pl.ANY)
+HBM = pl.BlockSpec(memory_space=pltpu.HBM)
 DMA = pltpu.SemaphoreType.DMA
 
 HOPS = ((1, 1), (3, 1), (2, 1), (2, 0), (1, 0), (3, 0), (0, 1))
+NEAR = HOPS[3:]
 
 
 def back(hop):
@@ -60,90 +62,138 @@
     )
 
 
-def enter(over_tensor, over_data):
+def enter(data_hops):
     d, t = places()
     barrier = pltpu.get_barrier_semaphore()
     peers = [(d, other_core(t))]
-    if over_tensor:
-        peers += [(d, tensor_at(t, hop)) for hop in HOPS]
-    if over_data:
-        peers += [(data_at(d, hop), t) for hop in HOPS]
+    peers += [(d, tensor_at(t, hop)) for hop in NEAR]
+    peers += [(data_at(d, hop), t) for hop in data_hops]
     for peer in peers:
         pl.semaphore_signal(barrier, inc=1, device_id=peer, device_id_type=MESH)
     pl.semaphore_wait(barrier, len(peers))
 
 
+def half_of(ref, half):
+    if half is None:
+        return ref
+    rows = ref.shape[0] // 2
+    return ref.at[pl.ds(half * rows, rows)]
+
+
 class RingGather:
-    ROUTES = (
-        ((0, 1), (0, 0), (0, 1)),
-        ((1, 0), (0, 0), (3, 0)),
-        ((3, 0), (0, 0), (1, 0)),
-        ((2, 0), (0, 0), (2, 0)),
-        ((1, 0), (0, 1), (3, 1)),
-        ((3, 0), (0, 1), (1, 1)),
-    )
-    LAST = ((0, 1), (2, 0), (2, 1))
-    WAITS = 7
+    ROUTES = ()
+    FIRST = 0
 
     def __init__(self, src, slot, sends, recvs):
         self.src, self.slot, self.sends, self.recvs = src, slot, sends, recvs
-        self.routes = self.ROUTES + (self.LAST,)
-
-    def place(self, hop):
-        d, t = places()
-        return data_at(d, hop)
-
-    def device(self, hop):
-        d, t = places()
-        return (data_at(d, hop), t)
 
     def out(self, j):
-        hop, block, unused = self.routes[j]
-        slot = self.slot(self.place(block))
-        src = self.src if j < 4 else slot
+        hop, block, unused, half = self.ROUTES[j]
+        slot = half_of(self.slot(self.place(block)), half)
+        src = self.src if j < self.FIRST else slot
         return remote(src, slot, self.sends, self.recvs, j, self.device(hop))
 
     def into(self, j):
-        slot = self.slot(self.place(self.routes[j][2]))
+        slot = half_of(self.slot(self.place(self.ROUTES[j][2])), self.ROUTES[j][3])
         return remote(slot, slot, self.sends, self.recvs, j, self.device((0, 1)))
 
     def own(self):
-        return pltpu.make_async_copy(self.src, self.slot(self.place((0, 0))), self.sends.at[7])
-
-    def hand(self, j):
-        pass
+        n = len(self.ROUTES)
+        return pltpu.make_async_copy(self.src, self.slot(self.place((0, 0))), self.sends.at[n])
 
     def start(self):
-        for j in range(4):
+        for j in range(self.FIRST):
             self.out(j).start()
         self.own().start()
+
+    def sent(self):
+        for j in range(len(self.ROUTES)):
+            self.out(j).wait_send()
+        self.own().wait()
+
+
+class DataGather(RingGather):
+    scratch = [DMA((8,)), DMA((7,))]
+    FIRST = 4
+    ROUTES = (
+        ((0, 1), (0, 0), (0, 1), None),
+        ((1, 0), (0, 0), (3, 0), None),
+        ((3, 0), (0, 0), (1, 0), None),
+        ((2, 0), (0, 0), (2, 0), None),
+        ((1, 0), (0, 1), (3, 1), None),
+        ((3, 0), (0, 1), (1, 1), None),
+        ((0, 1), (2, 0), (2, 1), None),
+    )
+
+    def place(self, hop):
+        d, t = places()
+        return data_at(d, hop)
+
+    def device(self, hop):
+        d, t = places()
+        return (data_at(d, hop), t)
 
     def relay(self):
         self.into(0).wait_recv()
         self.out(4).start()
         self.out(5).start()
-        if self.LAST[0] == (0, 1):
-            self.into(3).wait_recv()
+
+    def pass_on(self):
+        self.into(3).wait_recv()
         self.out(6).start()
-        self.hand(0)
 
     def finish(self):
-        for j in (1, 2, 3, 4, 5, 6):
-            if j != 3 or self.LAST[0] != (0, 1):
-                self.into(j).wait_recv()
-                self.hand(j)
-        for j in range(7):
-            self.out(j).wait_send()
-        self.own().wait()
-
-
-class DataGather(RingGather):
-    scratch = [DMA((8,)), DMA((7,))]
+        for j in (1, 2, 4, 5, 6):
+            self.into(j).wait_recv()
+        self.sent()
+
+
+class LargeGather(DataGather):
+    scratch = [DMA((12,)), DMA((11,))]
+    FIRST = 3
+    ROUTES = (
+        ((0, 1), (0, 0), (0, 1), None),
+        ((1, 0), (0, 0), (3, 0), None),
+        ((3, 0), (0, 0), (1, 0), None),
+        ((1, 0), (0, 1), (3, 1), 0),
+        ((3, 0), (0, 1), (1, 1), 1),
+        ((1, 0), (3, 0), (2, 0), 0),
+        ((0, 1), (3, 0), (3, 1), 1),
+        ((3, 0), (1, 0), (2, 0), 1),
+        ((0, 1), (1, 0), (1, 1), 0),
+        ((1, 0), (3, 1), (2, 1), 0),
+        ((3, 0), (1, 1), (2, 1), 1),
+    )
+
+    def relay(self):
+        for j in range(3):
+            self.into(j).wait_recv()
+            self.out(3 + 2 * j).start()
+            self.out(4 + 2 * j).start()
+
+    def pass_on(self):
+        for j in (3, 4):
+            self.into(j).wait_recv()
+            self.out(6 + j).start()
+
+    def finish(self):
+        for j in range(5, 11):
+            self.into(j).wait_recv()
+        self.sent()
 
 
 class TensorGather(RingGather):
     scratch = [DMA((16,)), DMA((15,))]
-    LAST = ((2, 0), (0, 1), (2, 1))
+    FIRST = 4
+    ROUTES = (
+        ((0, 1), (0, 0), (0, 1), None),
+        ((1, 0), (0, 0), (3, 0), None),
+        ((3, 0), (0, 0), (1, 0), None),
+        ((2, 0), (0, 0), (2, 0), None),
+        ((1, 0), (0, 1), (3, 1), None),
+        ((3, 0), (0, 1), (1, 1), None),
+        ((2, 0), (0, 1), (2, 1), None),
+    )
 
     def place(self, hop):
         d, t = places()
@@ -153,23 +203,11 @@
         d, t = places()
         return (d, tensor_at(t, hop))
 
-    def near(self):
+    def handover(self, j, src, block):
         d, t = places()
         return pltpu.make_async_remote_copy(
-            src_ref=self.src,
-            dst_ref=self.slot(t),
-            send_sem=self.sends.at[15],
-            recv_sem=self.recvs.at[14],
-            device_id=(d, other_core(t)),
-            device_id_type=MESH,
-        )
-
-    def handover(self, j, block):
-        d, t = places()
-        slot = self.slot(block)
-        return pltpu.make_async_remote_copy(
-            src_ref=slot,
-            dst_ref=slot,
+            src_ref=src,
+            dst_ref=self.slot(block),
             send_sem=self.sends.at[8 + j],
             recv_sem=self.recvs.at[7 + j],
             device_id=(d, other_core(t)),
@@ -177,29 +215,35 @@
         )
 
     def hand(self, j):
-        self.handover(j, self.place(self.routes[j][2])).start()
+        block = self.place(self.ROUTES[j][2])
+        return self.handover(j, self.slot(block), block)
+
+    def near(self):
+        return self.handover(7, self.src, self.place((0, 0)))
 
     def start(self):
         super().start()
         self.near().start()
 
+    def relay(self):
+        self.into(0).wait_recv()
+        for j in range(4, 7):
+            self.out(j).start()
+        self.hand(0).start()
+
     def finish(self):
-        super().finish()
+        for j in range(1, 7):
+            self.into(j).wait_recv()
+            self.hand(j).start()
+        self.sent()
         d, t = places()
         far = other_core(t)
-        slot = self.slot(far)
-        pltpu.make_async_remote_copy(
-            src_ref=slot,
-            dst_ref=slot,
-            send_sem=self.sends.at[15],
-            recv_sem=self.recvs.at[14],
-            device_id=(d, far),
-            device_id_type=MESH,
-        ).wait_recv()
+        self.handover(7, self.slot(far), far).wait_recv()
         self.near().wait_send()
         for j in range(7):
-            self.handover(j, tensor_at(far, self.routes[j][2])).wait_recv()
-            self.handover(j, self.place(self.routes[j][2])).wait_send()
+            block = tensor_at(far, self.ROUTES[j][2])
+            self.handover(j, self.slot(block), block).wait_recv()
+            self.hand(j).wait_send()
 
 
 class TensorSum:
@@ -209,14 +253,15 @@
     @staticmethod
     def scratch(columns):
         return [
-            pltpu.VMEM((8, 16, columns), BF16),
-            pltpu.VMEM((7, 16, columns), BF16),
-            pltpu.VMEM((7, 16, columns), BF16),
+            pltpu.VMEM((8, 8, columns), BF16),
+            pltpu.VMEM((7, 8, columns), BF16),
+            pltpu.VMEM((7, 8, columns), BF16),
             DMA((15,)),
             DMA((15,)),
         ]
 
-    def __init__(self, part, near, sent, far, sends, recvs):
+    def __init__(self, rows, part, near, sent, far, sends, recvs):
+        self.rows = rows
         self.part, self.near_, self.sent, self.far = part, near, sent, far
         self.sends, self.recvs = sends, recvs
 
@@ -225,7 +270,7 @@
         k = chip_at(t, self.BLOCKS[j])
         c = lax.rem(t, 2)
         return remote(
-            self.part.at[k, 1 - c], self.near_.at[k], self.sends, self.recvs, j, (d, other_core(t))
+            self.part.at[k, 1 - c, self.rows], self.near_.at[k], self.sends, self.recvs, j, (d, other_core(t))
         )
 
     def cross(self, j):
@@ -239,7 +284,7 @@
         d, t = places()
         k = chip_at(t, self.BLOCKS[j])
         c = lax.rem(t, 2)
-        return self.part[k, c].astype(F32) + self.near_[k].astype(F32)
+        return self.part[k, c, self.rows].astype(F32) + self.near_[k].astype(F32)
 
     def start(self):
         for j in range(8):
@@ -280,7 +325,7 @@
 
     def __init__(self, src, out, sends, recvs):
         self.src, self.out_, self.sends, self.recvs = src, out, sends, recvs
-        self.share = src.shape[1] // 8
+        self.share = src.shape[-1] // 8
 
     def columns(self, d):
         return pl.ds(pl.multiple_of(d * self.share, self.share), self.share)
@@ -289,7 +334,7 @@
         d, t = places()
         peer = data_at(d, HOPS[j])
         return remote(
-            self.src.at[:, self.columns(peer)],
+            self.src.at[:, :, self.columns(peer)],
             self.out_.at[d],
             self.sends,
             self.recvs,
@@ -305,7 +350,7 @@
     def own(self):
         d, t = places()
         return pltpu.make_async_copy(
-            self.src.at[:, self.columns(d)], self.out_.at[d], self.sends.at[7]
+            self.src.at[:, :, self.columns(d)], self.out_.at[d], self.sends.at[7]
         )
 
     def start(self):
@@ -373,12 +418,16 @@
         )
 
     def start(self):
-        for j in range(7):
+        for j in (3, 4, 5):
             self.cross(j).start()
         self.own().start()
 
+    def start_pairs(self):
+        for j in (6, 0, 1, 2):
+            self.cross(j).start()
+
     def finish(self):
-        for j in (6, 4, 5, 3, 0, 1, 2):
+        for j in (4, 5, 3, 6, 0, 1, 2):
             self.arrived(j).wait_recv()
             self.handed(j).start()
         for j in range(7):
@@ -396,7 +445,7 @@
     return out
 
 
-def comm_call(kernel, name, number, in_specs, out_specs, out_shape, scratch, args):
+def comm_call(kernel, name, number, in_specs, out_specs, out_shape, scratch, args, limit=24):
     return pl.pallas_call(
         kernel,
         name=name,
@@ -404,8 +453,9 @@
         out_specs=out_specs,
         out_shape=out_shape,
         scratch_shapes=scratch,
+        cost_estimate=pl.CostEstimate(flops=10**10, bytes_accessed=0, transcendentals=0),
         compiler_params=pltpu.CompilerParams(
-            collective_id=number, has_side_effects=True, vmem_limit_bytes=40 * 2**20
+            collective_id=number, has_side_effects=True, vmem_limit_bytes=limit * 2**20
         ),
     )(*args)
 
@@ -416,6 +466,10 @@
 
 def slot_of(ref):
     return lambda block: ref.at[block]
+
+
+def half_slot(ref, half):
+    return lambda block: ref.at[block, half]
 
 
 def columns_of(ref):
@@ -457,9 +511,11 @@
 
 class Probes:
     COUNT = 4
-    scratch = DataGather.scratch * 4 + CoreShare.scratch
-
-    def __init__(self, layer, probes, gathered, sems):
+    @staticmethod
+    def scratch(kind):
+        return kind.scratch * 4 + CoreShare.scratch
+
+    def __init__(self, kind, layer, probes, gathered, sems):
         q, k, v, o = probes
         gq, gkv, go = gathered
         d, t = places()
@@ -472,10 +528,10 @@
             ]
 
         self.jobs = [
-            DataGather(k.at[layer], part(0), *sems[0:2]),
-            DataGather(v.at[layer], part(1), *sems[2:4]),
-            DataGather(q.at[layer], slot_of(gq), *sems[4:6]),
-            DataGather(o.at[layer], columns_of(go), *sems[6:8]),
+            kind(k.at[layer], part(0), *sems[0:2]),
+            kind(v.at[layer], part(1), *sems[2:4]),
+            kind(q.at[layer], slot_of(gq), *sems[4:6]),
+            kind(o.at[layer], columns_of(go), *sems[6:8]),
         ]
         self.share = CoreShare(None, lambda j, c: gkv.at[strip(j, c)], *sems[8:10])
 
@@ -496,6 +552,10 @@
         for job in self.jobs:
             job.relay()
 
+    def pass_on(self):
+        for job in self.jobs:
+            job.pass_on()
+
     def finish(self):
         for job in self.jobs[:2]:
             job.finish()
@@ -505,29 +565,44 @@
         self.share.finish()
 
 
+def normed_kernel(tokens, gains, h_low):
+    wide = tokens[...].astype(F32)
+    inverse = lax.rsqrt(mean_of(wide * wide) + EPS)
+    h_low[...] = (wide * inverse * gains[0:1]).astype(BF16)
+
+
+def normed(tokens, gains):
+    return pl.pallas_call(
+        normed_kernel,
+        name="normed",
+        in_specs=[VMEM, VMEM],
+        out_specs=VMEM,
+        out_shape=shape(tokens.shape, BF16),
+        cost_estimate=pl.CostEstimate(flops=10**9, bytes_accessed=0, transcendentals=0),
+        compiler_params=pltpu.CompilerParams(vmem_limit_bytes=8 * 2**20),
+    )(tokens, gains)
+
+
 def first_kernel(*refs):
     (
-        (tokens, gains, q, k, v, o, kw, vw),
+        (h_low, q, k, v, o, kw, vw),
         (h_all, hs, gq, gkv, go, kv),
-        (h_low, mini),
+        (mini,),
         row_sems,
         spread_sems,
         slice_sems,
         share_sems,
         own_sems,
         probe_sems,
-    ) = taken(refs, 8, 6, 2, 2, 2, 2, 2, 1, 10)
+    ) = taken(refs, 7, 6, 1, 2, 2, 2, 2, 1, 10)
     d, t = places()
     core = lax.rem(t, 2)
-    wide = tokens[...].astype(F32)
-    inverse = lax.rsqrt(mean_of(wide * wide) + EPS)
-    h_low[...] = (wide * inverse * gains[0:1]).astype(BF16)
-    enter(True, True)
+    enter(HOPS)
     spread = DataSpread(h_low, mini, *spread_sems)
     rows = TensorGather(h_low, slot_of(h_all), *row_sems)
     slices = TensorGather(mini, lambda block: hs.at[:, block], *slice_sems)
     share = CoreShare((kw, vw), lambda j, c: kv.at[:, strip(j, c)], *share_sems)
-    probes = Probes(0, (q, k, v, o), (gq, gkv, go), probe_sems)
+    probes = Probes(LargeGather, 0, (q, k, v, o), (gq, gkv, go), probe_sems)
     own = [
         pltpu.make_async_copy(src, kv.at[:, strip(j, core)], own_sems[0].at[j])
         for j, src in enumerate((kw, vw))
@@ -544,6 +619,7 @@
     rows.finish()
     probes.relay()
     slices.relay()
+    probes.pass_on()
     slices.finish()
     share.finish()
     for copy in own:
@@ -551,25 +627,25 @@
     probes.finish()
 
 
-def first(tokens, gains, probes, kw, vw):
-    rows, width = tokens.shape
+def first(h_low, probes, kw, vw):
+    half, width = h_low.shape[1:]
     return comm_call(
         first_kernel,
         "first",
         1,
-        [VMEM, VMEM] + [HBM] * 6,
-        [VMEM] + [HBM] * 5,
-        [shape((16, rows, width), BF16), shape((8, 16, rows, width // 8), BF16)]
+        [VMEM] + [HBM] * 6,
+        [VMEM] + [ANY] * 5,
+        [shape((16, 2, half, width), BF16), shape((8, 16, 2, half, width // 8), BF16)]
         + Probes.shapes(probes)
         + [shape((2, 4 * kw.shape[1], width), BF16)],
-        [pltpu.VMEM((rows, width), BF16), pltpu.VMEM((8, rows, width // 8), BF16)]
+        [pltpu.VMEM((8, 2, half, width // 8), BF16)]
         + TensorGather.scratch
         + DataSpread.scratch
         + TensorGather.scratch
         + CoreShare.scratch
         + [DMA((2,))]
-        + Probes.scratch,
-        (tokens, gains) + probes + (kw, vw),
+        + Probes.scratch(LargeGather),
+        (h_low,) + probes + (kw, vw),
     )
 
 
@@ -578,67 +654,76 @@
         (primal, moved, tokens, gains, q, k, v, o),
         (x_out, t_out, h_all, th_all, gq, gkv, go),
         (h_low, th_low),
-        sum_a,
-        sum_b,
-        gather_a,
-        gather_b,
+        sum_refs,
+        gather_refs,
         sems,
-    ) = taken(refs, 8, 7, 2, 5, 5, 2, 2, 10)
+    ) = taken(refs, 8, 7, 2, 20, 8, 10)
     gain = gains[1:2]
-    enter(True, True)
-    sums = [TensorSum(primal, *sum_a), TensorSum(moved, *sum_b)]
-    probes = Probes(1, (q, k, v, o), (gq, gkv, go), sems)
+    enter(NEAR)
+    lots = taken(sum_refs, 5, 5, 5, 5)
+    primals = [TensorSum(r, primal, *lots[r]) for r in range(2)]
+    moves = [TensorSum(r, moved, *lots[2 + r]) for r in range(2)]
+    sums = [primals[0], moves[0], primals[1], moves[1]]
+    lots = taken(gather_refs, 2, 2, 2, 2)
+    rows_h = [TensorGather(h_low.at[r], half_slot(h_all, r), *lots[r]) for r in range(2)]
+    rows_th = [TensorGather(th_low.at[r], half_slot(th_all, r), *lots[2 + r]) for r in range(2)]
+    probes = Probes(DataGather, 1, (q, k, v, o), (gq, gkv, go), sems)
     for one in sums:
         one.start()
     for one in sums:
         one.send()
     probes.start()
-    for one in sums:
+    for one in sums[:2]:
         one.middle()
-    stream = (tokens[...].astype(F32) + sums[0].total()).astype(BF16)
-    x_out[...] = stream
-    wide = stream.astype(F32)
-    inverse = lax.rsqrt(mean_of(wide * wide) + EPS)
-    h_low[...] = (wide * inverse * gain).astype(BF16)
-    rows_a = TensorGather(h_low, slot_of(h_all), *gather_a)
-    rows_a.start()
-    tangent = sums[1].total()
-    t_out[...] = tangent
-    shift = mean_of(wide * tangent)
-    th_low[...] = (gain * (tangent * inverse - wide * inverse * inverse * inverse * shift)).astype(
-        BF16
-    )
-    rows_b = TensorGather(th_low, slot_of(th_all), *gather_b)
-    rows_b.start()
-    rows_a.relay()
+    for r in range(2):
+        stream = (tokens[r].astype(F32) + primals[r].total()).astype(BF16)
+        x_out[r] = stream
+        wide = stream.astype(F32)
+        inverse = lax.rsqrt(mean_of(wide * wide) + EPS)
+        h_low[r] = (wide * inverse * gain).astype(BF16)
+        rows_h[r].start()
+        tangent = moves[r].total()
+        t_out[r] = tangent
+        shift = mean_of(wide * tangent)
+        th_low[r] = (
+            gain * (tangent * inverse - wide * inverse * inverse * inverse * shift)
+        ).astype(BF16)
+        rows_th[r].start()
+        if r == 0:
+            for one in sums[2:]:
+                one.middle()
+            rows_h[0].relay()
+    rows_th[0].relay()
     probes.relay()
-    rows_b.relay()
+    rows_h[1].relay()
+    rows_th[1].relay()
+    probes.pass_on()
     for one in sums:
         one.finish()
-    rows_a.finish()
-    rows_b.finish()
+    for rows in rows_h + rows_th:
+        rows.finish()
     probes.finish()
 
 
 def between(primal, moved, tokens, gains, probes):
-    rows, width = tokens.shape
+    half, width = tokens.shape[1:]
     return comm_call(
         between_kernel,
         "between",
         2,
         [VMEM] * 4 + [HBM] * 4,
-        [VMEM] * 4 + [HBM] * 3,
+        [VMEM] * 4 + [ANY] * 3,
         [
-            shape((rows, width), BF16),
-            shape((rows, width), F32),
-            shape((16, rows, width), BF16),
-            shape((16, rows, width), BF16),
+            shape((2, half, width), BF16),
+            shape((2, half, width), F32),
+            shape((16, 2, half, width), BF16),
+            shape((16, 2, half, width), BF16),
         ]
         + Probes.shapes(probes),
-        [pltpu.VMEM((rows, width), BF16)] * 2
-        + TensorSum.scratch(width) * 2
-        + TensorGather.scratch * 2
-        + Probes.scratch,
+        [pltpu.VMEM((2, half, width), BF16)] * 2
+        + TensorSum.scratch(width) * 4
+        + TensorGather.scratch * 4
+        + Probes.scratch(DataGather),
         (primal, moved, tokens, gains) + probes,
     )
 
@@ -648,36 +733,47 @@
         (lengths, moved, t_one, a_zero, a_one, h_one),
         (c_out, cb_all, ga_zero, ga_one, hs_one),
         (c_low,),
-        sum_a,
-        gather_a,
+        sum_refs,
+        gather_refs,
         sems,
-    ) = taken(refs, 6, 5, 1, 5, 2, 6)
+    ) = taken(refs, 6, 5, 1, 10, 4, 6)
     d, t = places()
-    enter(True, True)
-    total = TensorSum(moved, *sum_a)
+    enter(HOPS)
+    lots = taken(sum_refs, 5, 5)
+    sums = [TensorSum(r, moved, *lots[r]) for r in range(2)]
+    lots = taken(gather_refs, 2, 2)
+    rows = [TensorGather(c_low.at[r], half_slot(cb_all, r), *lots[r]) for r in range(2)]
     jobs = [
         DataGather(a_zero, slot_of(ga_zero), *sems[0:2]),
         DataGather(a_one, slot_of(ga_one), *sems[2:4]),
     ]
     swap = DataExchange(h_one, hs_one, *sems[4:6])
-    total.start()
-    total.send()
+    for one in sums:
+        one.start()
+    for one in sums:
+        one.send()
     for job in jobs:
         job.start()
-    total.middle()
+    for one in sums:
+        one.middle()
     swap.start()
-    position = t * t_one.shape[0] + lax.broadcasted_iota(jnp.int32, t_one.shape, 0)
-    mask = jnp.where(position < lengths[d], 1.0, 0.0)
-    cotangent = mask * (t_one[...] + total.total())
-    c_out[...] = cotangent
-    c_low[...] = cotangent.astype(BF16)
-    rows = TensorGather(c_low, slot_of(cb_all), *gather_a)
-    rows.start()
+    half = t_one.shape[1]
+    for r in range(2):
+        position = (2 * t + r) * half + lax.broadcasted_iota(jnp.int32, t_one.shape[1:], 0)
+        mask = jnp.where(position < lengths[d], 1.0, 0.0)
+        cotangent = mask * (t_one[r] + sums[r].total())
+        c_out[r] = cotangent
+        c_low[r] = cotangent.astype(BF16)
+        rows[r].start()
+    swap.start_pairs()
+    for r in range(2):
+        rows[r].relay()
+        jobs[r].relay()
     for job in jobs:
-        job.relay()
-    rows.relay()
-    total.finish()
-    rows.finish()
+        job.pass_on()
+    for r in range(2):
+        sums[r].finish()
+        rows[r].finish()
     swap.finish()
     for job in jobs:
         job.finish()
@@ -687,23 +783,23 @@
 
 
 def turn(lengths, moved, t_one, a_zero, a_one, h_one):
-    rows, width = t_one.shape
+    half, width = t_one.shape[1:]
     return comm_call(
         turn_kernel,
         "turn",
         3,
-        [SMEM] + [VMEM] * 2 + [HBM] * 3,
-        [VMEM] * 2 + [HBM] * 3,
+        [SMEM] + [VMEM] * 2 + [ANY] * 3,
+        [VMEM] * 2 + [ANY] * 3,
         [
-            shape((rows, width), F32),
-            shape((16, rows, width), BF16),
+            shape((2, half, width), F32),
+            shape((16, 2, half, width), BF16),
             shape((8,) + a_zero.shape, BF16),
             shape((8,) + a_one.shape, BF16),
             shape((8, h_one.shape[0], h_one.shape[1] // 8), BF16),
         ],
-        [pltpu.VMEM((rows, width), BF16)]
-        + TensorSum.scratch(width)
-        + TensorGather.scratch
+        [pltpu.VMEM((2, half, width), BF16)]
+        + TensorSum.scratch(width) * 2
+        + TensorGather.scratch * 2
         + DataGather.scratch * 2
         + DataExchange.scratch,
         (lengths, moved, t_one, a_zero, a_one, h_one),
@@ -745,7 +841,6 @@
 
     def start(self):
         d, t = places()
-        self.swap().start()
         self.jobs[0].start()
         self.swap().wait()
         mine = self.gkv[lax.rem(t, 2)].astype(F32) + self.came[...].astype(F32)
@@ -756,6 +851,10 @@
         for job in self.jobs:
             job.relay()
 
+    def pass_on(self):
+        for job in self.jobs:
+            job.pass_on()
+
     def finish(self):
         for job in self.jobs:
             job.finish()
@@ -766,58 +865,69 @@
         (part, c_two, x_one, gains, gkv, gq, cb_one),
         (cb_all, gg, cbs, mini),
         (c_low,),
-        sum_a,
-        gather_a,
+        sum_refs,
+        gather_refs,
         (came, merged),
         sems,
         swap_sems,
         spread_sems,
-    ) = taken(refs, 7, 4, 1, 5, 2, 2, 6, 2, 2)
-    enter(True, True)
-    total = TensorSum(part, *sum_a)
+    ) = taken(refs, 7, 4, 1, 10, 4, 2, 6, 2, 2)
+    enter(HOPS)
+    lots = taken(sum_refs, 5, 5)
+    sums = [TensorSum(r, part, *lots[r]) for r in range(2)]
+    lots = taken(gather_refs, 2, 2)
+    rows = [TensorGather(c_low.at[r], half_slot(cb_all, r), *lots[r]) for r in range(2)]
     jobs = Cotangents(gq, gkv, gg, came, merged, sems)
     swap = DataExchange(cb_one, cbs, *swap_sems)
-    total.start()
-    total.send()
+    jobs.swap().start()
+    for one in sums:
+        one.start()
+    for one in sums:
+        one.send()
     jobs.start()
-    total.middle()
+    for one in sums:
+        one.middle()
     swap.start()
-    scaled = total.total() * gains[1:2]
-    wide = x_one[...].astype(F32)
-    inverse = lax.rsqrt(mean_of(wide * wide) + EPS)
-    shift = mean_of(wide * scaled)
-    cotangent = c_two[...] + inverse * (scaled - wide * inverse * inverse * shift)
-    c_low[...] = cotangent.astype(BF16)
-    rows = TensorGather(c_low, slot_of(cb_all), *gather_a)
+    for r in range(2):
+        scaled = sums[r].total() * gains[1:2]
+        wide = x_one[r].astype(F32)
+        inverse = lax.rsqrt(mean_of(wide * wide) + EPS)
+        shift = mean_of(wide * scaled)
+        cotangent = c_two[r] + inverse * (scaled - wide * inverse * inverse * shift)
+        c_low[r] = cotangent.astype(BF16)
+        rows[r].start()
     spread = DataSpread(c_low, mini, *spread_sems)
-    rows.start()
     spread.start()
+    swap.start_pairs()
+    for one in rows:
+        one.relay()
     jobs.relay()
-    rows.relay()
-    total.finish()
-    rows.finish()
+    jobs.pass_on()
+    for r in range(2):
+        sums[r].finish()
+        rows[r].finish()
     swap.finish()
     spread.finish()
     jobs.finish()
 
 
 def lower(part, c_two, x_one, gains, gkv, gq, cb_one):
-    rows, width = c_two.shape
+    half, width = c_two.shape[1:]
     return comm_call(
         lower_kernel,
         "lower",
         4,
-        [VMEM] * 5 + [HBM] * 2,
-        [VMEM] + [HBM] * 3,
+        [VMEM] * 5 + [ANY] * 2,
+        [VMEM] + [ANY] * 3,
         [
-            shape((16, rows, width), BF16),
+            shape((16, 2, half, width), BF16),
             shape((8, gq.shape[0], gq.shape[1] + gkv.shape[2]), BF16),
             shape((8, cb_one.shape[0], width // 8), BF16),
-            shape((8, rows, width // 8), BF16),
+            shape((8, 2, half, width // 8), BF16),
         ],
-        [pltpu.VMEM((rows, width), BF16)]
-        + TensorSum.scratch(width)
-        + TensorGather.scratch
+        [pltpu.VMEM((2, half, width), BF16)]
+        + TensorSum.scratch(width) * 2
+        + TensorGather.scratch * 2
         + Cotangents.scratch(gkv)
         + DataExchange.scratch
         + DataSpread.scratch,
@@ -827,13 +937,15 @@
 
 def last_kernel(*refs):
     (gkv, mini, gq), (gg, cbs), (came, merged), sems, slice_sems = taken(refs, 3, 2, 2, 6, 2)
-    enter(True, True)
+    enter(NEAR)
     slices = TensorGather(mini, lambda block: cbs.at[:, block], *slice_sems)
     jobs = Cotangents(gq, gkv, gg, came, merged, sems)
+    jobs.swap().start()
     slices.start()
     jobs.start()
     slices.relay()
     jobs.relay()
+    jobs.pass_on()
     slices.finish()
     jobs.finish()
 
@@ -843,8 +955,8 @@
         last_kernel,
         "last",
         5,
-        [VMEM] * 2 + [HBM],
-        [HBM] * 2,
+        [VMEM] * 2 + [ANY],
+        [ANY] * 2,
         [
             shape((8, gq.shape[0], gq.shape[1] + gkv.shape[2]), BF16),
             shape((8, 16) + mini.shape[1:], BF16),
@@ -1002,7 +1114,7 @@
             pltpu.VMEM((rows, 2 * HD), F32),
             pltpu.VMEM((rows, columns), BF16),
         ],
-        compiler_params=pltpu.CompilerParams(vmem_limit_bytes=40 * 2**20),
+        compiler_params=pltpu.CompilerParams(vmem_limit_bytes=20 * 2**20),
     )(*args)
 
 
@@ -1108,33 +1220,37 @@
             pltpu.VMEM((rows, columns), F32),
             pltpu.VMEM((rows, 2 * HD), BF16),
         ],
-        compiler_params=pltpu.CompilerParams(vmem_limit_bytes=40 * 2**20),
+        compiler_params=pltpu.CompilerParams(vmem_limit_bytes=20 * 2**20),
     )(*args)
 
 
 def products_kernel(*refs):
-    sides, (q_out, k_out, v_out, o_out) = taken(refs, 8, 4)
+    sides, (q_out, k_out, v_out, o_out), (q_sum,) = taken(refs, 8, 4, 1)
     i = pl.program_id(0)
     columns, half = q_out.shape[2], k_out.shape[1]
     for layer in range(2):
         hs, gg, ga, cs = [ref[...].reshape(-1, ref.shape[-1]) for ref in sides[4 * layer :][:4]]
-        q = contract(hs, gg[:, 0:columns], 0, 0)
-        kv = contract(gg[:, columns:], hs, 0, 0)
+        g = contract(gg, hs, 0, 0)
         o = contract(ga, cs, 0, 0)
 
         @pl.when(i == 0)
         def _():
-            q_out[layer] = q
-            k_out[layer] = kv[0:half]
-            v_out[layer] = kv[half:]
+            q_sum[layer] = g[0:columns]
+            k_out[layer] = g[columns : columns + half]
+            v_out[layer] = g[columns + half :]
             o_out[layer] = o
 
         @pl.when(i > 0)
         def _():
-            q_out[layer] += q
-            k_out[layer] += kv[0:half]
-            v_out[layer] += kv[half:]
+            q_sum[layer] += g[0:columns]
+            k_out[layer] += g[columns : columns + half]
+            v_out[layer] += g[columns + half :]
             o_out[layer] += o
+
+    @pl.when(i == pl.num_programs(0) - 1)
+    def _():
+        for layer in range(2):
+            q_out[layer] = q_sum[layer].T
 
 
 def products(*sides):
@@ -1156,7 +1272,8 @@
         ],
         out_specs=[whole(out.shape) for out in out_shape],
         out_shape=out_shape,
-        compiler_params=pltpu.CompilerParams(vmem_limit_bytes=40 * 2**20),
+        scratch_shapes=[pltpu.VMEM((2, columns, share), F32)],
+        compiler_params=pltpu.CompilerParams(vmem_limit_bytes=20 * 2**20),
     )(*sides)
 
 
@@ -1188,8 +1305,10 @@
     def turned_over(array):
         return jnp.swapaxes(array, 1, 2)
 
+    tokens = tokens.reshape(2, rows // 2, width)
+
     def by_owner(part):
-        return part.reshape(8, 2, rows, width)
+        return part.reshape(8, 2, 2, rows // 2, width)
 
     def all_rows(blocks):
         return blocks.reshape(-1, blocks.shape[-1])
@@ -1199,7 +1318,7 @@
 
     probes = (query_probe, turned_over(key_probe), turned_over(value_probe), out_probe)
     h_zero, hs_zero, pq, pkv, po, kv = first(
-        tokens, gains, probes, turned_over(key_weight), turned_over(value_weight)
+        normed(tokens, gains), probes, turned_over(key_weight), turned_over(value_weight)
     )
     q0, k0, v0, a_zero, moved, primal = forward(
         0, lengths, tables, query_weight, kv, all_rows(pq), pkv, out_weight, po, all_rows(h_zero)

time: 276 us -> 245 us (0.89)
  Pallas kernels: 261 us -> 241 us
  local copies, waits for them, and re-layouts: 13.4 us -> 2.63 us
    pallas_call x5, Pallas kernels: 222 us -> 207 us  [comm_call(): pl.pallas_call(kernel, name=name, in_specs=in_specs, out_specs=out_specs,...]
    unnamed x46 -> x30, local copies, waits for them, and re-layouts: 13.4 us -> 2.63 us
    pallas_call x2, Pallas kernels: 21.2 us -> 17.6 us  [forward(): pl.pallas_call(functools.partial(forward_kernel, steps, second), name=f'f...]
where the time goes in v3:
time: 245 us
  Pallas kernels  241 us (98%)
  local copies, waits for them, and re-layouts  2.63 us (1%)
    pallas_call x5, Pallas kernels, comm_call(): pl.pallas_call(kernel, name=name, in_specs=in_specs, out_specs=out_specs,...  207 us
    pallas_call x2, Pallas kernels, forward(): pl.pallas_call(functools.partial(forward_kernel, steps, second), name=f'f...  17.6 us
    pallas_call x2, Pallas kernels, backward(): pl.pallas_call(functools.partial(backward_kernel, steps, lowest), name=f'...  9.29 us
    pallas_call x1, Pallas kernels, products(): pl.pallas_call(products_kernel, name='products', grid=(8 // chunk,), in_s...  7.08 us

profile of v3, /device:TPU:1, one launch (start us, length us, event | category | flops | bytes accessed | tf_op | source)
XLA Modules:
  0.0 245.0 jit_solution(5249986028416331289)
XLA Ops:
  0.6 0.0 copy-start.8
  0.6 0.0 copy-start.7
  0.7 0.0 copy-start.6
  0.7 0.0 copy-start.5
  0.7 0.0 copy-start.9
  0.7 1.0 copy-done.9
  1.7 0.0 copy-start.13
  1.7 0.8 copy-done.13
  2.5 0.0 copy-start.11
  2.5 0.0 copy-start.12
  2.5 0.1 normed.1.refs_0_
  2.6 0.0 copy-done.8
  2.7 0.0 copy-done.7
  2.7 0.0 copy-done.6
  2.7 0.0 copy-done.5
  2.7 0.7 copy-done.11
  3.4 0.0 copy-done.12
  3.5 0.0 copy-start
  3.5 0.0 copy-start.1
  3.5 0.0 copy-start.2
  3.5 0.0 copy-start.3
  3.5 0.0 copy-start.4
  3.5 50.7 %first.1 = (bf16[16,2,8,4096]{3,2,1,0:T(8,128)(2,1)S(1)}, bf16[8,16,2,8,512]{4,3,2,1,0:T(8,128)(2,1)S(1)}, bf16[8,512,256]{2,1,0:T(8,128)(2,1)S(1)}, bf16[256,40...) custom-call(bf16[2,8,4096]{2,1,0:T(8,128)(2,1)S(1)} %normed.1.refs_0_, ...), custom_call_target="tpu_custom_call" | custom-call | flops 10000000000 | tf_op jit(solution)/shard_map/first/pallas_call | solution.py:449
  54.2 0.0 copy-done
  54.2 0.0 copy-done.1
  54.2 0.0 copy-done.2
  54.2 0.0 copy-done.3
  54.2 0.0 copy-done.4
  54.2 0.0 copy-start.10
  54.2 0.0 copy-start.14
  54.2 8.5 %forward_0.1 = (bf16[256,256]{1,0:T(8,128)(2,1)S(1)}, bf16[256,128]{1,0:T(8,128)(2,1)S(1)}, bf16[256,128]{1,0:T(8,128)(2,1)S(1)}, bf16[256,256]{1,0:T(8,128)(2,1...) custom-call(s32[8]{0:T(128)S(1)} %copy-done.4, f32[256,128]{1,0:T(8,128)S(1)} %copy-done.3, ...), custom_call_target="tpu_custom_call" | custom-call | tf_op jit(solution)/shard_map/forward_0/pallas_call | solution.py:1103
  62.8 0.0 copy-done.10
  62.8 0.0 copy-done.14
  62.8 57.1 %between.1 = (bf16[2,8,4096]{2,1,0:T(8,128)(2,1)S(1)}, f32[2,8,4096]{2,1,0:T(8,128)S(1)}, bf16[16,2,8,4096]{3,2,1,0:T(8,128)(2,1)S(1)}, bf16[16,2,8,4096]{3,2,1,...) custom-call(bf16[8,2,2,8,4096]{4,3,2,1,0:T(8,128)(2,1)S(1)} %bitcast, ...), custom_call_target="tpu_custom_call" | custom-call | flops 10000000000 | tf_op jit(solution)/shard_map/between/pallas_call | solution.py:449
  119.9 9.0 %forward_1.1 = (bf16[256,256]{1,0:T(8,128)(2,1)S(1)}, bf16[256,128]{1,0:T(8,128)(2,1)S(1)}, bf16[256,128]{1,0:T(8,128)(2,1)S(1)}, bf16[256,256]{1,0:T(8,128)(2,1)S(1)}, bf16[256,4096]{1,0:T(8,128)(2,1)S(1)}) custom-call(s32[8]{0:T(128)S(1)} %copy-done.4, f32[256,128]{1,0:T(8,128)S(1)} %copy-done.3, f32[256,128]{1,0:T(8,128)S(1)} %copy-done.2, ...), custom_call_target="tpu_custom_call" | custom-call | tf_op jit(solution)/shard_map/forward_1/pallas_call | solution.py:1103
  128.9 38.5 %turn.1 = (f32[2,8,4096]{2,1,0:T(8,128)S(1)}, bf16[16,2,8,4096]{3,2,1,0:T(8,128)(2,1)S(1)}, bf16[8,256,256]{2,1,0:T(8,128)(2,1)S(1)}, bf16[8,256,256]{2,1,0:T(8,128)(2,1)S(1)}, bf16[8,256,512]{2,1,0:T(8,128)(2,1)S(1)}) custom-call(s32[8]{0:T(128)S(1)} %copy-done.4, bf16[8,2,2,8,4096]{4,3,2,1,0:T(8,128)(2,1)S(1)} %bitcast.33, ...), custom_call_target="tpu_custom_call" | custom-call | flops 10000000000 | tf_op jit(solution)/shard_map/turn/pallas_call | solution.py:449
  167.4 5.9 %backward_1.1 = (bf16[256,256]{1,0:T(8,128)(2,1)S(1)}, bf16[2,256,128]{2,1,0:T(8,128)(2,1)S(1)}, bf16[256,4096]{1,0:T(8,128)(2,1)S(1)}) custom-call(s32[8]{0:T(128)S(1)} %copy-done.4, f32[256,128]{1,0:T(8,128)S(1)} %copy-done.3, f32[256,128]{1,0:T(8,128)S(1)} %copy-done.2, bf16[256,256]{1,0:T(8,128)(2,1)S(1)} %get-tuple-element.64.refs_3_, ...), custom_call_target="tpu_custom_call" | custom-call | tf_op jit(solution)/shard_map/backward_1/pallas_call | solution.py:1212
  173.3 43.1 %lower.1 = (bf16[16,2,8,4096]{3,2,1,0:T(8,128)(2,1)S(1)}, bf16[8,256,384]{2,1,0:T(8,128)(2,1)S(1)}, bf16[8,256,512]{2,1,0:T(8,128)(2,1)S(1)}, bf16[8,2,8,512]{3,2,1,0:T(8,128)(2,1)S(1)}) custom-call(bf16[8,2,2,8,4096]{4,3,2,1,0:T(8,128)(2,1)S(1)} %bitcast.34, f32[2,8,4096]{2,1,0:T(8,128)S(1)} %get-tuple-element.73.refs_1_, ...), custom_call_target="tpu_custom_call" | custom-call | flops 10000000000 | tf_op jit(solution)/shard_map/lower/pallas_call | solution.py:449
  216.5 3.4 %backward_0.1 = (bf16[256,256]{1,0:T(8,128)(2,1)S(1)}, bf16[2,256,128]{2,1,0:T(8,128)(2,1)S(1)}) custom-call(s32[8]{0:T(128)S(1)} %copy-done.4, f32[256,128]{1,0:T(8,128)S(1)} %copy-done.3, f32[256,128]{1,0:T(8,128)S(1)} %copy-done.2, bf16[256,256]{1,0:T(8,128)(2,1)S(1)} %get-tuple-element.54.refs_3_, bf16[256,128]{1,0:T(8,128)(2,1)S(1)} %get-tuple-element.55.refs_4_, ...), custom_call_target="tpu_custom_call" | custom-call | tf_op jit(solution)/shard_map/backward_0/pallas_call | solution.py:1212
  219.9 18.0 %last.1 = (bf16[8,256,384]{2,1,0:T(8,128)(2,1)S(1)}, bf16[8,16,2,8,512]{4,3,2,1,0:T(8,128)(2,1)S(1)}) custom-call(bf16[2,256,128]{2,1,0:T(8,128)(2,1)S(1)} %get-tuple-element.78.refs_0_, bf16[8,2,8,512]{3,2,1,0:T(8,128)(2,1)S(1)} %get-tuple-element.79.refs_1_, bf16[256,256]{1,0:T(8,128)(2,1)S(1)} %get-tuple-element.80.refs_2_), custom_call_target="tpu_custom_call" | custom-call | flops 10000000000 | tf_op jit(solution)/shard_map/last/pallas_call | solution.py:449
  237.9 7.1 %products.1 = (f32[2,512,256]{2,1,0:T(8,128)}, f32[2,64,512]{2,1,0:T(8,128)}, f32[2,64,512]{2,1,0:T(8,128)}, f32[2,256,512]{2,1,0:T(8,128)}) custom-call(bf16[8,256,512]{2,1,0:T(8,128)(2,1)S(1)} %bitcast.27, bf16[8,256,384]{2,1,0:T(8,128)(2,1)S(1)} %get-tuple-element.81.refs_1_, bf16[8,256,256]{2,1,0:T(8,128)(2,1)S(1)} %get-tuple-element.82.refs_2_, ...), custom_call_target="tpu_custom_call" | custom-call | tf_op jit(solution)/shard_map/products/pallas_call | solution.py:1266
Async XLA Ops:
  0.6 2.0 copy-start.8
  0.6 2.0 copy-start.7
  0.7 2.0 copy-start.6
  0.7 2.0 copy-start.5
  0.7 1.1 copy-start.9
  1.7 0.8 copy-start.13
  2.5 0.9 copy-start.11
  2.5 1.0 copy-start.12
  3.5 50.7 %copy-start = (bf16[2,256,4096]{2,1,0:T(8,128)(2,1)S(1)}, bf16[2,256,4096]{2,1,0:T(8,128)(2,1)}, u32[]{:S(2)}) copy-start(bf16[2,256,4096]{2,1,0:T(8,128)(2,1)} %refs_7_.9) | copy-start | bytes 12582916
  3.5 50.7 %copy-start.1 = (bf16[2,4096,256]{2,1,0:T(8,128)(2,1)S(1)}, bf16[2,4096,256]{2,1,0:T(8,128)(2,1)}, u32[]{:S(2)}) copy-start(bf16[2,4096,256]{2,1,0:T(8,128)(2,1)} %refs_8_.1) | copy-start | bytes 12582916
  3.5 50.7 %copy-start.2 = (f32[256,128]{1,0:T(8,128)S(1)}, f32[256,128]{1,0:T(8,128)}, u32[]{:S(2)}) copy-start(f32[256,128]{1,0:T(8,128)} %constant.5.clone.refs_2_) | copy-start | bytes 393220
  3.5 50.7 %copy-start.3 = (f32[256,128]{1,0:T(8,128)S(1)}, f32[256,128]{1,0:T(8,128)}, u32[]{:S(2)}) copy-start(f32[256,128]{1,0:T(8,128)} %constant.4.clone.refs_1_) | copy-start | bytes 393220
  3.5 50.7 %copy-start.4 = (s32[8]{0:T(128)S(1)}, s32[8]{0:T(128)}, u32[]{:S(2)}) copy-start(s32[8]{0:T(128)} %refs_0_.9) | copy-start | bytes 100
  54.2 8.6 %copy-start.10 = (bf16[16,4096]{1,0:T(8,128)(2,1)S(1)}, bf16[16,4096]{1,0:T(8,128)(2,1)}, u32[]{:S(2)}) copy-start(bf16[16,4096]{1,0:T(8,128)(2,1)} %param.13) | copy-start | bytes 393220
  54.2 8.6 %copy-start.14 = (f32[2,4096]{1,0:T(2,128)S(1)}, f32[2,4096]{1,0:T(2,128)}, u32[]{:S(2)}) copy-start(f32[2,4096]{1,0:T(2,128)} %refs_3_.7) | copy-start | bytes 98308

commit v4 on v3

--- a/solution.py
+++ b/solution.py
@@ -20,7 +20,9 @@
 VMEM = pl.BlockSpec(memory_space=pltpu.VMEM)
 ANY = pl.BlockSpec(memory_space=pl.ANY)
 HBM = pl.BlockSpec(memory_space=pltpu.HBM)
+SMEM = pl.BlockSpec(memory_space=pltpu.SMEM)
 DMA = pltpu.SemaphoreType.DMA
+TILE = 1024
 
 HOPS = ((1, 1), (3, 1), (2, 1), (2, 0), (1, 0), (3, 0), (0, 1))
 NEAR = HOPS[3:]
@@ -445,7 +447,7 @@
     return out
 
 
-def comm_call(kernel, name, number, in_specs, out_specs, out_shape, scratch, args, limit=24):
+def comm_call(kernel, name, number, in_specs, out_specs, out_shape, scratch, args, limit=12):
     return pl.pallas_call(
         kernel,
         name=name,
@@ -563,6 +565,93 @@
         for job in self.jobs[2:]:
             job.finish()
         self.share.finish()
+
+
+def contract(left_side, right_side, left_dim, right_dim):
+    return lax.dot_general(
+        left_side,
+        right_side,
+        (((left_dim,), (right_dim,)), ((), ())),
+        preferred_element_type=F32,
+    )
+
+
+def turned(values, cosine, sine):
+    return values * cosine + pltpu.roll(values, values.shape[1] // 2, 1) * sine
+
+
+def attention_weights(q, k, length):
+    size = q.shape[0]
+    row = lax.broadcasted_iota(jnp.int32, (size, size), 0)
+    column = lax.broadcasted_iota(jnp.int32, (size, size), 1)
+    allowed = (column <= row) & (column < length)
+    scores = contract(q, k, 1, 1) * (1.0 / math.sqrt(q.shape[1]))
+    powers = jnp.where(allowed, jnp.exp(scores), 0.0)
+    return powers / jnp.sum(powers, axis=-1, keepdims=True)
+
+
+def attend(length, cos, sin, sums, q_out, k_out, v_out, a_out, ta_out):
+    q_sum, tq_sum, kv_sum, tkv_sum = sums
+    scaling = 1.0 / math.sqrt(HD)
+    k = turned(kv_sum[:, 0:HD], cos, sin).astype(BF16)
+    v = kv_sum[:, HD:].astype(BF16)
+    tk = turned(tkv_sum[:, 0:HD], cos, sin).astype(BF16)
+    tv = tkv_sum[:, HD:].astype(BF16)
+    k_out[...] = k
+    v_out[...] = v
+    for at in range(0, q_sum.shape[1], HD):
+        head = slice(at, at + HD)
+        q = turned(q_sum[:, head], cos, sin).astype(BF16)
+        tq = turned(tq_sum[:, head], cos, sin).astype(BF16)
+        q_out[:, head] = q
+        weights = attention_weights(q, k, length)
+        low = weights.astype(BF16)
+        a_out[:, head] = contract(low, v, 1, 0).astype(BF16)
+        scores = (contract(tq, k, 1, 1) + contract(q, tk, 1, 1)) * scaling
+        change = weights * (scores - jnp.sum(weights * scores, axis=-1, keepdims=True))
+        ta = contract(change.astype(BF16), v, 1, 0) + contract(low, tv, 1, 0)
+        ta_out[:, head] = ta.astype(BF16)
+
+
+def attend_back(length, cos, sin, q_in, k, v, ga_sum, gq_out, gkv_out, gkv_low):
+    scaling = 1.0 / math.sqrt(HD)
+    gk, gv = None, None
+    for at in range(0, ga_sum.shape[1], HD):
+        head = slice(at, at + HD)
+        q = q_in[:, head]
+        ga = ga_sum[:, head].astype(BF16)
+        weights = attention_weights(q, k, length)
+        grads = contract(ga, v, 1, 1)
+        value = contract(weights.astype(BF16), ga, 0, 0)
+        scores = (
+            weights * (grads - jnp.sum(weights * grads, axis=-1, keepdims=True)) * scaling
+        ).astype(BF16)
+        gq_out[:, head] = turned(contract(scores, k, 1, 0), cos, -sin).astype(BF16)
+        key = contract(scores, q, 0, 0)
+        gk = key if gk is None else gk + key
+        gv = value if gv is None else gv + value
+    gk = turned(gk, cos, -sin).astype(BF16)
+    gv = gv.astype(BF16)
+    half = HD // 2
+    if gkv_low is not None:
+        gkv_low[:, 0:HD] = gk
+        gkv_low[:, HD:] = gv
+    gkv_out[0] = jnp.concatenate([gk[:, 0:half], gv[:, 0:half]], axis=-1)
+    gkv_out[1] = jnp.concatenate([gk[:, half:], gv[:, half:]], axis=-1)
+
+
+def tiles(width, size):
+    def over(function):
+        @pl.loop(0, width // size)
+        def _(i):
+            function(pl.ds(pl.multiple_of(i * size, size), size))
+
+    return over
+
+
+def store_by_owner(part, columns, values):
+    dims = part.shape[:-1] + (values.shape[1],)
+    part[:, :, :, :, columns] = values.reshape(dims).astype(BF16)
 
 
 def normed_kernel(tokens, gains, h_low):
@@ -651,13 +740,16 @@
 
 def between_kernel(*refs):
     (
-        (primal, moved, tokens, gains, q, k, v, o),
-        (x_out, t_out, h_all, th_all, gq, gkv, go),
-        (h_low, th_low),
+        (lengths, cosine, sine, wq, kv, pq, pkv, wo, po, h_zero, tokens, gains, q, k, v, o),
+        (q_out, k_out, v_out, a_out, x_out, t_out, h_all, th_all, gq, gkv, go),
+        (ta_low, primal, moved, h_low, th_low),
+        sums_f32,
         sum_refs,
         gather_refs,
         sems,
-    ) = taken(refs, 8, 7, 2, 20, 8, 10)
+    ) = taken(refs, 16, 11, 5, 4, 20, 8, 10)
+    d, t = places()
+    width = h_zero.shape[1]
     gain = gains[1:2]
     enter(NEAR)
     lots = taken(sum_refs, 5, 5, 5, 5)
@@ -668,13 +760,39 @@
     rows_h = [TensorGather(h_low.at[r], half_slot(h_all, r), *lots[r]) for r in range(2)]
     rows_th = [TensorGather(th_low.at[r], half_slot(th_all, r), *lots[2 + r]) for r in range(2)]
     probes = Probes(DataGather, 1, (q, k, v, o), (gq, gkv, go), sems)
+    probes.start()
+    q_sum, tq_sum, kv_sum, tkv_sum = sums_f32
+    for one in sums_f32:
+        one[...] = jnp.zeros_like(one)
+
+    @tiles(width, TILE)
+    def _(at):
+        h = h_zero[:, at]
+        q_sum[...] += contract(h, wq[0, at], 1, 0)
+        kv_sum[...] += contract(h, kv[0, :, at], 1, 1)
+        tq_sum[...] += contract(h, pq[at], 1, 0)
+        tkv_sum[...] += contract(h, pkv[:, at], 1, 1)
+
+    attend(lengths[d], cosine[...], sine[...], sums_f32, q_out, k_out, v_out, a_out, ta_low)
+
+    @tiles(width, TILE)
+    def _(at):
+        w = wo[0, :, at]
+        store_by_owner(primal, at, contract(a_out[...], w, 1, 0))
+        store_by_owner(
+            moved, at, contract(ta_low[...], w, 1, 0) + contract(a_out[...], po[:, at], 1, 0)
+        )
+
     for one in sums:
         one.start()
+    for job in probes.jobs[:2]:
+        job.relay()
     for one in sums:
         one.send()
-    probes.start()
     for one in sums[:2]:
         one.middle()
+    for job in probes.jobs[2:]:
+        job.relay()
     for r in range(2):
         stream = (tokens[r].astype(F32) + primals[r].total()).astype(BF16)
         x_out[r] = stream
@@ -694,7 +812,6 @@
                 one.middle()
             rows_h[0].relay()
     rows_th[0].relay()
-    probes.relay()
     rows_h[1].relay()
     rows_th[1].relay()
     probes.pass_on()
@@ -705,42 +822,60 @@
     probes.finish()
 
 
-def between(primal, moved, tokens, gains, probes):
+def between(lengths, tables, wq, kv, pq, pkv, wo, po, h_zero, tokens, gains, probes):
     half, width = tokens.shape[1:]
+    length, columns = h_zero.shape[0], wq.shape[2]
     return comm_call(
         between_kernel,
         "between",
         2,
-        [VMEM] * 4 + [HBM] * 4,
-        [VMEM] * 4 + [ANY] * 3,
+        [SMEM] + [VMEM] * 11 + [HBM] * 4,
+        [VMEM] * 8 + [ANY] * 3,
         [
+            shape((length, columns), BF16),
+            shape((length, HD), BF16),
+            shape((length, HD), BF16),
+            shape((length, columns), BF16),
             shape((2, half, width), BF16),
             shape((2, half, width), F32),
             shape((16, 2, half, width), BF16),
             shape((16, 2, half, width), BF16),
         ]
         + Probes.shapes(probes),
-        [pltpu.VMEM((2, half, width), BF16)] * 2
+        [
+            pltpu.VMEM((length, columns), BF16),
+            pltpu.VMEM((8, 2, 2, half, width), BF16),
+            pltpu.VMEM((8, 2, 2, half, width), BF16),
+            pltpu.VMEM((2, half, width), BF16),
+            pltpu.VMEM((2, half, width), BF16),
+            pltpu.VMEM((length, columns), F32),
+            pltpu.VMEM((length, columns), F32),
+            pltpu.VMEM((length, 2 * HD), F32),
+            pltpu.VMEM((length, 2 * HD), F32),
+        ]
         + TensorSum.scratch(width) * 4
         + TensorGather.scratch * 4
         + Probes.scratch(DataGather),
-        (primal, moved, tokens, gains) + probes,
+        (lengths,) + tables + (wq, kv, pq, pkv, wo, po, h_zero, tokens, gains) + probes,
+        limit=16,
     )
 
 
 def turn_kernel(*refs):
     (
-        (lengths, moved, t_one, a_zero, a_one, h_one),
-        (c_out, cb_all, ga_zero, ga_one, hs_one),
-        (c_low,),
+        (lengths, cosine, sine, wq, kv, pq, pkv, wo, po, h_one, th_one, t_one, a_zero),
+        (q_out, k_out, v_out, c_out, cb_all, ga_zero, ga_one, hs_one),
+        (a_one, ta_low, part, c_low),
+        sums_f32,
         sum_refs,
         gather_refs,
         sems,
-    ) = taken(refs, 6, 5, 1, 10, 4, 6)
+    ) = taken(refs, 13, 8, 4, 4, 10, 4, 6)
     d, t = places()
+    width = h_one.shape[1]
     enter(HOPS)
     lots = taken(sum_refs, 5, 5)
-    sums = [TensorSum(r, moved, *lots[r]) for r in range(2)]
+    sums = [TensorSum(r, part, *lots[r]) for r in range(2)]
     lots = taken(gather_refs, 2, 2)
     rows = [TensorGather(c_low.at[r], half_slot(cb_all, r), *lots[r]) for r in range(2)]
     jobs = [
@@ -748,15 +883,37 @@
         DataGather(a_one, slot_of(ga_one), *sems[2:4]),
     ]
     swap = DataExchange(h_one, hs_one, *sems[4:6])
+    jobs[0].start()
+    swap.start()
+    swap.start_pairs()
+    q_sum, tq_sum, kv_sum, tkv_sum = sums_f32
+    for one in sums_f32:
+        one[...] = jnp.zeros_like(one)
+
+    @tiles(width, TILE)
+    def _(at):
+        h, th = h_one[:, at], th_one[:, at]
+        w, k = wq[1, at], kv[1, :, at]
+        q_sum[...] += contract(h, w, 1, 0)
+        kv_sum[...] += contract(h, k, 1, 1)
+        tq_sum[...] += contract(h, pq[at], 1, 0) + contract(th, w, 1, 0)
+        tkv_sum[...] += contract(h, pkv[:, at], 1, 1) + contract(th, k, 1, 1)
+
+    attend(lengths[d], cosine[...], sine[...], sums_f32, q_out, k_out, v_out, a_one, ta_low)
+    jobs[1].start()
+    jobs[0].relay()
+
+    @tiles(width, TILE)
+    def _(at):
+        moved = contract(ta_low[...], wo[1, :, at], 1, 0) + contract(a_one[...], po[:, at], 1, 0)
+        store_by_owner(part, at, moved)
+
     for one in sums:
         one.start()
     for one in sums:
         one.send()
-    for job in jobs:
-        job.start()
     for one in sums:
         one.middle()
-    swap.start()
     half = t_one.shape[1]
     for r in range(2):
         position = (2 * t + r) * half + lax.broadcasted_iota(jnp.int32, t_one.shape[1:], 0)
@@ -765,10 +922,9 @@
         c_out[r] = cotangent
         c_low[r] = cotangent.astype(BF16)
         rows[r].start()
-    swap.start_pairs()
-    for r in range(2):
-        rows[r].relay()
-        jobs[r].relay()
+    rows[0].relay()
+    jobs[1].relay()
+    rows[1].relay()
     for job in jobs:
         job.pass_on()
     for r in range(2):
@@ -779,30 +935,40 @@
         job.finish()
 
 
-SMEM = pl.BlockSpec(memory_space=pltpu.SMEM)
-
-
-def turn(lengths, moved, t_one, a_zero, a_one, h_one):
+def turn(lengths, tables, wq, kv, pq, pkv, wo, po, h_one, th_one, t_one, a_zero):
     half, width = t_one.shape[1:]
+    length, columns = a_zero.shape
     return comm_call(
         turn_kernel,
         "turn",
         3,
-        [SMEM] + [VMEM] * 2 + [ANY] * 3,
-        [VMEM] * 2 + [ANY] * 3,
+        [SMEM] + [VMEM] * 12,
+        [VMEM] * 5 + [ANY] * 3,
         [
+            shape((length, columns), BF16),
+            shape((length, HD), BF16),
+            shape((length, HD), BF16),
             shape((2, half, width), F32),
             shape((16, 2, half, width), BF16),
             shape((8,) + a_zero.shape, BF16),
-            shape((8,) + a_one.shape, BF16),
-            shape((8, h_one.shape[0], h_one.shape[1] // 8), BF16),
+            shape((8,) + a_zero.shape, BF16),
+            shape((8, length, width // 8), BF16),
         ],
-        [pltpu.VMEM((2, half, width), BF16)]
+        [
+            pltpu.VMEM((length, columns), BF16),
+            pltpu.VMEM((length, columns), BF16),
+            pltpu.VMEM((8, 2, 2, half, width), BF16),
+            pltpu.VMEM((2, half, width), BF16),
+            pltpu.VMEM((length, columns), F32),
+            pltpu.VMEM((length, columns), F32),
+            pltpu.VMEM((length, 2 * HD), F32),
+            pltpu.VMEM((length, 2 * HD), F32),
+        ]
         + TensorSum.scratch(width) * 2
         + TensorGather.scratch * 2
         + DataGather.scratch * 2
         + DataExchange.scratch,
-        (lengths, moved, t_one, a_zero, a_one, h_one),
+        (lengths,) + tables + (wq, kv, pq, pkv, wo, po, h_one, th_one, t_one, a_zero),
     )
 
 
@@ -840,8 +1006,11 @@
         )
 
     def start(self):
-        d, t = places()
+        self.swap().start()
         self.jobs[0].start()
+
+    def merge(self):
+        d, t = places()
         self.swap().wait()
         mine = self.gkv[lax.rem(t, 2)].astype(F32) + self.came[...].astype(F32)
         self.merged[...] = mine.astype(BF16)
@@ -862,16 +1031,18 @@
 
 def lower_kernel(*refs):
     (
-        (part, c_two, x_one, gains, gkv, gq, cb_one),
+        (lengths, cosine, sine, q, k, v, cb_one, wo, wq, kv, c_two, x_one, gains),
         (cb_all, gg, cbs, mini),
-        (c_low,),
+        (ga_sum, gq, gkv, gkv_low, part, c_low),
         sum_refs,
         gather_refs,
         (came, merged),
         sems,
         swap_sems,
         spread_sems,
-    ) = taken(refs, 7, 4, 1, 10, 4, 2, 6, 2, 2)
+    ) = taken(refs, 13, 4, 6, 10, 4, 2, 6, 2, 2)
+    d, t = places()
+    width = cb_one.shape[1]
     enter(HOPS)
     lots = taken(sum_refs, 5, 5)
     sums = [TensorSum(r, part, *lots[r]) for r in range(2)]
@@ -879,15 +1050,31 @@
     rows = [TensorGather(c_low.at[r], half_slot(cb_all, r), *lots[r]) for r in range(2)]
     jobs = Cotangents(gq, gkv, gg, came, merged, sems)
     swap = DataExchange(cb_one, cbs, *swap_sems)
-    jobs.swap().start()
+    swap.start()
+    swap.start_pairs()
+    ga_sum[...] = jnp.zeros_like(ga_sum)
+
+    @tiles(width, TILE)
+    def _(at):
+        ga_sum[...] += contract(cb_one[:, at], wo[1, :, at], 1, 1)
+
+    attend_back(
+        lengths[d], cosine[...], sine[...], q, k[...], v[...], ga_sum, gq, gkv, gkv_low
+    )
+    jobs.start()
+
+    @tiles(width, TILE)
+    def _(at):
+        term = contract(gq[...], wq[1, at], 1, 1) + contract(gkv_low[...], kv[1, :, at], 1, 0)
+        store_by_owner(part, at, term)
+
     for one in sums:
         one.start()
+    jobs.merge()
     for one in sums:
         one.send()
-    jobs.start()
     for one in sums:
         one.middle()
-    swap.start()
     for r in range(2):
         scaled = sums[r].total() * gains[1:2]
         wide = x_one[r].astype(F32)
@@ -898,7 +1085,6 @@
         rows[r].start()
     spread = DataSpread(c_low, mini, *spread_sems)
     spread.start()
-    swap.start_pairs()
     for one in rows:
         one.relay()
     jobs.relay()
@@ -911,370 +1097,150 @@
     jobs.finish()
 
 
-def lower(part, c_two, x_one, gains, gkv, gq, cb_one):
+def lower(lengths, tables, q, k, v, cb_one, wo, wq, kv, c_two, x_one, gains):
     half, width = c_two.shape[1:]
+    length, columns = q.shape
+    gkv = shape((2, length, HD), BF16)
     return comm_call(
         lower_kernel,
         "lower",
         4,
-        [VMEM] * 5 + [ANY] * 2,
+        [SMEM] + [VMEM] * 12,
         [VMEM] + [ANY] * 3,
         [
             shape((16, 2, half, width), BF16),
-            shape((8, gq.shape[0], gq.shape[1] + gkv.shape[2]), BF16),
-            shape((8, cb_one.shape[0], width // 8), BF16),
+            shape((8, length, columns + HD), BF16),
+            shape((8, length, width // 8), BF16),
             shape((8, 2, half, width // 8), BF16),
         ],
-        [pltpu.VMEM((2, half, width), BF16)]
+        [
+            pltpu.VMEM((length, columns), F32),
+            pltpu.VMEM((length, columns), BF16),
+            pltpu.VMEM(gkv.shape, BF16),
+            pltpu.VMEM((length, 2 * HD), BF16),
+            pltpu.VMEM((8, 2, 2, half, width), BF16),
+            pltpu.VMEM((2, half, width), BF16),
+        ]
         + TensorSum.scratch(width) * 2
         + TensorGather.scratch * 2
         + Cotangents.scratch(gkv)
         + DataExchange.scratch
         + DataSpread.scratch,
-        (part, c_two, x_one, gains, gkv, gq, cb_one),
-    )
+        (lengths,) + tables + (q, k, v, cb_one, wo, wq, kv, c_two, x_one, gains),
+    )
+
+
+def inner(hs, gathered, g_sum):
+    g_sum[...] = jnp.zeros_like(g_sum)
+
+    @pl.loop(0, 4)
+    def _(i):
+        g = gathered[pl.ds(2 * i, 2)].reshape(-1, gathered.shape[2])
+        h = hs[pl.ds(2 * i, 2)].reshape(-1, hs.shape[2])
+        g_sum[...] += contract(g, h, 0, 0)
+
+
+def outer(ga, cs, o_sum):
+    o_sum[...] = jnp.zeros_like(o_sum)
+
+    @pl.loop(0, 4)
+    def _(i):
+        a = ga[pl.ds(2 * i, 2)].reshape(-1, ga.shape[2])
+        c = cs[pl.ds(2 * i, 2)].reshape(-1, cs.shape[2])
+        o_sum[...] += contract(a, c, 0, 0)
 
 
 def last_kernel(*refs):
-    (gkv, mini, gq), (gg, cbs), (came, merged), sems, slice_sems = taken(refs, 3, 2, 2, 6, 2)
+    (
+        (lengths, cosine, sine, q, k, v, cb, wo, mini, hs, gg_one, ga, cs),
+        (gg, cs_zero, q_out, g_sum, o_sum),
+        (ga_sum, gq, gkv),
+        (came, merged),
+        sems,
+        slice_sems,
+    ) = taken(refs, 13, 5, 3, 2, 6, 2)
+    d, t = places()
+    width, columns = cb.shape[1], gq.shape[1]
     enter(NEAR)
-    slices = TensorGather(mini, lambda block: cbs.at[:, block], *slice_sems)
+    slices = TensorGather(mini, lambda block: cs_zero.at[:, block], *slice_sems)
     jobs = Cotangents(gq, gkv, gg, came, merged, sems)
-    jobs.swap().start()
     slices.start()
+    ga_sum[...] = jnp.zeros_like(ga_sum)
+
+    @tiles(width, TILE)
+    def _(at):
+        ga_sum[...] += contract(cb[:, at], wo[0, :, at], 1, 1)
+
+    attend_back(lengths[d], cosine[...], sine[...], q, k[...], v[...], ga_sum, gq, gkv, None)
     jobs.start()
     slices.relay()
+    jobs.merge()
+    inner(hs, gg_one, g_sum)
+    q_out[...] = g_sum[0:columns].T
     jobs.relay()
+    outer(ga, cs, o_sum)
     jobs.pass_on()
     slices.finish()
     jobs.finish()
 
 
-def last(gkv, mini, gq):
+def last(lengths, tables, q, k, v, cb, wo, mini, *sides):
+    length, columns = q.shape
+    share = mini.shape[3]
+    gkv = shape((2, length, HD), BF16)
     return comm_call(
         last_kernel,
         "last",
         5,
-        [VMEM] * 2 + [ANY],
-        [ANY] * 2,
+        [SMEM] + [VMEM] * 12,
+        [ANY] * 2 + [VMEM] * 3,
         [
-            shape((8, gq.shape[0], gq.shape[1] + gkv.shape[2]), BF16),
+            shape((8, length, columns + HD), BF16),
             shape((8, 16) + mini.shape[1:], BF16),
+            shape((share, columns), F32),
+            shape((columns + HD, share), F32),
+            shape((columns, share), F32),
         ],
-        Cotangents.scratch(gkv) + TensorGather.scratch,
-        (gkv, mini, gq),
-    )
-
-
-def contract(left_side, right_side, left_dim, right_dim):
-    return lax.dot_general(
-        left_side,
-        right_side,
-        (((left_dim,), (right_dim,)), ((), ())),
-        preferred_element_type=F32,
-    )
-
-
-def turned(values, cosine, sine):
-    return values * cosine + pltpu.roll(values, values.shape[1] // 2, 1) * sine
-
-
-def attention_weights(q, k, length):
-    size = q.shape[0]
-    row = lax.broadcasted_iota(jnp.int32, (size, size), 0)
-    column = lax.broadcasted_iota(jnp.int32, (size, size), 1)
-    allowed = (column <= row) & (column < length)
-    scores = contract(q, k, 1, 1) * (1.0 / math.sqrt(q.shape[1]))
-    powers = jnp.where(allowed, jnp.exp(scores), 0.0)
-    return powers / jnp.sum(powers, axis=-1, keepdims=True)
-
-
-def forward_kernel(steps, second, *refs):
-    more = 1 if second else 0
-    (
-        (lengths, cosine, sine, wq, kv, pq, pkv, wo, po, h),
-        th,
-        (q_out, k_out, v_out, a_out, moved),
-        primal,
-        (q_sum, tq_sum, kv_sum, tkv_sum, ta_low),
-    ) = taken(refs, 10, more, 5, 1 - more, 5)
-    i = pl.program_id(0)
-    sums = (q_sum, tq_sum, kv_sum, tkv_sum)
-
-    @pl.when(i == 0)
-    def _():
-        for one in sums:
-            one[...] = jnp.zeros_like(one)
-
-    @pl.when(i < steps)
-    def _():
-        normed = h[...]
-        q_sum[...] += contract(normed, wq[...], 1, 0)
-        kv_sum[...] += contract(normed, kv[...], 1, 1)
-        tq = contract(normed, pq[...], 1, 0)
-        tkv = contract(normed, pkv[...], 1, 1)
-        if second:
-            tq = tq + contract(th[0][...], wq[...], 1, 0)
-            tkv = tkv + contract(th[0][...], kv[...], 1, 1)
-        tq_sum[...] += tq
-        tkv_sum[...] += tkv
-
-    @pl.when(i == steps - 1)
-    def _():
-        length = lengths[lax.axis_index("dp")]
-        scaling = 1.0 / math.sqrt(HD)
-        cos, sin = cosine[...], sine[...]
-        k = turned(kv_sum[:, 0:HD], cos, sin).astype(BF16)
-        v = kv_sum[:, HD:].astype(BF16)
-        tk = turned(tkv_sum[:, 0:HD], cos, sin).astype(BF16)
-        tv = tkv_sum[:, HD:].astype(BF16)
-        k_out[...] = k
-        v_out[...] = v
-        for at in range(0, q_sum.shape[1], HD):
-            head = slice(at, at + HD)
-            q = turned(q_sum[:, head], cos, sin).astype(BF16)
-            tq = turned(tq_sum[:, head], cos, sin).astype(BF16)
-            q_out[:, head] = q
-            weights = attention_weights(q, k, length)
-            low = weights.astype(BF16)
-            a_out[:, head] = contract(low, v, 1, 0).astype(BF16)
-            scores = (contract(tq, k, 1, 1) + contract(q, tk, 1, 1)) * scaling
-            change = weights * (scores - jnp.sum(weights * scores, axis=-1, keepdims=True))
-            ta = contract(change.astype(BF16), v, 1, 0) + contract(low, tv, 1, 0)
-            ta_low[:, head] = ta.astype(BF16)
-
-    @pl.when(i >= steps)
-    def _():
-        moved[...] = (
-            contract(ta_low[...], wo[...], 1, 0) + contract(a_out[...], po[...], 1, 0)
-        ).astype(BF16)
-        if not second:
-            primal[0][...] = contract(a_out[...], wo[...], 1, 0).astype(BF16)
-
-
-def whole(dims):
-    return pl.BlockSpec(dims, lambda i: (0,) * len(dims))
-
-
-TILE = 1024
-
-
-def forward(layer, lengths, tables, wq, kv, pq, pkv, wo, po, h, th=None):
-    rows, width = h.shape
-    columns = wq.shape[2]
-    steps = width // TILE
-    second = th is not None
-
-    def now(i):
-        return jnp.minimum(i, steps - 1)
-
-    def later(i):
-        return jnp.maximum(i - steps, 0)
-
-    into = pl.BlockSpec((rows, TILE), lambda i: (0, now(i)))
-    out = pl.BlockSpec((rows, TILE), lambda i: (0, later(i)))
-    in_specs = [
-        SMEM,
-        whole((rows, HD)),
-        whole((rows, HD)),
-        pl.BlockSpec((None, TILE, columns), lambda i: (layer, now(i), 0)),
-        pl.BlockSpec((None, 2 * HD, TILE), lambda i: (layer, 0, now(i))),
-        pl.BlockSpec((TILE, columns), lambda i: (now(i), 0)),
-        pl.BlockSpec((2 * HD, TILE), lambda i: (0, now(i))),
-        pl.BlockSpec((None, columns, TILE), lambda i: (layer, 0, later(i))),
-        pl.BlockSpec((columns, TILE), lambda i: (0, later(i))),
-        into,
-    ] + [into] * second
-    out_specs = [
-        whole((rows, columns)),
-        whole((rows, HD)),
-        whole((rows, HD)),
-        whole((rows, columns)),
-        out,
-    ] + [out] * (not second)
-    out_shape = [
-        shape((rows, columns), BF16),
-        shape((rows, HD), BF16),
-        shape((rows, HD), BF16),
-        shape((rows, columns), BF16),
-        shape((rows, width), BF16),
-    ] + [shape((rows, width), BF16)] * (not second)
-    args = (lengths,) + tables + (wq, kv, pq, pkv, wo, po, h) + ((th,) if second else ())
-    return pl.pallas_call(
-        functools.partial(forward_kernel, steps, second),
-        name=f"forward_{layer}",
-        grid=(2 * steps,),
-        in_specs=in_specs,
-        out_specs=out_specs,
-        out_shape=out_shape,
-        scratch_shapes=[
-            pltpu.VMEM((rows, columns), F32),
-            pltpu.VMEM((rows, columns), F32),
-            pltpu.VMEM((rows, 2 * HD), F32),
-            pltpu.VMEM((rows, 2 * HD), F32),
-            pltpu.VMEM((rows, columns), BF16),
-        ],
-        compiler_params=pltpu.CompilerParams(vmem_limit_bytes=20 * 2**20),
-    )(*args)
-
-
-def backward_kernel(steps, lowest, *refs):
-    more = 0 if lowest else 1
-    (
-        (lengths, cosine, sine, q_in, k_in, v_in, cb, wo),
-        weights_in,
-        (gq_out, gkv_out),
-        part,
-        (ga_sum, gkv_low),
-    ) = taken(refs, 8, 2 * more, 2, more, 2)
-    i = pl.program_id(0)
-
-    @pl.when(i == 0)
-    def _():
-        ga_sum[...] = jnp.zeros_like(ga_sum)
-
-    @pl.when(i < steps)
-    def _():
-        ga_sum[...] += contract(cb[...], wo[...], 1, 1)
-
-    @pl.when(i == steps - 1)
-    def _():
-        length = lengths[lax.axis_index("dp")]
-        scaling = 1.0 / math.sqrt(HD)
-        cos, sin = cosine[...], -sine[...]
-        k, v = k_in[...], v_in[...]
-        gk, gv = None, None
-        for at in range(0, ga_sum.shape[1], HD):
-            head = slice(at, at + HD)
-            q = q_in[:, head]
-            ga = ga_sum[:, head].astype(BF16)
-            weights = attention_weights(q, k, length)
-            grads = contract(ga, v, 1, 1)
-            value = contract(weights.astype(BF16), ga, 0, 0)
-            scores = (
-                weights * (grads - jnp.sum(weights * grads, axis=-1, keepdims=True)) * scaling
-            ).astype(BF16)
-            gq_out[:, head] = turned(contract(scores, k, 1, 0), cos, sin).astype(BF16)
-            key = contract(scores, q, 0, 0)
-            gk = key if gk is None else gk + key
-            gv = value if gv is None else gv + value
-        gk = turned(gk, cos, sin).astype(BF16)
-        gv = gv.astype(BF16)
-        half = HD // 2
-        gkv_low[:, 0:HD] = gk
-        gkv_low[:, HD:] = gv
-        gkv_out[0] = jnp.concatenate([gk[:, 0:half], gv[:, 0:half]], axis=-1)
-        gkv_out[1] = jnp.concatenate([gk[:, half:], gv[:, half:]], axis=-1)
-
-    if not lowest:
-
-        @pl.when(i >= steps)
-        def _():
-            part[0][...] = (
-                contract(gq_out[...], weights_in[0][...], 1, 1)
-                + contract(gkv_low[...], weights_in[1][...], 1, 0)
-            ).astype(BF16)
-
-
-def backward(layer, lengths, tables, q, k, v, cb, wo, wq, kv):
-    rows, width = cb.shape
-    columns = wo.shape[1]
-    steps = width // TILE
-    lowest = layer == 0
-
-    def now(i):
-        return jnp.minimum(i, steps - 1)
-
-    def later(i):
-        return jnp.maximum(i - steps, 0)
-
-    in_specs = [
-        SMEM,
-        whole((rows, HD)),
-        whole((rows, HD)),
-        whole((rows, columns)),
-        whole((rows, HD)),
-        whole((rows, HD)),
-        pl.BlockSpec((rows, TILE), lambda i: (0, now(i))),
-        pl.BlockSpec((None, columns, TILE), lambda i: (layer, 0, now(i))),
-    ]
-    out_specs = [whole((rows, columns)), whole((2, rows, HD))]
-    out_shape = [shape((rows, columns), BF16), shape((2, rows, HD), BF16)]
-    args = (lengths,) + tables + (q, k, v, cb, wo)
-    if not lowest:
-        in_specs += [
-            pl.BlockSpec((None, TILE, columns), lambda i: (layer, later(i), 0)),
-            pl.BlockSpec((None, 2 * HD, TILE), lambda i: (layer, 0, later(i))),
+        [
+            pltpu.VMEM((length, columns), F32),
+            pltpu.VMEM((length, columns), BF16),
+            pltpu.VMEM(gkv.shape, BF16),
         ]
-        out_specs.append(pl.BlockSpec((rows, TILE), lambda i: (0, later(i))))
-        out_shape.append(shape((rows, width), BF16))
-        args += (wq, kv)
-    return pl.pallas_call(
-        functools.partial(backward_kernel, steps, lowest),
-        name=f"backward_{layer}",
-        grid=(steps if lowest else 2 * steps,),
-        in_specs=in_specs,
-        out_specs=out_specs,
-        out_shape=out_shape,
-        scratch_shapes=[
-            pltpu.VMEM((rows, columns), F32),
-            pltpu.VMEM((rows, 2 * HD), BF16),
-        ],
-        compiler_params=pltpu.CompilerParams(vmem_limit_bytes=20 * 2**20),
-    )(*args)
-
-
-def products_kernel(*refs):
-    sides, (q_out, k_out, v_out, o_out), (q_sum,) = taken(refs, 8, 4, 1)
-    i = pl.program_id(0)
+        + Cotangents.scratch(gkv)
+        + TensorGather.scratch,
+        (lengths,) + tables + (q, k, v, cb, wo, mini) + sides,
+    )
+
+
+def products_kernel(hs, gg, ga, cs, q_one, g_one, o_one, q_out, k_out, v_out, o_out, g_sum):
     columns, half = q_out.shape[2], k_out.shape[1]
-    for layer in range(2):
-        hs, gg, ga, cs = [ref[...].reshape(-1, ref.shape[-1]) for ref in sides[4 * layer :][:4]]
-        g = contract(gg, hs, 0, 0)
-        o = contract(ga, cs, 0, 0)
-
-        @pl.when(i == 0)
-        def _():
-            q_sum[layer] = g[0:columns]
-            k_out[layer] = g[columns : columns + half]
-            v_out[layer] = g[columns + half :]
-            o_out[layer] = o
-
-        @pl.when(i > 0)
-        def _():
-            q_sum[layer] += g[0:columns]
-            k_out[layer] += g[columns : columns + half]
-            v_out[layer] += g[columns + half :]
-            o_out[layer] += o
-
-    @pl.when(i == pl.num_programs(0) - 1)
-    def _():
-        for layer in range(2):
-            q_out[layer] = q_sum[layer].T
-
-
-def products(*sides):
-    chunk = 2
-    columns, share = sides[2].shape[2], sides[0].shape[2]
-    half = (sides[1].shape[2] - columns) // 2
-    out_shape = [
-        shape((2, share, columns), F32),
-        shape((2, half, share), F32),
-        shape((2, half, share), F32),
-        shape((2, columns, share), F32),
-    ]
+    inner(hs, gg, g_sum)
+    outer(ga, cs, o_out.at[0])
+    q_out[0] = g_sum[0:columns].T
+    q_out[1] = q_one[...]
+    o_out[1] = o_one[...]
+    for layer, one in ((0, g_sum), (1, g_one)):
+        k_out[layer] = one[columns : columns + half]
+        v_out[layer] = one[columns + half :]
+
+
+def products(*operands):
+    share, columns = operands[4].shape
+    half = (operands[1].shape[2] - columns) // 2
     return pl.pallas_call(
         products_kernel,
         name="products",
-        grid=(8 // chunk,),
-        in_specs=[
-            pl.BlockSpec((chunk,) + side.shape[1:], lambda i: (i, 0, 0)) for side in sides
+        in_specs=[VMEM] * 7,
+        out_specs=[VMEM] * 4,
+        out_shape=[
+            shape((2, share, columns), F32),
+            shape((2, half, share), F32),
+            shape((2, half, share), F32),
+            shape((2, columns, share), F32),
         ],
-        out_specs=[whole(out.shape) for out in out_shape],
-        out_shape=out_shape,
-        scratch_shapes=[pltpu.VMEM((2, columns, share), F32)],
-        compiler_params=pltpu.CompilerParams(vmem_limit_bytes=20 * 2**20),
-    )(*sides)
+        scratch_shapes=[pltpu.VMEM(operands[5].shape, F32)],
+        compiler_params=pltpu.CompilerParams(vmem_limit_bytes=14 * 2**20),
+    )(*operands)
 
 
 def rope_tables():
@@ -1307,9 +1273,6 @@
 
     tokens = tokens.reshape(2, rows // 2, width)
 
-    def by_owner(part):
-        return part.reshape(8, 2, 2, rows // 2, width)
-
     def all_rows(blocks):
         return blocks.reshape(-1, blocks.shape[-1])
 
@@ -1320,15 +1283,7 @@
     h_zero, hs_zero, pq, pkv, po, kv = first(
         normed(tokens, gains), probes, turned_over(key_weight), turned_over(value_weight)
     )
-    q0, k0, v0, a_zero, moved, primal = forward(
-        0, lengths, tables, query_weight, kv, all_rows(pq), pkv, out_weight, po, all_rows(h_zero)
-    )
-    x_one, t_one, h_one, th_one, pq, pkv, po = between(
-        by_owner(primal), by_owner(moved), tokens, gains, probes
-    )
-    h_one = all_rows(h_one)
-    q1, k1, v1, a_one, moved = forward(
-        1,
+    q0, k0, v0, a_zero, x_one, t_one, h_one, th_one, pq, pkv, po = between(
         lengths,
         tables,
         query_weight,
@@ -1337,25 +1292,55 @@
         pkv,
         out_weight,
         po,
-        h_one,
+        all_rows(h_zero),
+        tokens,
+        gains,
+        probes,
+    )
+    q1, k1, v1, c_two, cb_one, ga_zero, ga_one, hs_one = turn(
+        lengths,
+        tables,
+        query_weight,
+        kv,
+        all_rows(pq),
+        pkv,
+        out_weight,
+        po,
+        all_rows(h_one),
         all_rows(th_one),
-    )
-    c_two, cb_one, ga_zero, ga_one, hs_one = turn(
-        lengths, by_owner(moved), t_one, a_zero, a_one, h_one
-    )
-    cb_one = all_rows(cb_one)
-    gq, gkv, part = backward(
-        1, lengths, tables, q1, k1, v1, cb_one, out_weight, query_weight, kv
+        t_one,
+        a_zero,
     )
     cb_zero, gg_one, cs_one, mini = lower(
-        by_owner(part), c_two, x_one, gains, gkv, gq, cb_one
-    )
-    gq, gkv = backward(
-        0, lengths, tables, q0, k0, v0, all_rows(cb_zero), out_weight, query_weight, kv
-    )
-    gg_zero, cs_zero = last(gkv, mini, gq)
+        lengths,
+        tables,
+        q1,
+        k1,
+        v1,
+        all_rows(cb_one),
+        out_weight,
+        query_weight,
+        kv,
+        c_two,
+        x_one,
+        gains,
+    )
+    gg_zero, cs_zero, q_one, g_one, o_one = last(
+        lengths,
+        tables,
+        q0,
+        k0,
+        v0,
+        all_rows(cb_zero),
+        out_weight,
+        mini,
+        hs_one,
+        gg_one,
+        ga_one,
+        cs_one,
+    )
     q, k, v, o = products(
-        by_batch(hs_zero), gg_zero, ga_zero, by_batch(cs_zero), hs_one, gg_one, ga_one, cs_one
+        by_batch(hs_zero), gg_zero, ga_zero, by_batch(cs_zero), q_one, g_one, o_one
     )
     return (q, turned_over(k), turned_over(v), o)
 

time: 245 us -> 231 us (0.943)
  Pallas kernels: 241 us -> 225 us
    pallas_call x5 -> x1, Pallas kernels: 33.9 us -> 4.56 us  [products(): pl.pallas_call(products_kernel, name='products', in_specs=[VMEM] * 7, out...]
    pallas_call x5, Pallas kernels: 207 us -> 220 us  [comm_call(): pl.pallas_call(kernel, name=name, in_specs=in_specs, out_specs=out_specs,...]
where the time goes in v4:
time: 231 us
  Pallas kernels  225 us (97%)
  local copies, waits for them, and re-layouts  4.81 us (2%)
    pallas_call x5, Pallas kernels, comm_call(): pl.pallas_call(kernel, name=name, in_specs=in_specs, out_specs=out_specs,...  220 us
    unnamed x34, local copies, waits for them, and re-layouts  4.81 us

profile of v4, /device:TPU:1, one launch (start us, length us, event | category | flops | bytes accessed | tf_op | source)
XLA Modules:
  0.0 230.8 jit_solution(12964325209084303626)
XLA Ops:
  0.6 0.0 copy-start.5
  0.6 0.0 copy-start.4
  0.7 0.0 copy-start.3
  0.7 0.0 copy-start.2
  0.7 0.0 copy-start.6
  0.7 1.0 copy-done.6
  1.7 0.0 copy-start.10
  1.7 0.8 copy-done.10
  2.5 0.0 copy-start.8
  2.5 0.0 copy-start.9
  2.5 0.1 normed.1.refs_0_
  2.6 0.0 copy-done.5
  2.7 0.0 copy-done.4
  2.7 0.0 copy-done.3
  2.7 0.0 copy-done.2
  2.7 0.7 copy-done.8
  3.4 0.0 copy-done.9
  3.5 0.0 copy-start
  3.5 0.0 copy-start.1
  3.5 0.0 copy-start.7
  3.5 0.0 copy-start.11
  3.5 0.0 copy-start.12
  3.5 0.0 copy-start.13
  3.5 0.0 copy-start.14
  3.5 50.7 %first.1 = (bf16[16,2,8,4096]{3,2,1,0:T(8,128)(2,1)S(1)}, bf16[8,16,2,8,512]{4,3,2,1,0:T(8,128)(2,1)S(1)}, bf16[8,512,256]{2,1,0:T(8,128)(2,1)S(1)}, bf16[256,40...) custom-call(bf16[2,8,4096]{2,1,0:T(8,128)(2,1)S(1)} %normed.1.refs_0_, ...), custom_call_target="tpu_custom_call" | custom-call | flops 10000000000 | tf_op jit(solution)/shard_map/first/pallas_call | solution.py:451
  54.2 0.0 copy-start.15
  54.2 0.0 copy-done
  54.2 0.0 copy-done.1
  54.2 0.0 copy-done.7
  54.2 0.0 copy-done.11
  54.2 0.0 copy-done.12
  54.2 0.0 copy-done.13
  54.2 0.0 copy-done.14
  54.3 64.3 %between.1 = (bf16[256,256]{1,0:T(8,128)(2,1)S(1)}, bf16[256,128]{1,0:T(8,128)(2,1)S(1)}, bf16[256,128]{1,0:T(8,128)(2,1)S(1)}, bf16[256,256]{1,0:T(8,128)(2,1)S...) custom-call(s32[8]{0:T(128)S(1)} %copy-done.12, ...), custom_call_target="tpu_custom_call" | custom-call | flops 10000000000 | tf_op jit(solution)/shard_map/between/pallas_call | solution.py:451
  118.6 0.0 copy-done.15
  118.6 43.3 %turn.1 = (bf16[256,256]{1,0:T(8,128)(2,1)S(1)}, bf16[256,128]{1,0:T(8,128)(2,1)S(1)}, bf16[256,128]{1,0:T(8,128)(2,1)S(1)}, f32[2,8,4096]{2,1,0:T(8,128)S(1)}, ...) custom-call(s32[8]{0:T(128)S(1)} %copy-done.12, ...), custom_call_target="tpu_custom_call" | custom-call | flops 10000000000 | tf_op jit(solution)/shard_map/turn/pallas_call | solution.py:451
  162.0 0.0 copy-start.16
  162.0 2.2 copy-done.16
  164.2 40.9 %lower.1 = (bf16[16,2,8,4096]{3,2,1,0:T(8,128)(2,1)S(1)}, bf16[8,256,384]{2,1,0:T(8,128)(2,1)S(1)}, bf16[8,256,512]{2,1,0:T(8,128)(2,1)S(1)}, bf16[8,2,8,512]{3,2,1,0:T(8,128)(2,1)S(1)}) custom-call(s32[8]{0:T(128)S(1)} %copy-done.12, f32[256,128]{1,0:T(8,128)S(1)} %copy-done.14, f32[256,128]{1,0:T(8,128)S(1)} %copy-done.13, ...), custom_call_target="tpu_custom_call" | custom-call | flops 10000000000 | tf_op jit(solution)/shard_map/lower/pallas_call | solution.py:451
  205.1 21.1 %last.1 = (bf16[8,256,384]{2,1,0:T(8,128)(2,1)S(1)}, bf16[8,16,2,8,512]{4,3,2,1,0:T(8,128)(2,1)S(1)}, f32[512,256]{1,0:T(8,128)S(1)}, f32[384,512]{1,0:T(8,128)S(1)}, f32[256,512]{1,0:T(8,128)S(1)}) custom-call(s32[8]{0:T(128)S(1)} %copy-done.12, f32[256,128]{1,0:T(8,128)S(1)} %copy-done.14, f32[256,128]{1,0:T(8,128)S(1)} %copy-done.13, ...), custom_call_target="tpu_custom_call" | custom-call | flops 10000000000 | tf_op jit(solution)/shard_map/last/pallas_call | solution.py:451
  226.2 4.6 %products.1 = (f32[2,512,256]{2,1,0:T(8,128)}, f32[2,64,512]{2,1,0:T(8,128)}, f32[2,64,512]{2,1,0:T(8,128)}, f32[2,256,512]{2,1,0:T(8,128)}) custom-call(bf16[8,256,512]{2,1,0:T(8,128)(2,1)S(1)} %bitcast.16, bf16[8,256,384]{2,1,0:T(8,128)(2,1)S(1)} %get-tuple-element.70.gg, bf16[8,256,256]{2,1,0:T(8,128)(2,1)S(1)} %get-tuple-element.71.ga, ...), custom_call_target="tpu_custom_call" | custom-call | tf_op jit(solution)/shard_map/products/pallas_call | solution.py:1230
Async XLA Ops:
  0.6 2.0 copy-start.5
  0.6 2.0 copy-start.4
  0.7 2.0 copy-start.3
  0.7 2.0 copy-start.2
  0.7 1.1 copy-start.6
  1.7 0.8 copy-start.10
  2.5 0.9 copy-start.8
  2.5 1.0 copy-start.9
  3.5 50.7 %copy-start = (bf16[2,4096,256]{2,1,0:T(8,128)(2,1)S(1)}, bf16[2,4096,256]{2,1,0:T(8,128)(2,1)}, u32[]{:S(2)}) copy-start(bf16[2,4096,256]{2,1,0:T(8,128)(2,1)} %refs_8_.1) | copy-start | bytes 12582916
  3.5 50.7 %copy-start.1 = (bf16[2,256,4096]{2,1,0:T(8,128)(2,1)S(1)}, bf16[2,256,4096]{2,1,0:T(8,128)(2,1)}, u32[]{:S(2)}) copy-start(bf16[2,256,4096]{2,1,0:T(8,128)(2,1)} %refs_7_.7) | copy-start | bytes 12582916
  3.5 50.8 %copy-start.7 = (bf16[16,4096]{1,0:T(8,128)(2,1)S(1)}, bf16[16,4096]{1,0:T(8,128)(2,1)}, u32[]{:S(2)}) copy-start(bf16[16,4096]{1,0:T(8,128)(2,1)} %param.13) | copy-start | bytes 393220
  3.5 50.8 %copy-start.11 = (f32[2,4096]{1,0:T(2,128)S(1)}, f32[2,4096]{1,0:T(2,128)}, u32[]{:S(2)}) copy-start(f32[2,4096]{1,0:T(2,128)} %refs_12_.3) | copy-start | bytes 98308
  3.5 50.8 %copy-start.12 = (s32[8]{0:T(128)S(1)}, s32[8]{0:T(128)}, u32[]{:S(2)}) copy-start(s32[8]{0:T(128)} %refs_0_.7) | copy-start | bytes 100
  3.5 50.8 %copy-start.13 = (f32[256,128]{1,0:T(8,128)S(1)}, f32[256,128]{1,0:T(8,128)}, u32[]{:S(2)}) copy-start(f32[256,128]{1,0:T(8,128)} %constant.5.clone.refs_2_) | copy-start | bytes 393220
  3.5 50.8 %copy-start.14 = (f32[256,128]{1,0:T(8,128)S(1)}, f32[256,128]{1,0:T(8,128)}, u32[]{:S(2)}) copy-start(f32[256,128]{1,0:T(8,128)} %constant.4.clone.refs_1_) | copy-start | bytes 393220
  54.2 64.4 %copy-start.15 = (bf16[2,256,4096]{2,1,0:T(8,128)(2,1)}, bf16[2,256,4096]{2,1,0:T(8,128)(2,1)S(1)}, u32[]{:S(2)}) copy-start(bf16[2,256,4096]{2,1,0:T(8,128)(2,1)S(1)} %get-tuple-element.43.refs_4_.refs_9_) | copy-start | bytes 12582916
  162.0 2.2 copy-start.16

commit v5 on v4

--- a/solution.py
+++ b/solution.py
@@ -167,11 +167,30 @@
         ((3, 0), (1, 1), (2, 1), 1),
     )
 
+    def start_ring(self):
+        self.out(1).start()
+        self.out(2).start()
+        self.own().start()
+
+    def start_pair(self):
+        self.out(0).start()
+
+    def relay_ring(self):
+        self.into(0).wait_recv()
+        self.out(3).start()
+        self.out(4).start()
+        self.into(1).wait_recv()
+        self.out(5).start()
+        self.into(2).wait_recv()
+        self.out(7).start()
+
+    def relay_pair(self):
+        self.out(6).start()
+        self.out(8).start()
+
     def relay(self):
-        for j in range(3):
-            self.into(j).wait_recv()
-            self.out(3 + 2 * j).start()
-            self.out(4 + 2 * j).start()
+        self.relay_ring()
+        self.relay_pair()
 
     def pass_on(self):
         for j in (3, 4):
@@ -332,11 +351,14 @@
     def columns(self, d):
         return pl.ds(pl.multiple_of(d * self.share, self.share), self.share)
 
+    def cut(self, d):
+        return self.src.at[(slice(None),) * (len(self.src.shape) - 1) + (self.columns(d),)]
+
     def cross(self, j):
         d, t = places()
         peer = data_at(d, HOPS[j])
         return remote(
-            self.src.at[:, :, self.columns(peer)],
+            self.cut(peer),
             self.out_.at[d],
             self.sends,
             self.recvs,
@@ -352,7 +374,7 @@
     def own(self):
         d, t = places()
         return pltpu.make_async_copy(
-            self.src.at[:, :, self.columns(d)], self.out_.at[d], self.sends.at[7]
+            self.cut(d), self.out_.at[d], self.sends.at[7]
         )
 
     def start(self):
@@ -470,6 +492,11 @@
     return lambda block: ref.at[block]
 
 
+def rows_of(ref, count):
+    size = ref.shape[0] // count
+    return lambda block: ref.at[pl.ds(pl.multiple_of(block * size, size), size)]
+
+
 def half_slot(ref, half):
     return lambda block: ref.at[block, half]
 
@@ -532,7 +559,7 @@
         self.jobs = [
             kind(k.at[layer], part(0), *sems[0:2]),
             kind(v.at[layer], part(1), *sems[2:4]),
-            kind(q.at[layer], slot_of(gq), *sems[4:6]),
+            kind(q.at[layer], rows_of(gq, 8), *sems[4:6]),
             kind(o.at[layer], columns_of(go), *sems[6:8]),
         ]
         self.share = CoreShare(None, lambda j, c: gkv.at[strip(j, c)], *sems[8:10])
@@ -541,7 +568,7 @@
     def shapes(probes):
         q, k, v, o = probes
         return [
-            shape((8,) + q.shape[1:], BF16),
+            shape((8 * q.shape[1], q.shape[2]), BF16),
             shape((4 * k.shape[1], 8 * k.shape[2]), BF16),
             shape((o.shape[1], 8 * o.shape[2]), BF16),
         ]
@@ -608,6 +635,35 @@
         low = weights.astype(BF16)
         a_out[:, head] = contract(low, v, 1, 0).astype(BF16)
         scores = (contract(tq, k, 1, 1) + contract(q, tk, 1, 1)) * scaling
+        change = weights * (scores - jnp.sum(weights * scores, axis=-1, keepdims=True))
+        ta = contract(change.astype(BF16), v, 1, 0) + contract(low, tv, 1, 0)
+        ta_out[:, head] = ta.astype(BF16)
+
+
+def attend_primal(length, cos, sin, q_sum, kv_sum, q_out, k_out, v_out, a_out, w_out):
+    k = turned(kv_sum[:, 0:HD], cos, sin).astype(BF16)
+    v = kv_sum[:, HD:].astype(BF16)
+    k_out[...] = k
+    v_out[...] = v
+    for n, at in enumerate(range(0, q_sum.shape[1], HD)):
+        head = slice(at, at + HD)
+        q = turned(q_sum[:, head], cos, sin).astype(BF16)
+        q_out[:, head] = q
+        weights = attention_weights(q, k, length)
+        w_out[n] = weights
+        a_out[:, head] = contract(weights.astype(BF16), v, 1, 0).astype(BF16)
+
+
+def attend_tangent(cos, sin, tq_sum, tkv_sum, q_in, k, v, w_in, ta_out):
+    scaling = 1.0 / math.sqrt(HD)
+    tk = turned(tkv_sum[:, 0:HD], cos, sin).astype(BF16)
+    tv = tkv_sum[:, HD:].astype(BF16)
+    for n, at in enumerate(range(0, tq_sum.shape[1], HD)):
+        head = slice(at, at + HD)
+        tq = turned(tq_sum[:, head], cos, sin).astype(BF16)
+        weights = w_in[n]
+        low = weights.astype(BF16)
+        scores = (contract(tq, k, 1, 1) + contract(q_in[:, head], tk, 1, 1)) * scaling
         change = weights * (scores - jnp.sum(weights * scores, axis=-1, keepdims=True))
         ta = contract(change.astype(BF16), v, 1, 0) + contract(low, tv, 1, 0)
         ta_out[:, head] = ta.astype(BF16)
@@ -667,197 +723,189 @@
         in_specs=[VMEM, VMEM],
         out_specs=VMEM,
         out_shape=shape(tokens.shape, BF16),
-        cost_estimate=pl.CostEstimate(flops=10**9, bytes_accessed=0, transcendentals=0),
+        cost_estimate=pl.CostEstimate(flops=10**10, bytes_accessed=0, transcendentals=0),
         compiler_params=pltpu.CompilerParams(vmem_limit_bytes=8 * 2**20),
     )(tokens, gains)
 
 
-def first_kernel(*refs):
+def head_kernel(*refs):
     (
-        (h_low, q, k, v, o, kw, vw),
-        (h_all, hs, gq, gkv, go, kv),
-        (mini,),
-        row_sems,
+        (lengths, cosine, sine, h_low, wq, wo, tokens, gains, kw, vw, q, k, v, o),
+        (q_out, k_out, v_out, a_out, x_out, t_out, h_all, th_all, kv, hs, gq, gkv, go),
+        (mini, h_zero, pq, pkv, po, weights, ta_low, part, h_one, th_one),
+        sums_f32,
+        sum_refs,
+        gather_refs,
         spread_sems,
-        slice_sems,
         share_sems,
         own_sems,
-        probe_sems,
-    ) = taken(refs, 7, 6, 1, 2, 2, 2, 2, 1, 10)
+        zero_sems,
+        one_sems,
+    ) = taken(refs, 14, 13, 10, 4, 20, 12, 2, 2, 1, 10, 10)
     d, t = places()
     core = lax.rem(t, 2)
+    width = h_zero.shape[1]
+    gain = gains[1:2]
+    cos, sin = cosine[...], sine[...]
     enter(HOPS)
+    lots = taken(sum_refs, 5, 5, 5, 5)
+    primals = [TensorSum(r, part, *lots[r]) for r in range(2)]
+    moves = [TensorSum(r, part, *lots[2 + r]) for r in range(2)]
+    lots = taken(gather_refs, 2, 2, 2, 2, 2, 2)
+    rows = TensorGather(h_low, rows_of(h_zero, 16), *lots[0])
+    slices = TensorGather(mini, lambda block: hs.at[:, block], *lots[1])
+    rows_h = [TensorGather(h_one.at[r], half_slot(h_all, r), *lots[2 + r]) for r in range(2)]
+    rows_th = [TensorGather(th_one.at[r], half_slot(th_all, r), *lots[4 + r]) for r in range(2)]
     spread = DataSpread(h_low, mini, *spread_sems)
-    rows = TensorGather(h_low, slot_of(h_all), *row_sems)
-    slices = TensorGather(mini, lambda block: hs.at[:, block], *slice_sems)
     share = CoreShare((kw, vw), lambda j, c: kv.at[:, strip(j, c)], *share_sems)
-    probes = Probes(LargeGather, 0, (q, k, v, o), (gq, gkv, go), probe_sems)
     own = [
         pltpu.make_async_copy(src, kv.at[:, strip(j, core)], own_sems[0].at[j])
         for j, src in enumerate((kw, vw))
     ]
+    zeros = Probes(LargeGather, 0, (q, k, v, o), (pq, pkv, po), zero_sems)
+    ones = Probes(LargeGather, 1, (q, k, v, o), (gq, gkv, go), one_sems)
+
     spread.start()
     rows.start()
-    probes.start()
+    zeros.start()
+    share.start()
+    for copy in own:
+        copy.start()
+    q_sum, tq_sum, kv_sum, tkv_sum = sums_f32
+    for one in sums_f32:
+        one[...] = jnp.zeros_like(one)
     rows.relay()
     spread.finish()
     slices.start()
-    share.start()
-    for copy in own:
-        copy.start()
+    for job in zeros.jobs[:3]:
+        job.relay()
     rows.finish()
-    probes.relay()
+    zeros.jobs[3].relay()
     slices.relay()
-    probes.pass_on()
-    slices.finish()
     share.finish()
     for copy in own:
         copy.wait()
-    probes.finish()
-
-
-def first(h_low, probes, kw, vw):
-    half, width = h_low.shape[1:]
-    return comm_call(
-        first_kernel,
-        "first",
-        1,
-        [VMEM] + [HBM] * 6,
-        [VMEM] + [ANY] * 5,
-        [shape((16, 2, half, width), BF16), shape((8, 16, 2, half, width // 8), BF16)]
-        + Probes.shapes(probes)
-        + [shape((2, 4 * kw.shape[1], width), BF16)],
-        [pltpu.VMEM((8, 2, half, width // 8), BF16)]
-        + TensorGather.scratch
-        + DataSpread.scratch
-        + TensorGather.scratch
-        + CoreShare.scratch
-        + [DMA((2,))]
-        + Probes.scratch(LargeGather),
-        (h_low,) + probes + (kw, vw),
-    )
-
-
-def between_kernel(*refs):
-    (
-        (lengths, cosine, sine, wq, kv, pq, pkv, wo, po, h_zero, tokens, gains, q, k, v, o),
-        (q_out, k_out, v_out, a_out, x_out, t_out, h_all, th_all, gq, gkv, go),
-        (ta_low, primal, moved, h_low, th_low),
-        sums_f32,
-        sum_refs,
-        gather_refs,
-        sems,
-    ) = taken(refs, 16, 11, 5, 4, 20, 8, 10)
-    d, t = places()
-    width = h_zero.shape[1]
-    gain = gains[1:2]
-    enter(NEAR)
-    lots = taken(sum_refs, 5, 5, 5, 5)
-    primals = [TensorSum(r, primal, *lots[r]) for r in range(2)]
-    moves = [TensorSum(r, moved, *lots[2 + r]) for r in range(2)]
-    sums = [primals[0], moves[0], primals[1], moves[1]]
-    lots = taken(gather_refs, 2, 2, 2, 2)
-    rows_h = [TensorGather(h_low.at[r], half_slot(h_all, r), *lots[r]) for r in range(2)]
-    rows_th = [TensorGather(th_low.at[r], half_slot(th_all, r), *lots[2 + r]) for r in range(2)]
-    probes = Probes(DataGather, 1, (q, k, v, o), (gq, gkv, go), sems)
-    probes.start()
-    q_sum, tq_sum, kv_sum, tkv_sum = sums_f32
-    for one in sums_f32:
-        one[...] = jnp.zeros_like(one)
 
     @tiles(width, TILE)
     def _(at):
         h = h_zero[:, at]
         q_sum[...] += contract(h, wq[0, at], 1, 0)
         kv_sum[...] += contract(h, kv[0, :, at], 1, 1)
-        tq_sum[...] += contract(h, pq[at], 1, 0)
-        tkv_sum[...] += contract(h, pkv[:, at], 1, 1)
-
-    attend(lengths[d], cosine[...], sine[...], sums_f32, q_out, k_out, v_out, a_out, ta_low)
+
+    attend_primal(lengths[d], cos, sin, q_sum, kv_sum, q_out, k_out, v_out, a_out, weights)
 
     @tiles(width, TILE)
     def _(at):
-        w = wo[0, :, at]
-        store_by_owner(primal, at, contract(a_out[...], w, 1, 0))
-        store_by_owner(
-            moved, at, contract(ta_low[...], w, 1, 0) + contract(a_out[...], po[:, at], 1, 0)
-        )
-
-    for one in sums:
+        store_by_owner(part, at, contract(a_out[...], wo[0, :, at], 1, 0))
+
+    for one in primals:
         one.start()
-    for job in probes.jobs[:2]:
-        job.relay()
-    for one in sums:
+    for job in zeros.jobs[:2]:
+        job.pass_on()
+    for one in primals:
         one.send()
-    for one in sums[:2]:
+    for job in zeros.jobs[2:]:
+        job.pass_on()
+    for job in ones.jobs:
+        job.start_ring()
+    for one in primals:
         one.middle()
-    for job in probes.jobs[2:]:
-        job.relay()
     for r in range(2):
         stream = (tokens[r].astype(F32) + primals[r].total()).astype(BF16)
         x_out[r] = stream
         wide = stream.astype(F32)
         inverse = lax.rsqrt(mean_of(wide * wide) + EPS)
-        h_low[r] = (wide * inverse * gain).astype(BF16)
+        h_one[r] = (wide * inverse * gain).astype(BF16)
         rows_h[r].start()
+    for job in ones.jobs:
+        job.start_pair()
+    for one in primals:
+        one.finish()
+    zeros.finish()
+
+    @tiles(width, TILE)
+    def _(at):
+        h = h_zero[:, at]
+        tq_sum[...] += contract(h, pq[at], 1, 0)
+        tkv_sum[...] += contract(h, pkv[:, at], 1, 1)
+
+    for one in rows_h:
+        one.relay()
+    attend_tangent(cos, sin, tq_sum, tkv_sum, q_out, k_out[...], v_out[...], weights, ta_low)
+
+    @tiles(width, TILE)
+    def _(at):
+        term = contract(ta_low[...], wo[0, :, at], 1, 0) + contract(a_out[...], po[:, at], 1, 0)
+        store_by_owner(part, at, term)
+
+    for one in moves:
+        one.start()
+    for one in moves:
+        one.send()
+    for job in ones.jobs:
+        job.relay_ring()
+    for one in moves:
+        one.middle()
+    for r in range(2):
         tangent = moves[r].total()
         t_out[r] = tangent
+        wide = x_out[r].astype(F32)
+        inverse = lax.rsqrt(mean_of(wide * wide) + EPS)
         shift = mean_of(wide * tangent)
-        th_low[r] = (
+        th_one[r] = (
             gain * (tangent * inverse - wide * inverse * inverse * inverse * shift)
         ).astype(BF16)
         rows_th[r].start()
-        if r == 0:
-            for one in sums[2:]:
-                one.middle()
-            rows_h[0].relay()
-    rows_th[0].relay()
-    rows_h[1].relay()
-    rows_th[1].relay()
-    probes.pass_on()
-    for one in sums:
+    for job in ones.jobs:
+        job.relay_pair()
+    for one in rows_th:
+        one.relay()
+    ones.pass_on()
+    for one in moves:
         one.finish()
-    for rows in rows_h + rows_th:
-        rows.finish()
-    probes.finish()
-
-
-def between(lengths, tables, wq, kv, pq, pkv, wo, po, h_zero, tokens, gains, probes):
+    slices.finish()
+    for one in rows_h + rows_th:
+        one.finish()
+    ones.finish()
+
+
+def head(lengths, tables, h_low, wq, wo, tokens, gains, kw, vw, probes):
     half, width = tokens.shape[1:]
-    length, columns = h_zero.shape[0], wq.shape[2]
+    columns = wq.shape[2]
+    wide = pltpu.VMEM((LEN, columns), F32)
     return comm_call(
-        between_kernel,
-        "between",
-        2,
-        [SMEM] + [VMEM] * 11 + [HBM] * 4,
-        [VMEM] * 8 + [ANY] * 3,
+        head_kernel,
+        "head",
+        1,
+        [SMEM] + [VMEM] * 7 + [HBM] * 6,
+        [VMEM] * 9 + [ANY] * 4,
         [
-            shape((length, columns), BF16),
-            shape((length, HD), BF16),
-            shape((length, HD), BF16),
-            shape((length, columns), BF16),
+            shape((LEN, columns), BF16),
+            shape((LEN, HD), BF16),
+            shape((LEN, HD), BF16),
+            shape((LEN, columns), BF16),
             shape((2, half, width), BF16),
             shape((2, half, width), F32),
             shape((16, 2, half, width), BF16),
             shape((16, 2, half, width), BF16),
+            shape((2, 4 * kw.shape[1], width), BF16),
+            shape((8, 16, 2 * half, width // 8), BF16),
         ]
         + Probes.shapes(probes),
-        [
-            pltpu.VMEM((length, columns), BF16),
-            pltpu.VMEM((8, 2, 2, half, width), BF16),
-            pltpu.VMEM((8, 2, 2, half, width), BF16),
-            pltpu.VMEM((2, half, width), BF16),
-            pltpu.VMEM((2, half, width), BF16),
-            pltpu.VMEM((length, columns), F32),
-            pltpu.VMEM((length, columns), F32),
-            pltpu.VMEM((length, 2 * HD), F32),
-            pltpu.VMEM((length, 2 * HD), F32),
-        ]
+        [pltpu.VMEM((8, 2 * half, width // 8), BF16), pltpu.VMEM((LEN, width), BF16)]
+        + [pltpu.VMEM(one.shape, BF16) for one in Probes.shapes(probes)]
+        + [pltpu.VMEM((columns // HD, LEN, LEN), F32), pltpu.VMEM((LEN, columns), BF16)]
+        + [pltpu.VMEM((8, 2, 2, half, width), BF16)]
+        + [pltpu.VMEM((2, half, width), BF16)] * 2
+        + [wide] * 4
         + TensorSum.scratch(width) * 4
-        + TensorGather.scratch * 4
-        + Probes.scratch(DataGather),
-        (lengths,) + tables + (wq, kv, pq, pkv, wo, po, h_zero, tokens, gains) + probes,
-        limit=16,
+        + TensorGather.scratch * 6
+        + DataSpread.scratch
+        + CoreShare.scratch
+        + [DMA((2,))]
+        + Probes.scratch(LargeGather) * 2,
+        (lengths,) + tables + (h_low, wq, wo, tokens, gains, kw, vw) + probes,
+        limit=19,
     )
 
 
@@ -1239,7 +1287,7 @@
             shape((2, columns, share), F32),
         ],
         scratch_shapes=[pltpu.VMEM(operands[5].shape, F32)],
-        compiler_params=pltpu.CompilerParams(vmem_limit_bytes=14 * 2**20),
+        compiler_params=pltpu.CompilerParams(vmem_limit_bytes=12 * 2**20),
     )(*operands)
 
 
@@ -1271,8 +1319,6 @@
     def turned_over(array):
         return jnp.swapaxes(array, 1, 2)
 
-    tokens = tokens.reshape(2, rows // 2, width)
-
     def all_rows(blocks):
         return blocks.reshape(-1, blocks.shape[-1])
 
@@ -1280,21 +1326,16 @@
         return blocks.reshape(blocks.shape[0], -1, blocks.shape[-1])
 
     probes = (query_probe, turned_over(key_probe), turned_over(value_probe), out_probe)
-    h_zero, hs_zero, pq, pkv, po, kv = first(
-        normed(tokens, gains), probes, turned_over(key_weight), turned_over(value_weight)
-    )
-    q0, k0, v0, a_zero, x_one, t_one, h_one, th_one, pq, pkv, po = between(
+    q0, k0, v0, a_zero, x_one, t_one, h_one, th_one, kv, hs_zero, pq, pkv, po = head(
         lengths,
         tables,
+        normed(tokens, gains),
         query_weight,
-        kv,
-        all_rows(pq),
-        pkv,
         out_weight,
-        po,
-        all_rows(h_zero),
-        tokens,
+        tokens.reshape(2, rows // 2, width),
         gains,
+        turned_over(key_weight),
+        turned_over(value_weight),
         probes,
     )
     q1, k1, v1, c_two, cb_one, ga_zero, ga_one, hs_one = turn(
@@ -1302,7 +1343,7 @@
         tables,
         query_weight,
         kv,
-        all_rows(pq),
+        pq,
         pkv,
         out_weight,
         po,

time: 231 us -> 217 us (0.939)
  Pallas kernels: 225 us -> 211 us
    pallas_call x5 -> x4, Pallas kernels: 220 us -> 206 us  [comm_call(): pl.pallas_call(kernel, name=name, in_specs=in_specs, out_specs=out_specs,...]
    unnamed x34 -> x30, local copies, waits for them, and re-layouts: 4.81 us -> 5.96 us
where the time goes in v5:
time: 217 us
  Pallas kernels  211 us (97%)
  local copies, waits for them, and re-layouts  5.96 us (3%)
    pallas_call x4, Pallas kernels, comm_call(): pl.pallas_call(kernel, name=name, in_specs=in_specs, out_specs=out_specs,...  206 us
    unnamed x30, local copies, waits for them, and re-layouts  5.96 us
    pallas_call x1, Pallas kernels, products(): pl.pallas_call(products_kernel, name='products', in_specs=[VMEM] * 7, out...  4.57 us

profile of v5, /device:TPU:1, one launch (start us, length us, event | category | flops | bytes accessed | tf_op | source)
XLA Modules:
  0.0 217.2 jit_solution(4985959571197566388)
XLA Ops:
  0.6 0.0 copy-start.6
  0.6 0.9 copy-done.6
  1.5 0.0 copy-start.10
  1.5 0.8 copy-done.10
  2.3 0.0 copy-start
  2.3 0.0 copy-start.1
  2.3 0.0 copy-start.2
  2.3 0.0 copy-start.3
  2.3 0.0 copy-start.4
  2.3 0.0 copy-start.5
  2.3 0.0 copy-start.7
  2.3 0.0 copy-start.8
  2.4 0.0 copy-start.9
  2.4 0.0 copy-start.11
  2.4 0.0 copy-start.12
  2.4 0.0 copy-start.13
  2.4 0.0 copy-start.14
  2.4 0.1 normed.1.refs_3_
  2.6 1.9 copy-done
  4.5 1.3 copy-done.1
  5.8 0.2 copy-done.2
  6.0 0.3 copy-done.3
  6.3 0.1 copy-done.4
  6.5 0.2 copy-done.5
  6.7 0.0 copy-done.7
  6.7 0.1 copy-done.8
  6.8 0.1 copy-done.9
  6.8 0.0 copy-done.11
  6.8 0.0 copy-done.12
  6.8 0.0 copy-done.13
  6.8 0.0 copy-done.14
  6.8 98.9 %head.1 = (bf16[256,256]{1,0:T(8,128)(2,1)S(1)}, bf16[256,128]{1,0:T(8,128)(2,1)S(1)}, bf16[256,128]{1,0:T(8,128)(2,1)S(1)}, bf16[256,256]{1,0:T(8,128)(2,1)S(1)...) custom-call(s32[8]{0:T(128)S(1)} %copy-done.12, ...), custom_call_target="tpu_custom_call" | custom-call | flops 10000000000 | tf_op jit(solution)/shard_map/head/pallas_call | solution.py:473
  105.8 45.0 %turn.1 = (bf16[256,256]{1,0:T(8,128)(2,1)S(1)}, bf16[256,128]{1,0:T(8,128)(2,1)S(1)}, bf16[256,128]{1,0:T(8,128)(2,1)S(1)}, f32[2,8,4096]{2,1,0:T(8,128)S(1)}, ...) custom-call(s32[8]{0:T(128)S(1)} %copy-done.12, ...), custom_call_target="tpu_custom_call" | custom-call | flops 10000000000 | tf_op jit(solution)/shard_map/turn/pallas_call | solution.py:473
  150.8 41.8 %lower.1 = (bf16[16,2,8,4096]{3,2,1,0:T(8,128)(2,1)S(1)}, bf16[8,256,384]{2,1,0:T(8,128)(2,1)S(1)}, bf16[8,256,512]{2,1,0:T(8,128)(2,1)S(1)}, bf16[8,2,8,512]{3,2,1,0:T(8,128)(2,1)S(1)}) custom-call(s32[8]{0:T(128)S(1)} %copy-done.12, f32[256,128]{1,0:T(8,128)S(1)} %copy-done.14, f32[256,128]{1,0:T(8,128)S(1)} %copy-done.13, ...), custom_call_target="tpu_custom_call" | custom-call | flops 10000000000 | tf_op jit(solution)/shard_map/lower/pallas_call | solution.py:473
  192.6 20.0 %last.1 = (bf16[8,256,384]{2,1,0:T(8,128)(2,1)S(1)}, bf16[8,16,2,8,512]{4,3,2,1,0:T(8,128)(2,1)S(1)}, f32[512,256]{1,0:T(8,128)S(1)}, f32[384,512]{1,0:T(8,128)S(1)}, f32[256,512]{1,0:T(8,128)S(1)}) custom-call(s32[8]{0:T(128)S(1)} %copy-done.12, f32[256,128]{1,0:T(8,128)S(1)} %copy-done.14, f32[256,128]{1,0:T(8,128)S(1)} %copy-done.13, ...), custom_call_target="tpu_custom_call" | custom-call | flops 10000000000 | tf_op jit(solution)/shard_map/last/pallas_call | solution.py:473
  212.7 4.6 %products.1 = (f32[2,512,256]{2,1,0:T(8,128)}, f32[2,64,512]{2,1,0:T(8,128)}, f32[2,64,512]{2,1,0:T(8,128)}, f32[2,256,512]{2,1,0:T(8,128)}) custom-call(bf16[8,256,512]{2,1,0:T(8,128)(2,1)S(1)} %bitcast.13, bf16[8,256,384]{2,1,0:T(8,128)(2,1)S(1)} %get-tuple-element.62.gg, bf16[8,256,256]{2,1,0:T(8,128)(2,1)S(1)} %get-tuple-element.63.ga, ...), custom_call_target="tpu_custom_call" | custom-call | tf_op jit(solution)/shard_map/products/pallas_call | solution.py:1278
Async XLA Ops:
  0.6 0.9 copy-start.6
  1.5 0.8 copy-start.10
  2.3 2.2 %copy-start = (bf16[2,4096,256]{2,1,0:T(8,128)(2,1)S(1)}, bf16[2,4096,256]{2,1,0:T(8,128)(2,1)}, u32[]{:S(2)}) copy-start(bf16[2,4096,256]{2,1,0:T(8,128)(2,1)} %refs_8_.1) | copy-start | bytes 12582916
  2.3 3.5 %copy-start.1 = (bf16[2,256,4096]{2,1,0:T(8,128)(2,1)S(1)}, bf16[2,256,4096]{2,1,0:T(8,128)(2,1)}, u32[]{:S(2)}) copy-start(bf16[2,256,4096]{2,1,0:T(8,128)(2,1)} %refs_7_.7) | copy-start | bytes 12582916
  2.3 3.7 %copy-start.2 = (bf16[2,4096,64]{1,2,0:T(8,128)(2,1)S(1)}, bf16[2,4096,64]{1,2,0:T(8,128)(2,1)}, u32[]{:S(2)}) copy-start(bf16[2,4096,64]{1,2,0:T(8,128)(2,1)} %param.17) | copy-start | bytes 3145732
  2.3 4.0 %copy-start.3 = (bf16[2,4096,64]{1,2,0:T(8,128)(2,1)S(1)}, bf16[2,4096,64]{1,2,0:T(8,128)(2,1)}, u32[]{:S(2)}) copy-start(bf16[2,4096,64]{1,2,0:T(8,128)(2,1)} %param.18) | copy-start | bytes 3145732
  2.3 4.2 %copy-start.4 = (bf16[2,512,256]{2,1,0:T(8,128)(2,1)S(1)}, bf16[2,512,256]{2,1,0:T(8,128)(2,1)}, u32[]{:S(2)}) copy-start(bf16[2,512,256]{2,1,0:T(8,128)(2,1)} %refs_10_.1) | copy-start | bytes 1572868
  2.3 4.3 %copy-start.5 = (bf16[2,256,512]{2,1,0:T(8,128)(2,1)S(1)}, bf16[2,256,512]{2,1,0:T(8,128)(2,1)}, u32[]{:S(2)}) copy-start(bf16[2,256,512]{2,1,0:T(8,128)(2,1)} %refs_13_.1) | copy-start | bytes 1572868
  2.3 4.4 %copy-start.7 = (bf16[16,4096]{1,0:T(8,128)(2,1)S(1)}, bf16[16,4096]{1,0:T(8,128)(2,1)}, u32[]{:S(2)}) copy-start(bf16[16,4096]{1,0:T(8,128)(2,1)} %tokens.1) | copy-start | bytes 393220
  2.3 4.4 %copy-start.8 = (bf16[2,512,64]{1,2,0:T(8,128)(2,1)S(1)}, bf16[2,512,64]{1,2,0:T(8,128)(2,1)}, u32[]{:S(2)}) copy-start(bf16[2,512,64]{1,2,0:T(8,128)(2,1)} %param.21) | copy-start | bytes 393220
  2.4 4.5 %copy-start.9 = (bf16[2,512,64]{1,2,0:T(8,128)(2,1)S(1)}, bf16[2,512,64]{1,2,0:T(8,128)(2,1)}, u32[]{:S(2)}) copy-start(bf16[2,512,64]{1,2,0:T(8,128)(2,1)} %param.22) | copy-start | bytes 393220
  2.4 4.4 %copy-start.11 = (f32[2,4096]{1,0:T(2,128)S(1)}, f32[2,4096]{1,0:T(2,128)}, u32[]{:S(2)}) copy-start(f32[2,4096]{1,0:T(2,128)} %refs_12_.1) | copy-start | bytes 98308
  2.4 4.4 %copy-start.12 = (s32[8]{0:T(128)S(1)}, s32[8]{0:T(128)}, u32[]{:S(2)}) copy-start(s32[8]{0:T(128)} %refs_0_.7) | copy-start | bytes 100
  2.4 4.4 %copy-start.13 = (f32[256,128]{1,0:T(8,128)S(1)}, f32[256,128]{1,0:T(8,128)}, u32[]{:S(2)}) copy-start(f32[256,128]{1,0:T(8,128)} %constant.5.clone.refs_2_) | copy-start | bytes 393220
  2.4 4.5 %copy-start.14 = (f32[256,128]{1,0:T(8,128)S(1)}, f32[256,128]{1,0:T(8,128)}, u32[]{:S(2)}) copy-start(f32[256,128]{1,0:T(8,128)} %constant.4.clone.refs_1_) | copy-start | bytes 393220

commit v6 on v5

--- a/solution.py
+++ b/solution.py
@@ -252,10 +252,12 @@
             self.out(j).start()
         self.hand(0).start()
 
-    def finish(self):
+    def collect(self):
         for j in range(1, 7):
             self.into(j).wait_recv()
             self.hand(j).start()
+
+    def close(self):
         self.sent()
         d, t = places()
         far = other_core(t)
@@ -265,6 +267,10 @@
             block = tensor_at(far, self.ROUTES[j][2])
             self.handover(j, self.slot(block), block).wait_recv()
             self.hand(j).wait_send()
+
+    def finish(self):
+        self.collect()
+        self.close()
 
 
 class TensorSum:
@@ -415,24 +421,24 @@
             (peer, t),
         )
 
-    def hand(self, j, t_of):
+    def landing(self, j, t_of):
         d, t = places()
         slot = self.out_.at[data_at(d, back(HOPS[j])), self.rows(t_of)]
         return slot
 
     def arrived(self, j):
         d, t = places()
-        slot = self.hand(j, t)
+        slot = self.landing(j, t)
         return remote(slot, slot, self.sends, self.recvs, j, (d, other_core(t)))
 
     def handed(self, j):
         d, t = places()
-        slot = self.hand(j, t)
+        slot = self.landing(j, t)
         return remote(slot, slot, self.sends, self.recvs, 7 + j, (d, other_core(t)))
 
     def received(self, j):
         d, t = places()
-        slot = self.hand(j, other_core(t))
+        slot = self.landing(j, other_core(t))
         return remote(slot, slot, self.sends, self.recvs, 7 + j, (d, other_core(t)))
 
     def own(self):
@@ -450,10 +456,12 @@
         for j in (6, 0, 1, 2):
             self.cross(j).start()
 
-    def finish(self):
+    def collect(self):
         for j in (4, 5, 3, 6, 0, 1, 2):
             self.arrived(j).wait_recv()
             self.handed(j).start()
+
+    def finish(self):
         for j in range(7):
             self.received(j).wait_recv()
             self.cross(j).wait_send()
@@ -861,11 +869,14 @@
     for one in rows_th:
         one.relay()
     ones.pass_on()
+    slices.collect()
+    for one in rows_h + rows_th:
+        one.collect()
     for one in moves:
         one.finish()
-    slices.finish()
+    slices.close()
     for one in rows_h + rows_th:
-        one.finish()
+        one.close()
     ones.finish()
 
 
@@ -970,15 +981,19 @@
         c_out[r] = cotangent
         c_low[r] = cotangent.astype(BF16)
         rows[r].start()
+    swap.collect()
     rows[0].relay()
+    rows[1].relay()
     jobs[1].relay()
-    rows[1].relay()
     for job in jobs:
         job.pass_on()
-    for r in range(2):
-        sums[r].finish()
-        rows[r].finish()
+    for one in rows:
+        one.collect()
+    for one in sums:
+        one.finish()
     swap.finish()
+    for one in rows:
+        one.close()
     for job in jobs:
         job.finish()
 
@@ -1133,15 +1148,19 @@
         rows[r].start()
     spread = DataSpread(c_low, mini, *spread_sems)
     spread.start()
+    swap.collect()
     for one in rows:
         one.relay()
     jobs.relay()
     jobs.pass_on()
-    for r in range(2):
-        sums[r].finish()
-        rows[r].finish()
+    for one in rows:
+        one.collect()
+    for one in sums:
+        one.finish()
     swap.finish()
     spread.finish()
+    for one in rows:
+        one.close()
     jobs.finish()
 
 
@@ -1189,24 +1208,24 @@
 
 
 def outer(ga, cs, o_sum):
-    o_sum[...] = jnp.zeros_like(o_sum)
+    o_sum[...] = jnp.zeros(o_sum.shape, F32)
 
     @pl.loop(0, 4)
     def _(i):
-        a = ga[pl.ds(2 * i, 2)].reshape(-1, ga.shape[2])
-        c = cs[pl.ds(2 * i, 2)].reshape(-1, cs.shape[2])
+        a = ga[pl.ds(2 * i, 2)].reshape(-1, ga.shape[-1])
+        c = cs[pl.ds(2 * i, 2)].reshape(-1, cs.shape[-1])
         o_sum[...] += contract(a, c, 0, 0)
 
 
 def last_kernel(*refs):
     (
-        (lengths, cosine, sine, q, k, v, cb, wo, mini, hs, gg_one, ga, cs),
+        (lengths, cosine, sine, q, k, v, cb, wo, mini, ga_zero, hs, gg_one, ga, cs),
         (gg, cs_zero, q_out, g_sum, o_sum),
         (ga_sum, gq, gkv),
         (came, merged),
         sems,
         slice_sems,
-    ) = taken(refs, 13, 5, 3, 2, 6, 2)
+    ) = taken(refs, 14, 5, 3, 2, 6, 2)
     d, t = places()
     width, columns = cb.shape[1], gq.shape[1]
     enter(NEAR)
@@ -1226,9 +1245,10 @@
     inner(hs, gg_one, g_sum)
     q_out[...] = g_sum[0:columns].T
     jobs.relay()
-    outer(ga, cs, o_sum)
+    outer(ga, cs, o_sum.at[1])
     jobs.pass_on()
     slices.finish()
+    outer(ga_zero, cs_zero, o_sum.at[0])
     jobs.finish()
 
 
@@ -1240,14 +1260,14 @@
         last_kernel,
         "last",
         5,
-        [SMEM] + [VMEM] * 12,
-        [ANY] * 2 + [VMEM] * 3,
+        [SMEM] + [VMEM] * 13,
+        [ANY] + [VMEM] * 4,
         [
             shape((8, length, columns + HD), BF16),
             shape((8, 16) + mini.shape[1:], BF16),
             shape((share, columns), F32),
             shape((columns + HD, share), F32),
-            shape((columns, share), F32),
+            shape((2, columns, share), F32),
         ],
         [
             pltpu.VMEM((length, columns), F32),
@@ -1260,25 +1280,24 @@
     )
 
 
-def products_kernel(hs, gg, ga, cs, q_one, g_one, o_one, q_out, k_out, v_out, o_out, g_sum):
+def products_kernel(hs, gg, q_one, g_one, o_both, q_out, k_out, v_out, o_out, g_sum):
     columns, half = q_out.shape[2], k_out.shape[1]
+    o_out[...] = o_both[...]
     inner(hs, gg, g_sum)
-    outer(ga, cs, o_out.at[0])
     q_out[0] = g_sum[0:columns].T
     q_out[1] = q_one[...]
-    o_out[1] = o_one[...]
     for layer, one in ((0, g_sum), (1, g_one)):
         k_out[layer] = one[columns : columns + half]
         v_out[layer] = one[columns + half :]
 
 
 def products(*operands):
-    share, columns = operands[4].shape
+    share, columns = operands[2].shape
     half = (operands[1].shape[2] - columns) // 2
     return pl.pallas_call(
         products_kernel,
         name="products",
-        in_specs=[VMEM] * 7,
+        in_specs=[VMEM] * 5,
         out_specs=[VMEM] * 4,
         out_shape=[
             shape((2, share, columns), F32),
@@ -1286,7 +1305,7 @@
             shape((2, half, share), F32),
             shape((2, columns, share), F32),
         ],
-        scratch_shapes=[pltpu.VMEM(operands[5].shape, F32)],
+        scratch_shapes=[pltpu.VMEM(operands[3].shape, F32)],
         compiler_params=pltpu.CompilerParams(vmem_limit_bytes=12 * 2**20),
     )(*operands)
 
@@ -1366,7 +1385,7 @@
         x_one,
         gains,
     )
-    gg_zero, cs_zero, q_one, g_one, o_one = last(
+    gg_zero, unused, q_one, g_one, o_both = last(
         lengths,
         tables,
         q0,
@@ -1375,14 +1394,13 @@
         all_rows(cb_zero),
         out_weight,
         mini,
+        ga_zero,
         hs_one,
         gg_one,
         ga_one,
         cs_one,
     )
-    q, k, v, o = products(
-        by_batch(hs_zero), gg_zero, ga_zero, by_batch(cs_zero), q_one, g_one, o_one
-    )
+    q, k, v, o = products(by_batch(hs_zero), gg_zero, q_one, g_one, o_both)
     return (q, turned_over(k), turned_over(v), o)
 
 

time: 217 us -> 213 us (0.982)
  Pallas kernels: 211 us -> 206 us
    pallas_call x4, Pallas kernels: 206 us -> 203 us  [comm_call(): pl.pallas_call(kernel, name=name, in_specs=in_specs, out_specs=out_specs,...]
where the time goes in v6:
time: 213 us
  Pallas kernels  206 us (97%)
  local copies, waits for them, and re-layouts  5.84 us (3%)
    pallas_call x4, Pallas kernels, comm_call(): pl.pallas_call(kernel, name=name, in_specs=in_specs, out_specs=out_specs,...  203 us
    unnamed x30, local copies, waits for them, and re-layouts  5.84 us

profile of v6, /device:TPU:1, one launch (start us, length us, event | category | flops | bytes accessed | tf_op | source)
XLA Modules:
  0.0 212.9 jit_solution(7429502520867132670)
XLA Ops:
  0.6 0.0 copy-start.6
  0.6 0.9 copy-done.6
  1.5 0.0 copy-start.10
  1.5 0.8 copy-done.10
  2.3 0.0 copy-start
  2.3 0.0 copy-start.1
  2.3 0.0 copy-start.2
  2.3 0.0 copy-start.3
  2.3 0.0 copy-start.4
  2.3 0.0 copy-start.5
  2.3 0.0 copy-start.7
  2.3 0.0 copy-start.8
  2.4 0.0 copy-start.9
  2.4 0.0 copy-start.11
  2.4 0.0 copy-start.12
  2.4 0.0 copy-start.13
  2.4 0.0 copy-start.14
  2.4 0.1 normed.1.refs_3_
  2.6 1.9 copy-done
  4.5 1.3 copy-done.1
  5.8 0.2 copy-done.2
  6.0 0.3 copy-done.3
  6.3 0.1 copy-done.4
  6.4 0.1 copy-done.5
  6.5 0.0 copy-done.7
  6.6 0.0 copy-done.8
  6.6 0.0 copy-done.9
  6.6 0.0 copy-done.11
  6.6 0.0 copy-done.12
  6.6 0.1 copy-done.13
  6.7 0.0 copy-done.14
  6.7 98.0 %head.1 = (bf16[256,256]{1,0:T(8,128)(2,1)S(1)}, bf16[256,128]{1,0:T(8,128)(2,1)S(1)}, bf16[256,128]{1,0:T(8,128)(2,1)S(1)}, bf16[256,256]{1,0:T(8,128)(2,1)S(1)...) custom-call(s32[8]{0:T(128)S(1)} %copy-done.12, ...), custom_call_target="tpu_custom_call" | custom-call | flops 10000000000 | tf_op jit(solution)/shard_map/head/pallas_call | solution.py:481
  104.7 43.7 %turn.1 = (bf16[256,256]{1,0:T(8,128)(2,1)S(1)}, bf16[256,128]{1,0:T(8,128)(2,1)S(1)}, bf16[256,128]{1,0:T(8,128)(2,1)S(1)}, f32[2,8,4096]{2,1,0:T(8,128)S(1)}, ...) custom-call(s32[8]{0:T(128)S(1)} %copy-done.12, ...), custom_call_target="tpu_custom_call" | custom-call | flops 10000000000 | tf_op jit(solution)/shard_map/turn/pallas_call | solution.py:481
  148.4 39.5 %lower.1 = (bf16[16,2,8,4096]{3,2,1,0:T(8,128)(2,1)S(1)}, bf16[8,256,384]{2,1,0:T(8,128)(2,1)S(1)}, bf16[8,256,512]{2,1,0:T(8,128)(2,1)S(1)}, bf16[8,2,8,512]{3,2,1,0:T(8,128)(2,1)S(1)}) custom-call(s32[8]{0:T(128)S(1)} %copy-done.12, f32[256,128]{1,0:T(8,128)S(1)} %copy-done.14, f32[256,128]{1,0:T(8,128)S(1)} %copy-done.13, ...), custom_call_target="tpu_custom_call" | custom-call | flops 10000000000 | tf_op jit(solution)/shard_map/lower/pallas_call | solution.py:481
  187.9 22.0 %last.1 = (bf16[8,256,384]{2,1,0:T(8,128)(2,1)S(1)}, bf16[8,16,2,8,512]{4,3,2,1,0:T(8,128)(2,1)}, f32[512,256]{1,0:T(8,128)S(1)}, f32[384,512]{1,0:T(8,128)S(1)}, f32[2,256,512]{2,1,0:T(8,128)S(1)}) custom-call(s32[8]{0:T(128)S(1)} %copy-done.12, f32[256,128]{1,0:T(8,128)S(1)} %copy-done.14, f32[256,128]{1,0:T(8,128)S(1)} %copy-done.13, ...), custom_call_target="tpu_custom_call" | custom-call | flops 10000000000 | tf_op jit(solution)/shard_map/last/pallas_call | solution.py:481
  209.9 3.0 %products.1 = (f32[2,512,256]{2,1,0:T(8,128)}, f32[2,64,512]{2,1,0:T(8,128)}, f32[2,64,512]{2,1,0:T(8,128)}, f32[2,256,512]{2,1,0:T(8,128)}) custom-call(bf16[8,256,512]{2,1,0:T(8,128)(2,1)S(1)} %bitcast.12, bf16[8,256,384]{2,1,0:T(8,128)(2,1)S(1)} %get-tuple-element.62.gg, f32[512,256]{1,0:T(8,128)S(1)} %get-tuple-element.63.q_one, ...), custom_call_target="tpu_custom_call" | custom-call | tf_op jit(solution)/shard_map/products/pallas_call | solution.py:1297
Async XLA Ops:
  0.6 0.9 copy-start.6
  1.5 0.8 copy-start.10
  2.3 2.2 %copy-start = (bf16[2,4096,256]{2,1,0:T(8,128)(2,1)S(1)}, bf16[2,4096,256]{2,1,0:T(8,128)(2,1)}, u32[]{:S(2)}) copy-start(bf16[2,4096,256]{2,1,0:T(8,128)(2,1)} %refs_8_.1) | copy-start | bytes 12582916
  2.3 3.5 %copy-start.1 = (bf16[2,256,4096]{2,1,0:T(8,128)(2,1)S(1)}, bf16[2,256,4096]{2,1,0:T(8,128)(2,1)}, u32[]{:S(2)}) copy-start(bf16[2,256,4096]{2,1,0:T(8,128)(2,1)} %refs_7_.7) | copy-start | bytes 12582916
  2.3 3.7 %copy-start.2 = (bf16[2,4096,64]{1,2,0:T(8,128)(2,1)S(1)}, bf16[2,4096,64]{1,2,0:T(8,128)(2,1)}, u32[]{:S(2)}) copy-start(bf16[2,4096,64]{1,2,0:T(8,128)(2,1)} %param.17) | copy-start | bytes 3145732
  2.3 4.0 %copy-start.3 = (bf16[2,4096,64]{1,2,0:T(8,128)(2,1)S(1)}, bf16[2,4096,64]{1,2,0:T(8,128)(2,1)}, u32[]{:S(2)}) copy-start(bf16[2,4096,64]{1,2,0:T(8,128)(2,1)} %param.18) | copy-start | bytes 3145732
  2.3 4.1 %copy-start.4 = (bf16[2,512,256]{2,1,0:T(8,128)(2,1)S(1)}, bf16[2,512,256]{2,1,0:T(8,128)(2,1)}, u32[]{:S(2)}) copy-start(bf16[2,512,256]{2,1,0:T(8,128)(2,1)} %refs_10_.1) | copy-start | bytes 1572868
  2.3 4.2 %copy-start.5 = (bf16[2,256,512]{2,1,0:T(8,128)(2,1)S(1)}, bf16[2,256,512]{2,1,0:T(8,128)(2,1)}, u32[]{:S(2)}) copy-start(bf16[2,256,512]{2,1,0:T(8,128)(2,1)} %refs_13_.1) | copy-start | bytes 1572868
  2.3 4.2 %copy-start.7 = (bf16[16,4096]{1,0:T(8,128)(2,1)S(1)}, bf16[16,4096]{1,0:T(8,128)(2,1)}, u32[]{:S(2)}) copy-start(bf16[16,4096]{1,0:T(8,128)(2,1)} %tokens.1) | copy-start | bytes 393220
  2.3 4.2 %copy-start.8 = (bf16[2,512,64]{1,2,0:T(8,128)(2,1)S(1)}, bf16[2,512,64]{1,2,0:T(8,128)(2,1)}, u32[]{:S(2)}) copy-start(bf16[2,512,64]{1,2,0:T(8,128)(2,1)} %param.21) | copy-start | bytes 393220
  2.4 4.3 %copy-start.9 = (bf16[2,512,64]{1,2,0:T(8,128)(2,1)S(1)}, bf16[2,512,64]{1,2,0:T(8,128)(2,1)}, u32[]{:S(2)}) copy-start(bf16[2,512,64]{1,2,0:T(8,128)(2,1)} %param.22) | copy-start | bytes 393220
  2.4 4.3 %copy-start.11 = (f32[2,4096]{1,0:T(2,128)S(1)}, f32[2,4096]{1,0:T(2,128)}, u32[]{:S(2)}) copy-start(f32[2,4096]{1,0:T(2,128)} %refs_12_.1) | copy-start | bytes 98308
  2.4 4.3 %copy-start.12 = (s32[8]{0:T(128)S(1)}, s32[8]{0:T(128)}, u32[]{:S(2)}) copy-start(s32[8]{0:T(128)} %refs_0_.7) | copy-start | bytes 100
  2.4 4.3 %copy-start.13 = (f32[256,128]{1,0:T(8,128)S(1)}, f32[256,128]{1,0:T(8,128)}, u32[]{:S(2)}) copy-start(f32[256,128]{1,0:T(8,128)} %constant.5.clone.refs_2_) | copy-start | bytes 393220
  2.4 4.3 %copy-start.14 = (f32[256,128]{1,0:T(8,128)S(1)}, f32[256,128]{1,0:T(8,128)}, u32[]{:S(2)}) copy-start(f32[256,128]{1,0:T(8,128)} %constant.4.clone.refs_1_) | copy-start | bytes 393220

commit v7 on v6

--- a/solution.py
+++ b/solution.py
@@ -794,7 +794,7 @@
     for copy in own:
         copy.wait()
 
-    @tiles(width, TILE)
+    @tiles(width, 2 * TILE)
     def _(at):
         h = h_zero[:, at]
         q_sum[...] += contract(h, wq[0, at], 1, 0)
@@ -831,7 +831,7 @@
         one.finish()
     zeros.finish()
 
-    @tiles(width, TILE)
+    @tiles(width, 2 * TILE)
     def _(at):
         h = h_zero[:, at]
         tq_sum[...] += contract(h, pq[at], 1, 0)
@@ -949,7 +949,7 @@
     for one in sums_f32:
         one[...] = jnp.zeros_like(one)
 
-    @tiles(width, TILE)
+    @tiles(width, 2 * TILE)
     def _(at):
         h, th = h_one[:, at], th_one[:, at]
         w, k = wq[1, at], kv[1, :, at]
@@ -1117,7 +1117,7 @@
     swap.start_pairs()
     ga_sum[...] = jnp.zeros_like(ga_sum)
 
-    @tiles(width, TILE)
+    @tiles(width, 2 * TILE)
     def _(at):
         ga_sum[...] += contract(cb_one[:, at], wo[1, :, at], 1, 1)
 
@@ -1234,7 +1234,7 @@
     slices.start()
     ga_sum[...] = jnp.zeros_like(ga_sum)
 
-    @tiles(width, TILE)
+    @tiles(width, 2 * TILE)
     def _(at):
         ga_sum[...] += contract(cb[:, at], wo[0, :, at], 1, 1)
 

time: 213 us -> 213 us (level)
  no operation moved by 1% of the time
where the time goes in v7:
time: 213 us; the launch traced here: 212 us
  Pallas kernels  206 us (97%)
  local copies, waits for them, and re-layouts  5.84 us (3%)
    pallas_call x4, Pallas kernels, comm_call(): pl.pallas_call(kernel, name=name, in_specs=in_specs, out_specs=out_specs,...  203 us
    unnamed x30, local copies, waits for them, and re-layouts  5.84 us

profile of v7, /device:TPU:1, one launch (start us, length us, event | category | flops | bytes accessed | tf_op | source)
XLA Modules:
  0.0 212.5 jit_solution(9707562620730403946)
XLA Ops:
  0.6 0.0 copy-start.6
  0.6 0.9 copy-done.6
  1.5 0.0 copy-start.10
  1.5 0.8 copy-done.10
  2.3 0.0 copy-start
  2.3 0.0 copy-start.1
  2.3 0.0 copy-start.2
  2.3 0.0 copy-start.3
  2.3 0.0 copy-start.4
  2.3 0.0 copy-start.5
  2.3 0.0 copy-start.7
  2.3 0.0 copy-start.8
  2.4 0.0 copy-start.9
  2.4 0.0 copy-start.11
  2.4 0.0 copy-start.12
  2.4 0.0 copy-start.13
  2.4 0.0 copy-start.14
  2.4 0.1 normed.1.refs_3_
  2.6 1.9 copy-done
  4.5 1.3 copy-done.1
  5.8 0.2 copy-done.2
  6.0 0.3 copy-done.3
  6.3 0.1 copy-done.4
  6.4 0.1 copy-done.5
  6.5 0.0 copy-done.7
  6.6 0.0 copy-done.8
  6.6 0.0 copy-done.9
  6.6 0.0 copy-done.11
  6.6 0.0 copy-done.12
  6.6 0.1 copy-done.13
  6.7 0.0 copy-done.14
  6.7 97.5 %head.1 = (bf16[256,256]{1,0:T(8,128)(2,1)S(1)}, bf16[256,128]{1,0:T(8,128)(2,1)S(1)}, bf16[256,128]{1,0:T(8,128)(2,1)S(1)}, bf16[256,256]{1,0:T(8,128)(2,1)S(1)...) custom-call(s32[8]{0:T(128)S(1)} %copy-done.12, ...), custom_call_target="tpu_custom_call" | custom-call | flops 10000000000 | tf_op jit(solution)/shard_map/head/pallas_call | solution.py:481
  104.3 43.5 %turn.1 = (bf16[256,256]{1,0:T(8,128)(2,1)S(1)}, bf16[256,128]{1,0:T(8,128)(2,1)S(1)}, bf16[256,128]{1,0:T(8,128)(2,1)S(1)}, f32[2,8,4096]{2,1,0:T(8,128)S(1)}, ...) custom-call(s32[8]{0:T(128)S(1)} %copy-done.12, ...), custom_call_target="tpu_custom_call" | custom-call | flops 10000000000 | tf_op jit(solution)/shard_map/turn/pallas_call | solution.py:481
  147.8 39.8 %lower.1 = (bf16[16,2,8,4096]{3,2,1,0:T(8,128)(2,1)S(1)}, bf16[8,256,384]{2,1,0:T(8,128)(2,1)S(1)}, bf16[8,256,512]{2,1,0:T(8,128)(2,1)S(1)}, bf16[8,2,8,512]{3,2,1,0:T(8,128)(2,1)S(1)}) custom-call(s32[8]{0:T(128)S(1)} %copy-done.12, f32[256,128]{1,0:T(8,128)S(1)} %copy-done.14, f32[256,128]{1,0:T(8,128)S(1)} %copy-done.13, ...), custom_call_target="tpu_custom_call" | custom-call | flops 10000000000 | tf_op jit(solution)/shard_map/lower/pallas_call | solution.py:481
  187.6 21.9 %last.1 = (bf16[8,256,384]{2,1,0:T(8,128)(2,1)S(1)}, bf16[8,16,2,8,512]{4,3,2,1,0:T(8,128)(2,1)}, f32[512,256]{1,0:T(8,128)S(1)}, f32[384,512]{1,0:T(8,128)S(1)}, f32[2,256,512]{2,1,0:T(8,128)S(1)}) custom-call(s32[8]{0:T(128)S(1)} %copy-done.12, f32[256,128]{1,0:T(8,128)S(1)} %copy-done.14, f32[256,128]{1,0:T(8,128)S(1)} %copy-done.13, ...), custom_call_target="tpu_custom_call" | custom-call | flops 10000000000 | tf_op jit(solution)/shard_map/last/pallas_call | solution.py:481
  209.5 3.0 %products.1 = (f32[2,512,256]{2,1,0:T(8,128)}, f32[2,64,512]{2,1,0:T(8,128)}, f32[2,64,512]{2,1,0:T(8,128)}, f32[2,256,512]{2,1,0:T(8,128)}) custom-call(bf16[8,256,512]{2,1,0:T(8,128)(2,1)S(1)} %bitcast.12, bf16[8,256,384]{2,1,0:T(8,128)(2,1)S(1)} %get-tuple-element.62.gg, f32[512,256]{1,0:T(8,128)S(1)} %get-tuple-element.63.q_one, ...), custom_call_target="tpu_custom_call" | custom-call | tf_op jit(solution)/shard_map/products/pallas_call | solution.py:1297
Async XLA Ops:
  0.6 0.9 copy-start.6
  1.5 0.8 copy-start.10
  2.3 2.2 %copy-start = (bf16[2,4096,256]{2,1,0:T(8,128)(2,1)S(1)}, bf16[2,4096,256]{2,1,0:T(8,128)(2,1)}, u32[]{:S(2)}) copy-start(bf16[2,4096,256]{2,1,0:T(8,128)(2,1)} %refs_8_.1) | copy-start | bytes 12582916
  2.3 3.5 %copy-start.1 = (bf16[2,256,4096]{2,1,0:T(8,128)(2,1)S(1)}, bf16[2,256,4096]{2,1,0:T(8,128)(2,1)}, u32[]{:S(2)}) copy-start(bf16[2,256,4096]{2,1,0:T(8,128)(2,1)} %refs_7_.7) | copy-start | bytes 12582916
  2.3 3.7 %copy-start.2 = (bf16[2,4096,64]{1,2,0:T(8,128)(2,1)S(1)}, bf16[2,4096,64]{1,2,0:T(8,128)(2,1)}, u32[]{:S(2)}) copy-start(bf16[2,4096,64]{1,2,0:T(8,128)(2,1)} %param.17) | copy-start | bytes 3145732
  2.3 4.0 %copy-start.3 = (bf16[2,4096,64]{1,2,0:T(8,128)(2,1)S(1)}, bf16[2,4096,64]{1,2,0:T(8,128)(2,1)}, u32[]{:S(2)}) copy-start(bf16[2,4096,64]{1,2,0:T(8,128)(2,1)} %param.18) | copy-start | bytes 3145732
  2.3 4.1 %copy-start.4 = (bf16[2,512,256]{2,1,0:T(8,128)(2,1)S(1)}, bf16[2,512,256]{2,1,0:T(8,128)(2,1)}, u32[]{:S(2)}) copy-start(bf16[2,512,256]{2,1,0:T(8,128)(2,1)} %refs_10_.1) | copy-start | bytes 1572868
  2.3 4.2 %copy-start.5 = (bf16[2,256,512]{2,1,0:T(8,128)(2,1)S(1)}, bf16[2,256,512]{2,1,0:T(8,128)(2,1)}, u32[]{:S(2)}) copy-start(bf16[2,256,512]{2,1,0:T(8,128)(2,1)} %refs_13_.1) | copy-start | bytes 1572868
  2.3 4.2 %copy-start.7 = (bf16[16,4096]{1,0:T(8,128)(2,1)S(1)}, bf16[16,4096]{1,0:T(8,128)(2,1)}, u32[]{:S(2)}) copy-start(bf16[16,4096]{1,0:T(8,128)(2,1)} %tokens.1) | copy-start | bytes 393220
  2.3 4.2 %copy-start.8 = (bf16[2,512,64]{1,2,0:T(8,128)(2,1)S(1)}, bf16[2,512,64]{1,2,0:T(8,128)(2,1)}, u32[]{:S(2)}) copy-start(bf16[2,512,64]{1,2,0:T(8,128)(2,1)} %param.21) | copy-start | bytes 393220
  2.4 4.3 %copy-start.9 = (bf16[2,512,64]{1,2,0:T(8,128)(2,1)S(1)}, bf16[2,512,64]{1,2,0:T(8,128)(2,1)}, u32[]{:S(2)}) copy-start(bf16[2,512,64]{1,2,0:T(8,128)(2,1)} %param.22) | copy-start | bytes 393220
  2.4 4.3 %copy-start.11 = (f32[2,4096]{1,0:T(2,128)S(1)}, f32[2,4096]{1,0:T(2,128)}, u32[]{:S(2)}) copy-start(f32[2,4096]{1,0:T(2,128)} %refs_12_.1) | copy-start | bytes 98308
  2.4 4.3 %copy-start.12 = (s32[8]{0:T(128)S(1)}, s32[8]{0:T(128)}, u32[]{:S(2)}) copy-start(s32[8]{0:T(128)} %refs_0_.7) | copy-start | bytes 100
  2.4 4.3 %copy-start.13 = (f32[256,128]{1,0:T(8,128)S(1)}, f32[256,128]{1,0:T(8,128)}, u32[]{:S(2)}) copy-start(f32[256,128]{1,0:T(8,128)} %constant.5.clone.refs_2_) | copy-start | bytes 393220
  2.4 4.3 %copy-start.14 = (f32[256,128]{1,0:T(8,128)S(1)}, f32[256,128]{1,0:T(8,128)}, u32[]{:S(2)}) copy-start(f32[256,128]{1,0:T(8,128)} %constant.4.clone.refs_1_) | copy-start | bytes 393220
